TPU v7x, 32 devices: a whole 2x2x4 slice. The times are simulated.
32 devices in a mesh: gx: 4 (over y, x), gy: 4 (over z), gz: 2 (over core).
Axes of the slice: x: 2, y: 2, z: 4, core: 2. Of those that a mesh axis runs over, the one named last changes fastest.
Arguments:
- estimate: float32 [16, 256, 512], P('gz', 'gx', 'gy'), may hold values from 0.25 to 4
- view_data: float32 [16, 256, 512], P('gz', 'gx', 'gy'), may hold values from 0.25 to 4
- psf_stack: float32 [6, 31, 31, 31], replicated, may hold values from 0.01 to 1.53, as said below
- view_index: int32 [1], replicated, may hold values from 0 to 5
Outputs:
- updated_estimate: float32 [16, 256, 512], P('gz', 'gx', 'gy')
- level_one: float32 [8, 128, 256], P('gz', 'gx', 'gy')
- level_two: float32 [4, 64, 128], P('gz', 'gx', 'gy')
- level_three: float32 [2, 32, 64], P('gz', 'gx', 'gy')
- level_four: float32 [1, 16, 32], P(None, 'gx', 'gy')
- level_five: float32 [1, 8, 16], replicated
Inputs may be any that keep to these rules, and one draw needn't show every extreme that they name: `psf_stack`: every entry of every view's point spread function is positive.
All inputs are finite; a program needn't handle non-finite values.
Results may differ from a plain program's by a relative error of at most 0.000075.
Values sent between devices are 32-bit elements; how exact they have to be, the bound alone decides.
No kernel may reach another device: no remote copies, remote signals or barrier semaphores. Data moves between devices by JAX's collectives and lax.ppermute only.
A program may use at most 128 MiB of HBM per device.

v0:
```python
import functools

import jax
import jax.numpy as jnp
import ml_dtypes
import numpy as np
from jax import lax
from jax.experimental import pallas as pl
from jax.experimental.pallas import tpu as pltpu
from jax.sharding import PartitionSpec as P

F32 = jnp.float32
BF16 = jnp.bfloat16
ALL = ("gx", "gy", "gz")
VMEM_LIMIT = 40 * 1024 * 1024


def up8(count):
    return (count + 7) // 8 * 8


class Sizes:
    def __init__(self, estimate_shape, psf_shape, gx, gy):
        self.planes, self.rows, self.cols = estimate_shape
        self.extent = psf_shape[1]
        self.radius = (self.extent - 1) // 2
        self.depth = 2 * self.planes
        self.half = self.cols // 2
        self.wide = up8(2 * self.radius)
        self.near = up8(self.radius)
        self.length = self.rows + 2 * self.wide
        self.view_rows = self.rows + 2 * self.near
        self.stack_rows = self.length + self.view_rows
        self.freqs = self.cols // 2
        self.q_wide = self.cols // self.wide
        self.r_wide = self.length // self.q_wide
        self.q_near = self.cols // self.near
        self.r_near = self.view_rows * 2 // self.q_near
        self.pack_e = self.planes * self.r_wide
        self.pack_v = self.planes // 2 * self.r_near
        self.gx, self.gy = gx, gy
        assert self.half + 2 * self.wide == self.cols == 128
        assert self.wide <= self.rows and self.r_wide % 8 == 0 and self.r_near % 8 == 0
        assert self.depth == 16


def split_np(matrix):
    high = matrix.astype(np.float32).astype(ml_dtypes.bfloat16)
    low = (matrix - high.astype(np.float64)).astype(np.float32).astype(ml_dtypes.bfloat16)
    return high, low


def lane_positions(s, core):
    lanes = np.arange(s.cols)
    return (lanes + s.wide) % s.cols if core == 0 else (lanes - s.wide) % s.cols


def right_pair(matrix):
    high, low = split_np(matrix)
    return np.block([[high, low], [high, np.zeros_like(low)]])


def tables(s):
    y_freq = 2.0 * np.pi * (np.arange(s.freqs) + 0.5) / s.cols
    x_freq = 2.0 * np.pi * np.arange(s.length) / s.length
    y_forward, y_inverse = [], []
    for core in (0, 1):
        angle = lane_positions(s, core)[:, None] * y_freq[None, :]
        y_forward.append(right_pair(np.concatenate([np.cos(angle), -np.sin(angle)], 1)))
        back = np.concatenate([np.cos(angle), -np.sin(angle)], 1).T * (2.0 / s.cols / s.length)
        y_inverse.append(right_pair(back))
    offset = np.zeros(s.cols)
    offset[: s.extent] = np.arange(s.extent) - s.radius
    angle = offset[:, None] * y_freq[None, :]
    y_kernel = np.concatenate([np.cos(angle), -np.sin(angle)], 1)
    y_kernel[s.extent :] = 0.0

    def x_matrix(positions):
        angle = x_freq[:, None] * positions[None, :]
        return np.cos(angle), np.sin(angle)

    def stacked(cosine, sine):
        high, low = split_np(np.concatenate([cosine, sine], 1))
        return np.concatenate([high, low], 0)

    window = np.arange(s.length) - s.wide
    near = np.arange(s.view_rows) - s.near
    own = np.arange(s.rows)
    taps = np.arange(up8(s.extent)) - s.radius
    x_window = stacked(*x_matrix(window))
    x_near = stacked(*x_matrix(near))
    cosine, sine = x_matrix(near)
    x_back_near = stacked(cosine.T, sine.T)
    cosine, sine = x_matrix(own)
    x_back_own = stacked(cosine.T, sine.T)
    high, low = split_np(np.concatenate(x_matrix(taps), 1))
    x_kernel = np.concatenate([high, low, high], 1)
    return dict(
        y_forward=np.stack(y_forward),
        y_inverse=np.stack(y_inverse),
        y_kernel=right_pair(y_kernel),
        x_window=x_window,
        x_near=x_near,
        x_back_near=x_back_near,
        x_back_own=x_back_own,
        x_kernel=x_kernel,
    )


def split(x):
    high = x.astype(BF16)
    return high, (x - high.astype(F32)).astype(BF16)


def dot(a, b):
    return lax.dot_general(a, b, (((1,), (0,)), ((), ())), preferred_element_type=F32)


def lane_iota(rows, cols):
    return lax.broadcasted_iota(jnp.int32, (rows, cols), 1)


def turn(x, shift):
    shift %= x.shape[1]
    return pltpu.roll(x, shift, 1) if shift else x


def times_right(x, pair):
    width = x.shape[1]
    both = dot(jnp.concatenate(split(x), 1), pair)
    return both[:, :width] + both[:, width:]


def times_left(matrix, x):
    count = matrix.shape[0] // 2
    high, low = split(x)
    both = dot(matrix, high)
    return both[:count] + both[count:] + dot(matrix[:count], low)


def quarter_turn(x, sign):
    half = x.shape[1] // 2
    lanes = lane_iota(*x.shape)
    moved = turn(x, half)
    return jnp.where((lanes < half) == (sign > 0), moved, -moved)


def pack_kernel(s, where_ref, e_ref, v_ref, below_ref, above_ref, stack_ref, same_ref, other_ref):
    w, n, length = s.wide, s.near, s.length
    stack_ref[:, :w] = below_ref[:, :w]
    stack_ref[:, w : w + s.rows] = e_ref[...]
    stack_ref[:, w + s.rows : length] = above_ref[:, :w]
    stack_ref[:, length : length + n] = below_ref[:, w:]
    stack_ref[:, length + n : length + n + s.rows] = v_ref[...]
    stack_ref[:, length + n + s.rows :] = above_ref[:, w:]
    first_core = where_ref[1] == 0

    def put(start, count, last, first):
        same_ref[pl.ds(start, count)] = jnp.where(first_core, last, first)
        other_ref[pl.ds(start, count)] = jnp.where(first_core, first, last)

    group = lane_iota(s.r_wide, s.cols) // w
    for z in range(s.planes):
        last = first = jnp.zeros((s.r_wide, s.cols), F32)
        for q in range(s.q_wide):
            moved = turn(stack_ref[z, q * s.r_wide : (q + 1) * s.r_wide], q * w)
            last = jnp.where(group == (q - 1) % s.q_wide, moved, last)
            first = jnp.where(group == q, moved, first)
        put(z * s.r_wide, s.r_wide, last, first)
    group = lane_iota(s.r_near, s.cols) // n
    per_plane = s.q_near // 2
    for low in range(s.planes // 2):
        last = first = jnp.zeros((s.r_near, s.cols), F32)
        for j in range(s.q_near):
            plane = j // per_plane * (s.planes // 2) + low
            start = length + j % per_plane * s.r_near
            moved = turn(stack_ref[plane, start : start + s.r_near], j * n)
            last = jnp.where(group == (j - 1) % s.q_near, moved, last)
            first = jnp.where(group == j, moved, first)
        put(s.pack_e + low * s.r_near, s.r_near, last, first)


def kernel_spectrum(s, where_ref, psf_ref, y_ref, x_ref, k1_ref, k2_ref, pad_ref, a_ref):
    taps = up8(s.extent)
    pad_ref[...] = jnp.zeros_like(pad_ref)
    total = jnp.zeros((s.extent, s.extent), F32)
    for a in range(s.extent):
        total = total + psf_ref[0, a]
    total = jnp.sum(total)
    for a in range(s.extent):
        pad_ref[a * taps : a * taps + s.extent, : s.extent] = psf_ref[0, a] / total
    a_ref[...] = times_right(pad_ref[...], y_ref[...])
    lanes = lane_iota(s.length, s.cols)
    half = s.cols // 2
    for pair in range((s.extent + 1) // 2):
        one = a_ref[2 * pair * taps : (2 * pair + 1) * taps]
        two = a_ref[(2 * pair + 1) * taps : (2 * pair + 2) * taps]
        right = jnp.concatenate(
            [
                jnp.concatenate([one, two], 1),
                jnp.concatenate([quarter_turn(one, 1), quarter_turn(two, 1)], 1),
            ],
            0,
        )
        high, low = split(right)
        out = dot(x_ref[...], jnp.concatenate([high, high, low], 0))
        for side in (0, 1):
            a = 2 * pair + side
            if a < s.extent:
                value = out[:, side * s.cols : (side + 1) * s.cols]
                moved = turn(value, half)
                k1_ref[a] = jnp.where(lanes < half, value, moved)
                k2_ref[a] = jnp.where(lanes < half, -moved, value)


def main_kernel(
    s,
    where_ref,
    own_ref,
    partner_ref,
    same_ref,
    other_ref,
    k1_ref,
    k2_ref,
    yf_ref,
    yi_ref,
    xw_ref,
    xn_ref,
    xbn_ref,
    xbo_ref,
    mine_ref,
    theirs_ref,
    five_ref,
    e_ref,
    v_ref,
    x1_ref,
    x2_ref,
    p_ref,
    u_ref,
    t_ref,
):
    core, gx, gy = where_ref[1], where_ref[2], where_ref[3]
    half = s.cols // 2
    depth = s.depth
    for source_ref, halo_ref, base in (
        (own_ref, same_ref, core * s.planes),
        (partner_ref, other_ref, (1 - core) * s.planes),
    ):
        lanes = lane_iota(s.r_wide, s.cols)
        from_halo = jnp.where(core == 0, lanes - (s.cols - s.wide), s.wide - 1 - lanes) >= 0
        for z in range(s.planes):
            packed = halo_ref[z * s.r_wide : (z + 1) * s.r_wide]
            for q in range(s.q_wide):
                rows = slice(q * s.r_wide, (q + 1) * s.r_wide)
                e_ref[base + z, rows] = jnp.where(from_halo, turn(packed, -q * s.wide), source_ref[z, rows])
        lanes = lane_iota(s.r_near, s.cols)
        from_halo = jnp.where(core == 0, lanes - (s.cols - s.near), s.near - 1 - lanes) >= 0
        per_plane = s.q_near // 2
        for low in range(s.planes // 2):
            packed = halo_ref[s.pack_e + low * s.r_near : s.pack_e + (low + 1) * s.r_near]
            for j in range(s.q_near):
                plane = j // per_plane * (s.planes // 2) + low
                start = j % per_plane * s.r_near
                v_ref[base + plane, start : start + s.r_near] = jnp.where(
                    from_halo,
                    turn(packed, -j * s.near),
                    source_ref[plane, s.length + start : s.length + start + s.r_near],
                )

    def forward(load, x_table, sign):
        for pair in range(depth // 2):
            parts = [times_right(load(2 * pair + side), yf_ref[0]) for side in (0, 1)]
            right = jnp.concatenate(
                [
                    jnp.concatenate(parts, 1),
                    jnp.concatenate([quarter_turn(part, 1) for part in parts], 1),
                ],
                0,
            )
            out = times_left(x_table[...], right)
            for side in (0, 1):
                value = out[:, side * s.cols : (side + 1) * s.cols]
                moved = turn(value, half)
                x1_ref[2 * pair + side] = value
                x2_ref[2 * pair + side] = moved if sign > 0 else -moved

    def along_z(flip):
        block = 4

        def tile(t, carry):
            rows = pl.ds(t * 8, 8)
            ones = [x1_ref[z, rows] for z in range(depth)]
            twos = [x2_ref[z, rows] for z in range(depth)]
            for start in range(0, depth, block):
                sums = [None] * block
                for d in range(2 * depth - 1):
                    hits = []
                    for k in range(block):
                        zi = start + k + (d - (depth - 1)) * (1 if flip else -1)
                        if 0 <= zi < depth:
                            hits.append((k, zi))
                    if not hits:
                        continue
                    tap = d - (depth - 1) + s.radius
                    k1, k2 = k1_ref[tap, rows], k2_ref[tap, rows]
                    for k, zi in hits:
                        term = k1 * ones[zi] + k2 * twos[zi]
                        sums[k] = term if sums[k] is None else sums[k] + term
                for k in range(block):
                    p_ref[start + k, rows] = sums[k]
            return carry

        lax.fori_loop(0, s.length // 8, tile, 0)

    def backward(x_table, use):
        for pair in range(depth // 2):
            parts = [p_ref[2 * pair + side] for side in (0, 1)]
            right = jnp.concatenate(
                [
                    jnp.concatenate(parts, 1),
                    jnp.concatenate([quarter_turn(part, -1) for part in parts], 1),
                ],
                0,
            )
            out = times_left(x_table[...], right)
            for side in (0, 1):
                use(2 * pair + side, times_right(out[:, side * s.cols : (side + 1) * s.cols], yi_ref[0]))

    forward(lambda z: e_ref[z], xw_ref, 1)
    along_z(False)

    shape = (s.view_rows, s.cols)
    row = lax.broadcasted_iota(jnp.int32, shape, 0) - s.near
    lane = lane_iota(*shape)
    column = lane + jnp.where(core == 0, jnp.where(lane < s.cols - s.near, 0, -s.cols), jnp.where(lane < s.near, s.cols, 0))
    first_row, last_row = -gx * s.rows, (s.gx - gx) * s.rows
    first_column, last_column = -gy * s.cols, (s.gy - gy) * s.cols
    inside = (row >= first_row) & (row < last_row) & (column >= first_column) & (column < last_column)
    begin = core * half - s.near
    inside = inside & (column >= begin) & (column < begin + half + 2 * s.near)

    def to_ratio(z, blurred):
        safe = jnp.where(inside, blurred, 1.0)
        v_ref[z] = jnp.where(inside, v_ref[z] / safe, 0.0)

    backward(xbn_ref, to_ratio)
    forward(lambda z: v_ref[z], xn_ref, -1)
    along_z(True)

    lane = lane_iota(s.rows, s.cols)
    owned = (lane // half) == core

    def to_update(z, correction):
        u_ref[z] = jnp.where(owned, e_ref[z, s.wide : s.wide + s.rows] * correction, 0.0)

    backward(xbo_ref, to_update)

    def pooled(x, factor, scale):
        count = s.cols // factor
        weights = jnp.where(
            lax.broadcasted_iota(jnp.int32, (s.cols, count), 0) // factor
            == lax.broadcasted_iota(jnp.int32, (s.cols, count), 1),
            scale,
            0.0,
        ).astype(BF16)
        high, rest = split(x)
        middle = x - high.astype(F32)
        low = (middle - rest.astype(F32)).astype(BF16)
        return dot(high, weights) + dot(rest, weights) + dot(low, weights)

    u_rows = s.planes * s.rows
    source = u_ref
    planes, rows, start = depth, s.rows, u_rows
    levels = []
    for level in (1, 2, 3, 4):
        planes, rows = planes // 2, rows // 2
        here = t_ref.at[level - 1]
        for z in range(planes):
            here[z, : 2 * rows] = source[2 * z, : 2 * rows] + source[2 * z + 1, : 2 * rows]
        sums = [
            here[z, pl.ds(0, rows, stride=2)] + here[z, pl.ds(1, rows, stride=2)] for z in range(planes)
        ]
        for z in range(planes):
            here[z, :rows] = sums[z]
        factor = 2**level
        value = pooled(jnp.concatenate(sums, 0), factor, 1.0 / factor**3)
        levels.append((value, planes, rows, s.cols // factor))
        source = here
    for half_index in (0, 1):
        for mine, out_ref in ((True, mine_ref), (False, theirs_ref)):

            @pl.when((core == half_index) == mine)
            def _():
                for z in range(s.planes):
                    out_ref[z * s.rows : (z + 1) * s.rows] = u_ref[half_index * s.planes + z]
                start = u_rows
                for value, planes, rows, columns in levels:
                    count = max(planes * rows // 2, rows)
                    begin = half_index * count if planes > 1 else 0
                    out_ref[start : start + count, :columns] = value[begin : begin + count]
                    start += up8(count)
    top = sums[0]
    rows5, columns5 = five_ref.shape[1:]
    own_rows = top.shape[0] // 2
    row = lax.broadcasted_iota(jnp.int32, (rows5, s.cols), 0)
    spread = jnp.zeros((rows5, s.cols), F32)
    for i in range(own_rows):
        spread = jnp.where(row == gx * own_rows + i, top[2 * i : 2 * i + 1] + top[2 * i + 1 : 2 * i + 2], spread)
    factor = 32
    per_chip = s.cols // factor
    weights = jnp.where(
        lax.broadcasted_iota(jnp.int32, (s.cols, columns5), 0) // factor + gy * per_chip
        == lax.broadcasted_iota(jnp.int32, (s.cols, columns5), 1),
        1.0 / (factor * factor * depth),
        0.0,
    ).astype(BF16)
    high, rest = split(spread)
    low = (spread - high.astype(F32) - rest.astype(F32)).astype(BF16)
    five = dot(high, weights) + dot(rest, weights) + dot(low, weights)
    for k in range(five_ref.shape[0]):
        five_ref[k] = five


def last_kernel(s, mine_ref, got_ref, fives_ref, u_ref, one_ref, two_ref, three_ref, four_ref, five_ref):
    for z in range(s.planes):
        part = slice(z * s.rows, (z + 1) * s.rows)
        u_ref[z] = mine_ref[part] + got_ref[part]
    start = s.planes * s.rows
    for out_ref in (one_ref, two_ref, three_ref, four_ref):
        planes, rows, columns = out_ref.shape
        for z in range(planes):
            part = slice(start + z * rows, start + (z + 1) * rows)
            out_ref[z] = mine_ref[part, :columns] + got_ref[part, :columns]
        start += up8(planes * rows)
    total = fives_ref[0]
    for k in range(1, fives_ref.shape[0]):
        total = total + fives_ref[k]
    five_ref[0] = total


def whole(shape):
    return pl.BlockSpec(shape, lambda *_: (0,) * len(shape))


def call(body, where, arrays, in_specs, outs, scratch=(), name=None):
    grid_spec = pltpu.PrefetchScalarGridSpec(
        num_scalar_prefetch=1,
        grid=(1,),
        in_specs=in_specs,
        out_specs=[whole(shape) for shape in outs],
        scratch_shapes=[pltpu.VMEM(shape, F32) for shape in scratch],
    )
    return pl.pallas_call(
        body,
        grid_spec=grid_spec,
        out_shape=[jax.ShapeDtypeStruct(shape, F32) for shape in outs],
        compiler_params=pltpu.CompilerParams(vmem_limit_bytes=VMEM_LIMIT),
        name=name,
    )(where, *arrays)


def shift(axis, step):
    count = lax.axis_size(axis)
    return [(i, i + step) for i in range(count) if 0 <= i + step < count]


def to_side(same):
    pairs = []
    for h in range(lax.axis_size("gy")):
        sender_up, sender_down = (0, 1) if same else (1, 0)
        if h + 1 < lax.axis_size("gy"):
            pairs.append((2 * h + sender_up, 2 * (h + 1)))
        if h > 0:
            pairs.append((2 * h + sender_down, 2 * (h - 1) + 1))
    return pairs


def local(estimate, view_data, psf_stack, view_index):
    assert lax.axis_size("gz") == 2
    gx, gy = lax.axis_size("gx"), lax.axis_size("gy")
    s = Sizes(estimate.shape, psf_stack.shape, gx, gy)
    t = {key: jnp.asarray(value) for key, value in tables(s).items()}
    where = jnp.stack(
        [view_index[0], lax.axis_index("gz"), lax.axis_index("gx"), lax.axis_index("gy")]
    ).astype(jnp.int32)

    below = lax.ppermute(
        jnp.concatenate([estimate[:, s.rows - s.wide :], view_data[:, s.rows - s.near :]], 1), "gx", shift("gx", 1)
    )
    above = lax.ppermute(
        jnp.concatenate([estimate[:, : s.wide], view_data[:, : s.near]], 1), "gx", shift("gx", -1)
    )
    psf_shape = (1,) + psf_stack.shape[1:]
    taps = up8(s.extent)
    k1, k2 = call(
        functools.partial(kernel_spectrum, s),
        where,
        (psf_stack, t["y_kernel"], t["x_kernel"]),
        [pl.BlockSpec(psf_shape, lambda i, w: (w[0], 0, 0, 0)), whole(t["y_kernel"].shape), whole(t["x_kernel"].shape)],
        [(s.extent, s.length, s.cols)] * 2,
        scratch=[((s.extent + 1) // 2 * 2 * taps, s.cols)] * 2,
        name="kernel_spectrum",
    )
    stack_shape = (s.planes, s.stack_rows, s.cols)
    slab_shape = (s.pack_e + s.pack_v, s.cols)
    arrays = (estimate, view_data, below, above)
    stack, same, other = call(
        functools.partial(pack_kernel, s),
        where,
        arrays,
        [whole(a.shape) for a in arrays],
        [stack_shape, slab_shape, slab_shape],
        name="pack",
    )
    partner = lax.ppermute(stack, "gz", [(0, 1), (1, 0)])
    same = lax.ppermute(same, ("gy", "gz"), to_side(True))
    other = lax.ppermute(other, ("gy", "gz"), to_side(False))

    u_rows = s.planes * s.rows
    out_rows = u_rows
    level_shapes = []
    planes, rows, columns = s.depth, s.rows, s.cols
    for _ in range(4):
        planes, rows, columns = planes // 2, rows // 2, columns // 2
        level_shapes.append((max(planes // 2, 1), rows, columns))
        out_rows += up8(level_shapes[-1][0] * rows)
    devices = 2 * gx * gy
    five_shape = (rows // 2 * gx, columns // 2 * gy)
    arrays = (
        stack,
        partner,
        same,
        other,
        k1,
        k2,
        t["y_forward"],
        t["y_inverse"],
        t["x_window"],
        t["x_near"],
        t["x_back_near"],
        t["x_back_own"],
    )
    specs = [whole(a.shape) for a in arrays]
    for k in (6, 7):
        specs[k] = pl.BlockSpec((1,) + arrays[k].shape[1:], lambda i, w: (w[1], 0, 0))
    spectrum = (s.depth, s.length, s.cols)
    mine, theirs, five = call(
        functools.partial(main_kernel, s),
        where,
        arrays,
        specs,
        [(out_rows, s.cols), (out_rows, s.cols), (devices,) + five_shape],
        scratch=[
            spectrum,
            (s.depth, s.view_rows, s.cols),
            spectrum,
            spectrum,
            spectrum,
            (s.depth, s.rows, s.cols),
            (4, s.depth // 2, s.rows, s.cols),
        ],
        name="update",
    )
    got = lax.ppermute(theirs, "gz", [(0, 1), (1, 0)])
    fives = lax.all_to_all(five, ALL, split_axis=0, concat_axis=0, tiled=True)
    outs = [estimate.shape] + level_shapes + [(1,) + five_shape]
    arrays = (mine, got, fives)
    return tuple(
        pl.pallas_call(
            functools.partial(last_kernel, s),
            in_specs=[whole(a.shape) for a in arrays],
            out_specs=[whole(shape) for shape in outs],
            out_shape=[jax.ShapeDtypeStruct(shape, F32) for shape in outs],
            grid=(1,),
            compiler_params=pltpu.CompilerParams(vmem_limit_bytes=VMEM_LIMIT),
            name="assemble",
        )(*arrays)
    )


def solution(mesh):
    return jax.shard_map(
        local,
        mesh=mesh,
        in_specs=(P("gz", "gx", "gy"), P("gz", "gx", "gy"), P(), P()),
        out_specs=(
            P("gz", "gx", "gy"),
            P("gz", "gx", "gy"),
            P("gz", "gx", "gy"),
            P("gz", "gx", "gy"),
            P(None, "gx", "gy"),
            P(),
        ),
        check_vma=False,
    )
```

profile of v0, /device:TPU:0, one launch (start us, length us, event | category | flops | bytes accessed | tf_op | source)
XLA Modules:
  0.0 58.3 jit_solution(324762247617392273)
XLA Ops:
  0.6 0.0 copy-start.10
  0.7 1.0 %fusion = (f32[8,32,128]{2,1,0:T(8,128)S(1)}, f32[8,32,128]{2,1,0:T(8,128)S(1)}) fusion(f32[8,64,128]{2,1,0:T(8,128)} %e_ref.1), kind=kLoop, calls=%fused_computation.3 | loop fusion | bytes 524288 | tf_op jit(solution)/shard_map/slice | solution.py:491
  1.7 0.9 %fusion.1 = (f32[8,16,128]{2,1,0:T(8,128)S(1)}, f32[8,16,128]{2,1,0:T(8,128)S(1)}) fusion(f32[8,64,128]{2,1,0:T(8,128)} %v_ref.1), kind=kLoop, calls=%fused_computation.4 | loop fusion | bytes 262144 | tf_op jit(solution)/shard_map/slice | solution.py:491
  2.6 4.9 %collective-permute-start = (f32[8,48,128]{2,1,0:T(8,128)S(1)}, f32[8,48,128]{2,1,0:T(8,128)S(1)}, u32[]{:S(2)}, u32[]{:S(2)}) collective-permute-start(f32[8,48,128]{2,1,0:T(8,128)S(1)} %pad_maximum_fusion), channel_id=1, source_target_pairs={{0,8},{8,16},{16,24},{1,9},{9,17},{17,25},{2,10},{10,18},{18,26},{... | collective-permute-start | bytes 589832 | tf_op jit(solution)/shard_map/ppermute | solution.py:487
  7.5 1.3 %collective-permute-start.1 = (f32[8,48,128]{2,1,0:T(8,128)S(1)}, f32[8,48,128]{2,1,0:T(8,128)S(1)}, u32[]{:S(2)}, u32[]{:S(2)}) collective-permute-start(f32[8,48,128]{2,1,0:T(8,128)S(1)} %pad_maximum_fusion.1), channel_id=1, source_target_pairs={{8,0},{16,8},{24,16},{9,1},{17,9},{25,17},{10,2},{18,10},{26,18},{... | collective-permute-start | bytes 589832 | tf_op jit(solution)/shard_map/ppermute | solution.py:490
  9.5 0.1 pad_add_fusion.where_ref
  9.6 2.1 %collective-permute-done.below_ref = f32[8,48,128]{2,1,0:T(8,128)S(1)} collective-permute-done((f32[8,48,128]{2,1,0:T(8,128)S(1)}, f32[8,48,128]{2,1,0:T(8,128)S(1)}, u32[]{:S(2)}, u32[]{:S(2)}) %collective-permute-start) | collective-permute-done | bytes 196640 | tf_op jit(solution)/shard_map/ppermute | solution.py:487
  11.6 6.2 %collective-permute-done.1.above_ref = f32[8,48,128]{2,1,0:T(8,128)S(1)} collective-permute-done((f32[8,48,128]{2,1,0:T(8,128)S(1)}, f32[8,48,128]{2,1,0:T(8,128)S(1)}, u32[]{:S(2)}, u32[]{:S(2)}) %collective-permute-start.1) | collective-permute-done | bytes 196640 | tf_op jit(solution)/shard_map/ppermute | solution.py:490
  17.8 0.9 %copy-done.1 = f32[8,64,128]{2,1,0:T(8,128)S(1)} copy-done((f32[8,64,128]{2,1,0:T(8,128)S(1)}, f32[8,64,128]{2,1,0:T(8,128)}, u32[]{:S(2)}) %copy-start.1) | copy-done | bytes 262168
  18.7 0.9 %copy-done.2 = f32[8,64,128]{2,1,0:T(8,128)S(1)} copy-done((f32[8,64,128]{2,1,0:T(8,128)S(1)}, f32[8,64,128]{2,1,0:T(8,128)}, u32[]{:S(2)}) %copy-start.2) | copy-done | bytes 262168
  19.7 0.8 %pack.1 = (f32[8,224,128]{2,1,0:T(8,128)S(1)}, f32[352,128]{1,0:T(8,128)S(1)}, f32[352,128]{1,0:T(8,128)S(1)}) custom-call(s32[4]{0:T(128)S(1)} %pad_add_fusion.where_ref, f32[8,64,128]{2,1,0:T(8,128)S(1)} %copy-done.1, f32[8,64,128]{2,1,0:T(8,128)S(1)} %copy-done.2, f32[8,48,128]{2,1,0:T(8,128)S(1)} %collective-permute-done.below_ref, ...), custom_call_target="tpu_custom_call" | custom-call | tf_op jit(solution)/shard_map/pack/pallas_call | solution.py:453
  20.5 0.1 collective-permute-start.2
  20.6 3.5 %collective-permute-start.3 = (f32[352,128]{1,0:T(8,128)S(1)}, f32[352,128]{1,0:T(8,128)S(1)}, u32[]{:S(2)}, u32[]{:S(2)}) collective-permute-start(f32[352,128]{1,0:T(8,128)S(1)} %get-tuple-element.15), channel_id=1, source_target_pairs={{0,2},{2,4},{3,1},{4,6},{5,3},{7,5},{8,10},{10,12},{11,9},{12,14},... | collective-permute-start | bytes 540680 | tf_op jit(solution)/shard_map/ppermute | solution.py:516
  24.1 0.7 %collective-permute-start.4 = (f32[352,128]{1,0:T(8,128)S(1)}, f32[352,128]{1,0:T(8,128)S(1)}, u32[]{:S(2)}, u32[]{:S(2)}) collective-permute-start(f32[352,128]{1,0:T(8,128)S(1)} %get-tuple-element.16), channel_id=1, source_target_pairs={{1,2},{3,4},{2,1},{5,6},{4,3},{6,5},{9,10},{11,12},{10,9},{13,14},... | collective-permute-start | bytes 540680 | tf_op jit(solution)/shard_map/ppermute | solution.py:517
  24.8 1.9 %copy-done = f32[6,31,31,31]{3,2,1,0:T(8,128)S(1)} copy-done((f32[6,31,31,31]{3,2,1,0:T(8,128)S(1)}, f32[6,31,31,31]{3,2,1,0:T(8,128)}, u32[]{:S(2)}) %copy-start) | copy-done | bytes 715008
  26.7 1.7 %kernel_spectrum.1 = (f32[31,128,128]{2,1,0:T(8,128)S(1)}, f32[31,128,128]{2,1,0:T(8,128)S(1)}) custom-call(s32[4]{0:T(128)S(1)} %pad_add_fusion.where_ref, f32[6,31,31,31]{3,2,1,0:T(8,128)S(1)} %copy-done, bf16[256,256]{1,0:T(8,128)(2,1)S(1)} %copy-done.7, bf16[128,192]{1,0:T(8,128)(2,1)S(1)} %copy-done.10), custom_call_target="tpu_custom_call" | custom-call | tf_op jit(solution)/shard_map/kernel_spectrum/pallas_call | solution.py:453
  28.5 14.1 %update.1 = (f32[688,128]{1,0:T(8,128)S(1)}, f32[688,128]{1,0:T(8,128)S(1)}, f32[32,8,16]{2,1,0:T(8,128)S(1)}) custom-call(s32[4]{0:T(128)S(1)} %pad_add_fusion.where_ref, f32[8,224,128]{2,1,0:T(8,128)S(1)} %get-tuple-element.14.own_ref, f32[8,224,128]{2,1,0:T(8,128)S(1)} %collective-permute-done.2.partner_ref, ...), custom_call_target="tpu_custom_call" | custom-call | tf_op jit(solution)/shard_map/update/pallas_call | solution.py:453
  42.5 3.0 %collective-permute-start.5 = (f32[688,128]{1,0:T(8,128)S(1)}, f32[688,128]{1,0:T(8,128)S(1)}, u32[]{:S(2)}, u32[]{:S(2)}) collective-permute-start(f32[688,128]{1,0:T(8,128)S(1)} %get-tuple-element.20), channel_id=1, source_target_pairs={{0,1},{1,0},{2,3},{3,2},{4,5},{5,4},{6,7},{7,6},{8,9},{9,8},{10,11... | collective-permute-start | bytes 1056776 | tf_op jit(solution)/shard_map/ppermute | solution.py:564
  45.5 0.1 reshape.12
  45.6 10.6 %all_to_all.5 = f32[32,1,128]{2,1,0:T(1,128)S(1)} all-to-all(f32[32,1,128]{2,1,0:T(1,128)S(1)} %reshape.12), channel_id=1, replica_groups=mesh['gx'=4,'gy'=4,'gz'=2] {'gx','gy','gz'}, dimensions={0} | all-to-all | bytes 32768 | tf_op jit(solution)/shard_map/all_to_all | solution.py:565
  56.2 0.5 broadcast
  56.7 0.7 %reduce = f32[32,128]{1,0:T(8,128)S(1)} reduce(f32[32,1,128]{2,1,0:T(1,128)S(1)} %all_to_all.5, f32[]{:T(128)} %broadcast), dimensions={1}, to_apply=%all_to_all.3.reduce_sub_computation | reduce | bytes 32772 | tf_op jit(solution)/shard_map/all_to_all | solution.py:565
  57.4 0.1 reshape.13.fives_ref
  57.5 0.8 %assemble.1 = (f32[8,64,128]{2,1,0:T(8,128)}, f32[4,32,64]{2,1,0:T(8,128)}, f32[2,16,32]{2,1,0:T(8,128)}, f32[1,8,16]{2,1,0:T(8,128)}, f32[1,4,8]{2,1,0:T(4,128)}, /*index=5*/f32[1,8,16]{2,1,0:T(8,128)}) custom-call(f32[688,128]{1,0:T(8,128)S(1)} %get-tuple-element.19.mine_ref, f32[688,128]{1,0:T(8,128)S(1)} %collective-permute-done.5.got_ref, ...), custom_call_target="tpu_custom_call" | custom-call | tf_op jit(solution)/shard_map/assemble/pallas_call | solution.py:569
  (24 shorter events, 0.1 us)
Async XLA Ops:
  0.6 24.2 %copy-start.7 = (bf16[256,256]{1,0:T(8,128)(2,1)S(1)}, bf16[256,256]{1,0:T(8,128)(2,1)}, u32[]{:S(2)}) copy-start(bf16[256,256]{1,0:T(8,128)(2,1)} %constant.29.clone.y_ref) | copy-start | bytes 393220
  0.6 24.2 %copy-start.10 = (bf16[128,192]{1,0:T(8,128)(2,1)S(1)}, bf16[128,192]{1,0:T(8,128)(2,1)}, u32[]{:S(2)}) copy-start(bf16[128,192]{1,0:T(8,128)(2,1)} %constant.34.clone.x_ref) | copy-start | bytes 147460
  2.6 9.0 %collective-permute-start = (f32[8,48,128]{2,1,0:T(8,128)S(1)}, f32[8,48,128]{2,1,0:T(8,128)S(1)}, u32[]{:S(2)}, u32[]{:S(2)}) collective-permute-start(f32[8,48,128]{2,1,0:T(8,128)S(1)} %pad_maximum_fusion), channel_id=1, source_target_pairs={{0,8},{8,16},{16,24},{1,9},{9,17},{17,25},{2,10},{10,18},{18,26},{... | collective-permute-start | bytes 589832 | tf_op jit(solution)/shard_map/ppermute | solution.py:487
  7.5 10.3 %collective-permute-start.1 = (f32[8,48,128]{2,1,0:T(8,128)S(1)}, f32[8,48,128]{2,1,0:T(8,128)S(1)}, u32[]{:S(2)}, u32[]{:S(2)}) collective-permute-start(f32[8,48,128]{2,1,0:T(8,128)S(1)} %pad_maximum_fusion.1), channel_id=1, source_target_pairs={{8,0},{16,8},{24,16},{9,1},{17,9},{25,17},{10,2},{18,10},{26,18},{... | collective-permute-start | bytes 589832 | tf_op jit(solution)/shard_map/ppermute | solution.py:490
  17.8 1.0 %copy-start.1 = (f32[8,64,128]{2,1,0:T(8,128)S(1)}, f32[8,64,128]{2,1,0:T(8,128)}, u32[]{:S(2)}) copy-start(f32[8,64,128]{2,1,0:T(8,128)} %e_ref.1) | copy-start | bytes 786436
  18.7 0.9 %copy-start.2 = (f32[8,64,128]{2,1,0:T(8,128)S(1)}, f32[8,64,128]{2,1,0:T(8,128)}, u32[]{:S(2)}) copy-start(f32[8,64,128]{2,1,0:T(8,128)} %v_ref.1) | copy-start | bytes 786436
  19.7 8.7 %copy-start.3 = (bf16[2,256,256]{2,1,0:T(8,128)(2,1)S(1)}, bf16[2,256,256]{2,1,0:T(8,128)(2,1)}, u32[]{:S(2)}) copy-start(bf16[2,256,256]{2,1,0:T(8,128)(2,1)} %constant.27.clone.yf_ref) | copy-start | bytes 786436
  19.7 8.7 %copy-start.4 = (bf16[2,256,256]{2,1,0:T(8,128)(2,1)S(1)}, bf16[2,256,256]{2,1,0:T(8,128)(2,1)}, u32[]{:S(2)}) copy-start(bf16[2,256,256]{2,1,0:T(8,128)(2,1)} %constant.28.clone.yi_ref) | copy-start | bytes 786436
  19.7 8.7 %copy-start.5 = (bf16[256,256]{1,0:T(8,128)(2,1)S(1)}, bf16[256,256]{1,0:T(8,128)(2,1)}, u32[]{:S(2)}) copy-start(bf16[256,256]{1,0:T(8,128)(2,1)} %constant.30.clone.xw_ref) | copy-start | bytes 393220
  19.7 8.7 %copy-start.6 = (bf16[256,192]{1,0:T(8,128)(2,1)S(1)}, bf16[256,192]{1,0:T(8,128)(2,1)}, u32[]{:S(2)}) copy-start(bf16[256,192]{1,0:T(8,128)(2,1)} %constant.31.clone.xn_ref) | copy-start | bytes 294916
  19.7 8.7 %copy-start.8 = (bf16[192,256]{1,0:T(8,128)(2,1)S(1)}, bf16[192,256]{1,0:T(8,128)(2,1)}, u32[]{:S(2)}) copy-start(bf16[192,256]{1,0:T(8,128)(2,1)} %constant.32.clone.xbn_ref) | copy-start | bytes 294916
  20.5 7.9 %collective-permute-start.2 = (f32[8,224,128]{2,1,0:T(8,128)S(1)}, f32[8,224,128]{2,1,0:T(8,128)S(1)}, u32[]{:S(2)}, u32[]{:S(2)}) collective-permute-start(f32[8,224,128]{2,1,0:T(8,128)S(1)} %get-tuple-element.14.own_ref), channel_id=1, source_target_pairs={{0,1},{1,0},{2,3},{3,2},{4,5},{5,4},{6,7},{7,6},{8,9},{9,8},{10,11... | collective-permute-start | bytes 2752520 | tf_op jit(solution)/shard_map/ppermute | solution.py:515
  20.6 7.8 %collective-permute-start.3 = (f32[352,128]{1,0:T(8,128)S(1)}, f32[352,128]{1,0:T(8,128)S(1)}, u32[]{:S(2)}, u32[]{:S(2)}) collective-permute-start(f32[352,128]{1,0:T(8,128)S(1)} %get-tuple-element.15), channel_id=1, source_target_pairs={{0,2},{2,4},{3,1},{4,6},{5,3},{7,5},{8,10},{10,12},{11,9},{12,14},... | collective-permute-start | bytes 540680 | tf_op jit(solution)/shard_map/ppermute | solution.py:516
  24.1 4.3 %collective-permute-start.4 = (f32[352,128]{1,0:T(8,128)S(1)}, f32[352,128]{1,0:T(8,128)S(1)}, u32[]{:S(2)}, u32[]{:S(2)}) collective-permute-start(f32[352,128]{1,0:T(8,128)S(1)} %get-tuple-element.16), channel_id=1, source_target_pairs={{1,2},{3,4},{2,1},{5,6},{4,3},{6,5},{9,10},{11,12},{10,9},{13,14},... | collective-permute-start | bytes 540680 | tf_op jit(solution)/shard_map/ppermute | solution.py:517
  24.8 1.9 %copy-start = (f32[6,31,31,31]{3,2,1,0:T(8,128)S(1)}, f32[6,31,31,31]{3,2,1,0:T(8,128)}, u32[]{:S(2)}) copy-start(f32[6,31,31,31]{3,2,1,0:T(8,128)} %psf_ref.1) | copy-start | bytes 2144956
  26.7 1.8 %copy-start.9 = (bf16[128,256]{1,0:T(8,128)(2,1)S(1)}, bf16[128,256]{1,0:T(8,128)(2,1)}, u32[]{:S(2)}) copy-start(bf16[128,256]{1,0:T(8,128)(2,1)} %constant.33.clone.xbo_ref) | copy-start | bytes 196612
  42.5 15.0 %collective-permute-start.5 = (f32[688,128]{1,0:T(8,128)S(1)}, f32[688,128]{1,0:T(8,128)S(1)}, u32[]{:S(2)}, u32[]{:S(2)}) collective-permute-start(f32[688,128]{1,0:T(8,128)S(1)} %get-tuple-element.20), channel_id=1, source_target_pairs={{0,1},{1,0},{2,3},{3,2},{4,5},{5,4},{6,7},{7,6},{8,9},{9,8},{10,11... | collective-permute-start | bytes 1056776 | tf_op jit(solution)/shard_map/ppermute | solution.py:564
where the time goes:
time: 58.7 us; the launch traced here: 58.3 us
  Pallas kernels  17.3 us (29%)
  starting transfers between devices  13.4 us (23%)
  blocking collectives  10.6 us (18%)
  waiting for transfers between devices  8.25 us (14%)
  local copies, waits for them, and re-layouts  6.42 us (11%)
  between operations  1.52 us (3%)
  other arithmetic  0.79 us (1%)
    pallas_call x3, Pallas kernels, call(): pl.pallas_call(body, grid_spec=grid_spec, out_shape=[jax.ShapeDtypeStruct...  16.6 us
    all_to_all x1, blocking collectives, local(): fives = lax.all_to_all(five, ALL, split_axis=0, concat_axis=0, tiled=True)  10.6 us
    ppermute x1, waiting for transfers between devices, local(): lax.ppermute(jnp.concatenate([estimate[:, :s.wide], view_data[:, :s.near]...  6.16 us
    ppermute x1, starting transfers between devices, local(): lax.ppermute(jnp.concatenate([estimate[:, s.rows - s.wide:], view_data[:,...  4.88 us
    unnamed x24, local copies, waits for them, and re-layouts  3.99 us
    ppermute x1, starting transfers between devices, local(): same = lax.ppermute(same, ('gy', 'gz'), to_side(True))  3.49 us
    ppermute x1, starting transfers between devices, local(): got = lax.ppermute(theirs, 'gz', [(0, 1), (1, 0)])  2.99 us
    ppermute x1, waiting for transfers between devices, local(): lax.ppermute(jnp.concatenate([estimate[:, s.rows - s.wide:], view_data[:,...  2.08 us
  transfers between devices with their start and end apart: 6, of which 2 were waited for; matrix products, arithmetic and copies ran while one was open for 3% of the time, Pallas kernels for 3%

commit v1 on v0

--- a/solution.py
+++ b/solution.py
@@ -12,7 +12,7 @@
 F32 = jnp.float32
 BF16 = jnp.bfloat16
 ALL = ("gx", "gy", "gz")
-VMEM_LIMIT = 40 * 1024 * 1024
+MIB = 1024 * 1024
 
 
 def up8(count):
@@ -80,8 +80,8 @@
         return np.cos(angle), np.sin(angle)
 
     def stacked(cosine, sine):
-        high, low = split_np(np.concatenate([cosine, sine], 1))
-        return np.concatenate([high, low], 0)
+        high, low = split_np(np.concatenate([cosine, sine], 0))
+        return np.concatenate([high, high, low], 1)
 
     window = np.arange(s.length) - s.wide
     near = np.arange(s.view_rows) - s.near
@@ -125,17 +125,17 @@
     return pltpu.roll(x, shift, 1) if shift else x
 
 
-def times_right(x, pair):
-    width = x.shape[1]
-    both = dot(jnp.concatenate(split(x), 1), pair)
+def wide_split(x):
+    return jnp.concatenate(split(x), 1)
+
+
+def fold(both):
+    width = both.shape[1] // 2
     return both[:, :width] + both[:, width:]
 
 
-def times_left(matrix, x):
-    count = matrix.shape[0] // 2
-    high, low = split(x)
-    both = dot(matrix, high)
-    return both[:count] + both[count:] + dot(matrix[:count], low)
+def signs(rows, cols, left):
+    return jnp.where(lane_iota(rows, cols) < cols // 2, left, -left).astype(F32)
 
 
 def quarter_turn(x, sign):
@@ -145,7 +145,22 @@
     return jnp.where((lanes < half) == (sign > 0), moved, -moved)
 
 
-def pack_kernel(s, where_ref, e_ref, v_ref, below_ref, above_ref, stack_ref, same_ref, other_ref):
+def send_kernel(s, e_in, v_in, e_ref, v_ref, up_ref, down_ref, sem_ref):
+    moves = [
+        pltpu.make_async_copy(e_in, e_ref, sem_ref.at[0]),
+        pltpu.make_async_copy(v_in, v_ref, sem_ref.at[1]),
+    ]
+    for move in moves:
+        move.start()
+    for move in moves:
+        move.wait()
+    up_ref[:, : s.wide] = e_ref[:, s.rows - s.wide :]
+    up_ref[:, s.wide :] = v_ref[:, s.rows - s.near :]
+    down_ref[:, : s.wide] = e_ref[:, : s.wide]
+    down_ref[:, s.wide :] = v_ref[:, : s.near]
+
+
+def pack_kernel(s, where_ref, e_ref, v_ref, below_ref, above_ref, k_ref, stack_ref, same_ref, other_ref):
     w, n, length = s.wide, s.near, s.length
     stack_ref[:, :w] = below_ref[:, :w]
     stack_ref[:, w : w + s.rows] = e_ref[...]
@@ -180,18 +195,53 @@
         put(s.pack_e + low * s.r_near, s.r_near, last, first)
 
 
-def kernel_spectrum(s, where_ref, psf_ref, y_ref, x_ref, k1_ref, k2_ref, pad_ref, a_ref):
+def toeplitz_parts(taps, size):
+    half = size // 2
+    middle = size - 1
+    parts = [[], [], []]
+    for d in range(-half + 1, half):
+        centre = taps[middle + d]
+        parts[0].append(centre)
+        for part, other in ((1, taps[middle + d - half]), (2, taps[middle + d + half])):
+            parts[part].append([other, centre])
+    return parts
+
+
+def combine(load, expression):
+    if isinstance(expression, int):
+        return load(expression)
+    return combine(load, expression[0]) - combine(load, expression[1])
+
+
+def leaves(s):
+    found = []
+    first = s.radius - (s.depth - 1)
+    for part in toeplitz_parts(list(range(first, first + 2 * s.depth - 1)), s.depth):
+        found += toeplitz_parts(part, s.depth // 2)
+    return found
+
+
+def kernel_spectrum(
+    s, where_ref, psf_in, y_in, x_in, k1_ref, k2_ref, pad_ref, a_ref, k_ref, psf_ref, y_ref, x_ref, sem_ref
+):
     taps = up8(s.extent)
+    moves = [
+        pltpu.make_async_copy(psf_in.at[pl.ds(where_ref[0], 1)], psf_ref, sem_ref.at[0]),
+        pltpu.make_async_copy(y_in, y_ref, sem_ref.at[1]),
+        pltpu.make_async_copy(x_in, x_ref, sem_ref.at[2]),
+    ]
+    for move in moves:
+        move.start()
     pad_ref[...] = jnp.zeros_like(pad_ref)
+    for move in moves:
+        move.wait()
     total = jnp.zeros((s.extent, s.extent), F32)
     for a in range(s.extent):
         total = total + psf_ref[0, a]
     total = jnp.sum(total)
     for a in range(s.extent):
         pad_ref[a * taps : a * taps + s.extent, : s.extent] = psf_ref[0, a] / total
-    a_ref[...] = times_right(pad_ref[...], y_ref[...])
-    lanes = lane_iota(s.length, s.cols)
-    half = s.cols // 2
+    a_ref[...] = fold(dot(wide_split(pad_ref[...]), y_ref[...]))
     for pair in range((s.extent + 1) // 2):
         one = a_ref[2 * pair * taps : (2 * pair + 1) * taps]
         two = a_ref[(2 * pair + 1) * taps : (2 * pair + 2) * taps]
@@ -205,12 +255,30 @@
         high, low = split(right)
         out = dot(x_ref[...], jnp.concatenate([high, high, low], 0))
         for side in (0, 1):
-            a = 2 * pair + side
-            if a < s.extent:
-                value = out[:, side * s.cols : (side + 1) * s.cols]
+            if 2 * pair + side < s.extent:
+                k_ref[2 * pair + side] = out[:, side * s.cols : (side + 1) * s.cols]
+    per_leaf = s.depth // 2 - 1
+    lanes = lane_iota(8, s.cols)
+    half = s.cols // 2
+
+    def tile(t, carry):
+        rows = pl.ds(t * 8, 8)
+        planes = {}
+
+        def load(a):
+            if a not in planes:
+                planes[a] = k_ref[a, rows]
+            return planes[a]
+
+        for leaf, diagonals in enumerate(leaves(s)):
+            for d, expression in enumerate(diagonals):
+                value = combine(load, expression)
                 moved = turn(value, half)
-                k1_ref[a] = jnp.where(lanes < half, value, moved)
-                k2_ref[a] = jnp.where(lanes < half, -moved, value)
+                k1_ref[leaf * per_leaf + d, rows] = jnp.where(lanes < half, value, moved)
+                k2_ref[leaf * per_leaf + d, rows] = jnp.where(lanes < half, -moved, value)
+        return carry
+
+    lax.fori_loop(0, s.length // 8, tile, 0)
 
 
 def main_kernel(
@@ -238,10 +306,14 @@
     p_ref,
     u_ref,
     t_ref,
+    l_ref,
+    a_ref,
+    b_ref,
 ):
     core, gx, gy = where_ref[1], where_ref[2], where_ref[3]
     half = s.cols // 2
     depth = s.depth
+    group = 4
     for source_ref, halo_ref, base in (
         (own_ref, same_ref, core * s.planes),
         (partner_ref, other_ref, (1 - core) * s.planes),
@@ -251,8 +323,12 @@
         for z in range(s.planes):
             packed = halo_ref[z * s.r_wide : (z + 1) * s.r_wide]
             for q in range(s.q_wide):
-                rows = slice(q * s.r_wide, (q + 1) * s.r_wide)
-                e_ref[base + z, rows] = jnp.where(from_halo, turn(packed, -q * s.wide), source_ref[z, rows])
+                first = q * s.r_wide
+                rows = slice(first, first + s.r_wide)
+                value = jnp.where(from_halo, turn(packed, -q * s.wide), source_ref[z, rows])
+                l_ref[base + z, rows] = wide_split(value)
+                if s.wide <= first < s.wide + s.rows:
+                    e_ref[base + z, first - s.wide : first - s.wide + s.r_wide] = value
         lanes = lane_iota(s.r_near, s.cols)
         from_halo = jnp.where(core == 0, lanes - (s.cols - s.near), s.near - 1 - lanes) >= 0
         per_plane = s.q_near // 2
@@ -267,66 +343,87 @@
                     source_ref[plane, s.length + start : s.length + start + s.r_near],
                 )
 
-    def forward(load, x_table, sign):
-        for pair in range(depth // 2):
-            parts = [times_right(load(2 * pair + side), yf_ref[0]) for side in (0, 1)]
-            right = jnp.concatenate(
-                [
-                    jnp.concatenate(parts, 1),
-                    jnp.concatenate([quarter_turn(part, 1) for part in parts], 1),
-                ],
-                0,
-            )
-            out = times_left(x_table[...], right)
+    def forward(rows, x_table, sign):
+        for z in range(0, depth, group):
+            left = l_ref[z : z + group, :rows].reshape(group * rows, 2 * s.cols)
+            high, low = split(fold(dot(left, yf_ref[0])))
+            a_ref[z : z + group, :rows] = high.reshape(group, rows, s.cols)
+            a_ref[z : z + group, s.length : s.length + rows] = low.reshape(group, rows, s.cols)
+        turned = signs(s.length, s.cols, 1.0)
+        for z in range(0, depth, 2):
+            columns = []
+            for side in (z, z + 1):
+                high, low = a_ref[side, :rows], a_ref[side, s.length : s.length + rows]
+                columns.append(jnp.concatenate([high, low, high], 0))
+            out = dot(x_table[...], jnp.concatenate(columns, 1))
             for side in (0, 1):
                 value = out[:, side * s.cols : (side + 1) * s.cols]
+                value = value[: s.length] + turned * turn(value[s.length :], half)
                 moved = turn(value, half)
-                x1_ref[2 * pair + side] = value
-                x2_ref[2 * pair + side] = moved if sign > 0 else -moved
+                x1_ref[z + side] = value
+                x2_ref[z + side] = moved if sign > 0 else -moved
 
     def along_z(flip):
-        block = 4
+        quarter = depth // 4
 
         def tile(t, carry):
             rows = pl.ds(t * 8, 8)
-            ones = [x1_ref[z, rows] for z in range(depth)]
-            twos = [x2_ref[z, rows] for z in range(depth)]
-            for start in range(0, depth, block):
-                sums = [None] * block
-                for d in range(2 * depth - 1):
-                    hits = []
-                    for k in range(block):
-                        zi = start + k + (d - (depth - 1)) * (1 if flip else -1)
-                        if 0 <= zi < depth:
-                            hits.append((k, zi))
-                    if not hits:
-                        continue
-                    tap = d - (depth - 1) + s.radius
-                    k1, k2 = k1_ref[tap, rows], k2_ref[tap, rows]
-                    for k, zi in hits:
-                        term = k1 * ones[zi] + k2 * twos[zi]
-                        sums[k] = term if sums[k] is None else sums[k] + term
-                for k in range(block):
-                    p_ref[start + k, rows] = sums[k]
+            order = (lambda z: depth - 1 - z) if flip else (lambda z: z)
+            sources = [[ref[order(z), rows] for z in range(depth)] for ref in (x1_ref, x2_ref)]
+            middle = 2 * quarter
+
+            def parts(x):
+                n = len(x) // 2
+                return [[p + q for p, q in zip(x[:n], x[n:])], x[n:], x[:n]]
+
+            def small(leaf, first, second):
+                out = []
+                for i in range(quarter):
+                    total = None
+                    for j in range(quarter):
+                        d = leaf * (2 * quarter - 1) + i - j + quarter - 1
+                        term = k1_ref[d, rows] * first[j] + k2_ref[d, rows] * second[j]
+                        total = term if total is None else total + term
+                    out.append(total)
+                return out
+
+            ones, twos = parts(sources[0]), parts(sources[1])
+            kept = None
+            for part in range(3):
+                inner_ones, inner_twos = parts(ones[part]), parts(twos[part])
+                whole_part, upper, lower = (
+                    small(3 * part + k, inner_ones[k], inner_twos[k]) for k in range(3)
+                )
+                value = [p + q for p, q in zip(whole_part, upper)] + [p + q for p, q in zip(whole_part, lower)]
+                if part == 0:
+                    kept = value
+                else:
+                    start = 0 if part == 1 else middle
+                    for i in range(middle):
+                        p_ref[order(start + i), rows] = kept[i] + value[i]
             return carry
 
         lax.fori_loop(0, s.length // 8, tile, 0)
 
-    def backward(x_table, use):
-        for pair in range(depth // 2):
-            parts = [p_ref[2 * pair + side] for side in (0, 1)]
-            right = jnp.concatenate(
-                [
-                    jnp.concatenate(parts, 1),
-                    jnp.concatenate([quarter_turn(part, -1) for part in parts], 1),
-                ],
-                0,
-            )
-            out = times_left(x_table[...], right)
+    def backward(rows, x_table, use):
+        turned = signs(rows, s.cols, -1.0)
+        for z in range(0, depth, 2):
+            columns = []
+            for side in (z, z + 1):
+                high, low = split(p_ref[side])
+                columns.append(jnp.concatenate([high, low, high], 0))
+            out = dot(x_table[...], jnp.concatenate(columns, 1))
             for side in (0, 1):
-                use(2 * pair + side, times_right(out[:, side * s.cols : (side + 1) * s.cols], yi_ref[0]))
-
-    forward(lambda z: e_ref[z], xw_ref, 1)
+                value = out[:, side * s.cols : (side + 1) * s.cols]
+                value = value[:rows] + turned * turn(value[rows:], half)
+                b_ref[z + side, :rows] = wide_split(value)
+        for z in range(0, depth, group):
+            left = b_ref[z : z + group, :rows].reshape(group * rows, 2 * s.cols)
+            out = fold(dot(left, yi_ref[0]))
+            for k in range(group):
+                use(z + k, out[k * rows : (k + 1) * rows])
+
+    forward(s.length, xw_ref, 1)
     along_z(False)
 
     shape = (s.view_rows, s.cols)
@@ -341,19 +438,24 @@
 
     def to_ratio(z, blurred):
         safe = jnp.where(inside, blurred, 1.0)
-        v_ref[z] = jnp.where(inside, v_ref[z] / safe, 0.0)
-
-    backward(xbn_ref, to_ratio)
-    forward(lambda z: v_ref[z], xn_ref, -1)
+        l_ref[z, : s.view_rows] = wide_split(jnp.where(inside, v_ref[z] / safe, 0.0))
+
+    backward(s.view_rows, xbn_ref, to_ratio)
+    forward(s.view_rows, xn_ref, -1)
     along_z(True)
 
     lane = lane_iota(s.rows, s.cols)
     owned = (lane // half) == core
 
     def to_update(z, correction):
-        u_ref[z] = jnp.where(owned, e_ref[z, s.wide : s.wide + s.rows] * correction, 0.0)
-
-    backward(xbo_ref, to_update)
+        value = jnp.where(owned, e_ref[z] * correction, 0.0)
+        u_ref[z] = value
+
+    backward(s.rows, xbo_ref, to_update)
+
+    def three(x):
+        high, rest = split(x)
+        return high, rest, (x - high.astype(F32) - rest.astype(F32)).astype(BF16)
 
     def pooled(x, factor, scale):
         count = s.cols // factor
@@ -363,15 +465,12 @@
             scale,
             0.0,
         ).astype(BF16)
-        high, rest = split(x)
-        middle = x - high.astype(F32)
-        low = (middle - rest.astype(F32)).astype(BF16)
-        return dot(high, weights) + dot(rest, weights) + dot(low, weights)
+        return dot(jnp.concatenate(three(x), 1), jnp.concatenate([weights] * 3, 0))
 
     u_rows = s.planes * s.rows
     source = u_ref
-    planes, rows, start = depth, s.rows, u_rows
-    levels = []
+    planes, rows = depth, s.rows
+    sums_of = []
     for level in (1, 2, 3, 4):
         planes, rows = planes // 2, rows // 2
         here = t_ref.at[level - 1]
@@ -382,10 +481,25 @@
         ]
         for z in range(planes):
             here[z, :rows] = sums[z]
+        sums_of.append(sums)
+        source = here
+    levels = []
+    for level, sums in enumerate(sums_of, 1):
         factor = 2**level
         value = pooled(jnp.concatenate(sums, 0), factor, 1.0 / factor**3)
-        levels.append((value, planes, rows, s.cols // factor))
-        source = here
+        levels.append((value, len(sums), sums[0].shape[0], s.cols // factor))
+    top = sums_of[-1][0]
+    own_rows = top.shape[0] // 2
+    per_chip = s.cols // 32
+    line = jnp.concatenate([top[2 * i : 2 * i + 1] + top[2 * i + 1 : 2 * i + 2] for i in range(own_rows)], 1)
+    cells = five_ref.shape[2]
+    source_lane = lax.broadcasted_iota(jnp.int32, (line.shape[1], cells), 0)
+    place = (gx * own_rows + source_lane // s.cols) * (s.gy * per_chip) + gy * per_chip + source_lane % s.cols // 32
+    weights = jnp.where(
+        place == lax.broadcasted_iota(jnp.int32, place.shape, 1), 1.0 / (32 * 32 * depth), 0.0
+    ).astype(BF16)
+    five = dot(jnp.concatenate(three(line), 1), jnp.concatenate([weights] * 3, 0))
+    five_ref[...] = jnp.broadcast_to(five[None], five_ref.shape)
     for half_index in (0, 1):
         for mine, out_ref in ((True, mine_ref), (False, theirs_ref)):
 
@@ -399,26 +513,6 @@
                     begin = half_index * count if planes > 1 else 0
                     out_ref[start : start + count, :columns] = value[begin : begin + count]
                     start += up8(count)
-    top = sums[0]
-    rows5, columns5 = five_ref.shape[1:]
-    own_rows = top.shape[0] // 2
-    row = lax.broadcasted_iota(jnp.int32, (rows5, s.cols), 0)
-    spread = jnp.zeros((rows5, s.cols), F32)
-    for i in range(own_rows):
-        spread = jnp.where(row == gx * own_rows + i, top[2 * i : 2 * i + 1] + top[2 * i + 1 : 2 * i + 2], spread)
-    factor = 32
-    per_chip = s.cols // factor
-    weights = jnp.where(
-        lax.broadcasted_iota(jnp.int32, (s.cols, columns5), 0) // factor + gy * per_chip
-        == lax.broadcasted_iota(jnp.int32, (s.cols, columns5), 1),
-        1.0 / (factor * factor * depth),
-        0.0,
-    ).astype(BF16)
-    high, rest = split(spread)
-    low = (spread - high.astype(F32) - rest.astype(F32)).astype(BF16)
-    five = dot(high, weights) + dot(rest, weights) + dot(low, weights)
-    for k in range(five_ref.shape[0]):
-        five_ref[k] = five
 
 
 def last_kernel(s, mine_ref, got_ref, fives_ref, u_ref, one_ref, two_ref, three_ref, four_ref, five_ref):
@@ -432,29 +526,41 @@
             part = slice(start + z * rows, start + (z + 1) * rows)
             out_ref[z] = mine_ref[part, :columns] + got_ref[part, :columns]
         start += up8(planes * rows)
-    total = fives_ref[0]
-    for k in range(1, fives_ref.shape[0]):
-        total = total + fives_ref[k]
-    five_ref[0] = total
+    rows, columns = five_ref.shape[1:]
+    total = jnp.sum(fives_ref[...], axis=0)
+    cells = rows * columns
+    shape = (rows, cells)
+    lane = lane_iota(*shape)
+    spread = jnp.where(lane // columns == lax.broadcasted_iota(jnp.int32, shape, 0), jnp.broadcast_to(total, shape), 0.0)
+    shape = (cells, columns)
+    ones = (lax.broadcasted_iota(jnp.int32, shape, 0) % columns == lane_iota(*shape)).astype(BF16)
+    high, rest = split(spread)
+    low = (spread - high.astype(F32) - rest.astype(F32)).astype(BF16)
+    five_ref[0] = dot(jnp.concatenate([high, rest, low], 1), jnp.concatenate([ones] * 3, 0))
+
+
+def in_hbm(x):
+    return pltpu.with_memory_space_constraint(x, pltpu.HBM)
 
 
 def whole(shape):
     return pl.BlockSpec(shape, lambda *_: (0,) * len(shape))
 
 
-def call(body, where, arrays, in_specs, outs, scratch=(), name=None):
+def call(body, where, arrays, in_specs, outs, scratch=(), narrow=(), name=None, flops=0, mib=16, copies=()):
     grid_spec = pltpu.PrefetchScalarGridSpec(
         num_scalar_prefetch=1,
         grid=(1,),
         in_specs=in_specs,
         out_specs=[whole(shape) for shape in outs],
-        scratch_shapes=[pltpu.VMEM(shape, F32) for shape in scratch],
+        scratch_shapes=[pltpu.VMEM(shape, F32) for shape in scratch] + [pltpu.VMEM(shape, BF16) for shape in narrow] + list(copies),
     )
     return pl.pallas_call(
         body,
         grid_spec=grid_spec,
         out_shape=[jax.ShapeDtypeStruct(shape, F32) for shape in outs],
-        compiler_params=pltpu.CompilerParams(vmem_limit_bytes=VMEM_LIMIT),
+        compiler_params=pltpu.CompilerParams(vmem_limit_bytes=mib * MIB),
+        cost_estimate=pl.CostEstimate(flops=flops, bytes_accessed=0, transcendentals=0) if flops else None,
         name=name,
     )(where, *arrays)
 
@@ -484,31 +590,42 @@
         [view_index[0], lax.axis_index("gz"), lax.axis_index("gx"), lax.axis_index("gy")]
     ).astype(jnp.int32)
 
-    below = lax.ppermute(
-        jnp.concatenate([estimate[:, s.rows - s.wide :], view_data[:, s.rows - s.near :]], 1), "gx", shift("gx", 1)
-    )
-    above = lax.ppermute(
-        jnp.concatenate([estimate[:, : s.wide], view_data[:, : s.near]], 1), "gx", shift("gx", -1)
-    )
+    slab = (s.planes, s.wide + s.near, s.cols)
+    outs = [estimate.shape, view_data.shape, slab, slab]
+    arrays = (in_hbm(estimate), in_hbm(view_data))
+    estimate_here, view_here, up, down = pl.pallas_call(
+        functools.partial(send_kernel, s),
+        in_specs=[pl.BlockSpec(memory_space=pltpu.HBM)] * 2,
+        out_specs=[pl.BlockSpec(memory_space=pltpu.VMEM)] * len(outs),
+        out_shape=[jax.ShapeDtypeStruct(shape, F32) for shape in outs],
+        scratch_shapes=[pltpu.SemaphoreType.DMA((2,))],
+        compiler_params=pltpu.CompilerParams(vmem_limit_bytes=8 * MIB),
+        name="send",
+    )(*arrays)
+    below = lax.ppermute(up, "gx", shift("gx", 1))
+    above = lax.ppermute(down, "gx", shift("gx", -1))
     psf_shape = (1,) + psf_stack.shape[1:]
     taps = up8(s.extent)
     k1, k2 = call(
         functools.partial(kernel_spectrum, s),
         where,
-        (psf_stack, t["y_kernel"], t["x_kernel"]),
-        [pl.BlockSpec(psf_shape, lambda i, w: (w[0], 0, 0, 0)), whole(t["y_kernel"].shape), whole(t["x_kernel"].shape)],
-        [(s.extent, s.length, s.cols)] * 2,
-        scratch=[((s.extent + 1) // 2 * 2 * taps, s.cols)] * 2,
+        (in_hbm(psf_stack), in_hbm(t["y_kernel"]), in_hbm(t["x_kernel"])),
+        [pl.BlockSpec(memory_space=pltpu.HBM)] * 3,
+        [(9 * (s.depth // 2 - 1), s.length, s.cols)] * 2,
+        scratch=[((s.extent + 1) // 2 * 2 * taps, s.cols)] * 2 + [(s.extent, s.length, s.cols), psf_shape],
+        narrow=[t["y_kernel"].shape, t["x_kernel"].shape],
+        copies=[pltpu.SemaphoreType.DMA((3,))],
         name="kernel_spectrum",
+        flops=10**8,
     )
     stack_shape = (s.planes, s.stack_rows, s.cols)
     slab_shape = (s.pack_e + s.pack_v, s.cols)
-    arrays = (estimate, view_data, below, above)
+    arrays = (estimate_here, view_here, below, above)
     stack, same, other = call(
         functools.partial(pack_kernel, s),
         where,
-        arrays,
-        [whole(a.shape) for a in arrays],
+        arrays + (k1,),
+        [whole(a.shape) for a in arrays] + [pl.BlockSpec(memory_space=pl.ANY)],
         [stack_shape, slab_shape, slab_shape],
         name="pack",
     )
@@ -549,9 +666,9 @@
         where,
         arrays,
         specs,
-        [(out_rows, s.cols), (out_rows, s.cols), (devices,) + five_shape],
+        [(out_rows, s.cols), (out_rows, s.cols), (devices, 1, five_shape[0] * five_shape[1])],
         scratch=[
-            spectrum,
+            (s.depth, s.rows, s.cols),
             (s.depth, s.view_rows, s.cols),
             spectrum,
             spectrum,
@@ -559,7 +676,13 @@
             (s.depth, s.rows, s.cols),
             (4, s.depth // 2, s.rows, s.cols),
         ],
+        narrow=[
+            (s.depth, s.length, 2 * s.cols),
+            (s.depth, 2 * s.length, s.cols),
+            (s.depth, s.view_rows, 2 * s.cols),
+        ],
         name="update",
+        mib=24,
     )
     got = lax.ppermute(theirs, "gz", [(0, 1), (1, 0)])
     fives = lax.all_to_all(five, ALL, split_axis=0, concat_axis=0, tiled=True)
@@ -572,7 +695,7 @@
             out_specs=[whole(shape) for shape in outs],
             out_shape=[jax.ShapeDtypeStruct(shape, F32) for shape in outs],
             grid=(1,),
-            compiler_params=pltpu.CompilerParams(vmem_limit_bytes=VMEM_LIMIT),
+            compiler_params=pltpu.CompilerParams(vmem_limit_bytes=8 * MIB),
             name="assemble",
         )(*arrays)
     )

time: 58.7 us -> 49.1 us (0.84)
  local copies, waits for them, and re-layouts: 6.42 us -> 0.03 us
  waiting for transfers between devices: 8.25 us -> 5.79 us
  Pallas kernels: 17.3 us -> 16.2 us
  starting transfers between devices: 13.4 us -> 14.3 us
  other arithmetic: 0.79 us -> 0.08 us
    ppermute x2, waiting for transfers between devices: 8.24 us -> 3.48 us  [the longest x1 3.48 us: local(): above = lax.ppermute(down, 'gx', shift('gx', -1))]
    unnamed x24 -> x12, local copies, waits for them, and re-layouts: 3.99 us -> 0.03 us
    ppermute x1, waiting for transfers between devices: 0.01 us -> 2.3 us  [local(): same = lax.ppermute(same, ('gy', 'gz'), to_side(True))]
    pallas_call x3, Pallas kernels: 16.6 us -> 14.4 us  [call(): pl.pallas_call(body, grid_spec=grid_spec, out_shape=[jax.ShapeDtypeStruct...]
    slice x2 -> x0, local copies, waits for them, and re-layouts: 1.92 us -> none  [the longest x1 1.03 us: local(): estimate[:, :s.wide]]
    pallas_call x0 -> x1, Pallas kernels: none -> 1.07 us  [local(): pl.pallas_call(functools.partial(send_kernel, s), in_specs=[pl.BlockSpec(...]
    ppermute x1, starting transfers between devices: 2.99 us -> 3.85 us  [local(): got = lax.ppermute(theirs, 'gz', [(0, 1), (1, 0)])]
    all_to_all x1 -> x0, other arithmetic: 0.68 us -> none  [local(): fives = lax.all_to_all(five, ALL, split_axis=0, concat_axis=0, tiled=True)]
  transfers between devices with their start and end apart: 6 -> 6, of which waited for: 2 -> 2; matrix products, arithmetic and copies ran while one was open for 3% -> 0% of each run, Pallas kernels for 3% -> 10%
where the time goes in v1:
time: 49.1 us; the launch traced here: 48.9 us
  Pallas kernels  16.2 us (33%)
  starting transfers between devices  14.3 us (29%)
  blocking collectives  11 us (22%)
  waiting for transfers between devices  5.79 us (12%)
  between operations  1.43 us (3%)
    pallas_call x3, Pallas kernels, call(): pl.pallas_call(body, grid_spec=grid_spec, out_shape=[jax.ShapeDtypeStruct...  14.4 us
    all_to_all x1, blocking collectives, local(): fives = lax.all_to_all(five, ALL, split_axis=0, concat_axis=0, tiled=True)  11 us
    ppermute x1, starting transfers between devices, local(): below = lax.ppermute(up, 'gx', shift('gx', 1))  4.88 us
    ppermute x1, starting transfers between devices, local(): got = lax.ppermute(theirs, 'gz', [(0, 1), (1, 0)])  3.85 us
    ppermute x1, starting transfers between devices, local(): same = lax.ppermute(same, ('gy', 'gz'), to_side(True))  3.49 us
    ppermute x1, waiting for transfers between devices, local(): above = lax.ppermute(down, 'gx', shift('gx', -1))  3.48 us
    ppermute x1, waiting for transfers between devices, local(): same = lax.ppermute(same, ('gy', 'gz'), to_side(True))  2.3 us
    ppermute x1, starting transfers between devices, local(): above = lax.ppermute(down, 'gx', shift('gx', -1))  1.29 us
  transfers between devices with their start and end apart: 6, of which 2 were waited for; matrix products, arithmetic and copies ran while one was open for 0% of the time, Pallas kernels for 10%

profile of v1, /device:TPU:0, one launch (start us, length us, event | category | flops | bytes accessed | tf_op | source)
XLA Modules:
  0.0 48.9 jit_solution(16100130484438181052)
XLA Ops:
  0.6 1.1 %send.1 = (f32[8,64,128]{2,1,0:T(8,128)S(1)}, f32[8,64,128]{2,1,0:T(8,128)S(1)}, f32[8,48,128]{2,1,0:T(8,128)S(1)}, f32[8,48,128]{2,1,0:T(8,128)S(1)}) custom-call(f32[8,64,128]{2,1,0:T(8,128)} %e_in.1, f32[8,64,128]{2,1,0:T(8,128)} %v_in.1), custom_call_target="tpu_custom_call" | custom-call | tf_op jit(solution)/shard_map/send/pallas_call | solution.py:596
  1.7 4.9 %collective-permute-start = (f32[8,48,128]{2,1,0:T(8,128)S(1)}, f32[8,48,128]{2,1,0:T(8,128)S(1)}, u32[]{:S(2)}, u32[]{:S(2)}) collective-permute-start(f32[8,48,128]{2,1,0:T(8,128)S(1)} %get-tuple-element.20), channel_id=1, source_target_pairs={{0,8},{8,16},{16,24},{1,9},{9,17},{17,25},{2,10},{10,18},{18,26},{... | collective-permute-start | bytes 589832 | tf_op jit(solution)/shard_map/ppermute | solution.py:605
  6.6 1.3 %collective-permute-start.1 = (f32[8,48,128]{2,1,0:T(8,128)S(1)}, f32[8,48,128]{2,1,0:T(8,128)S(1)}, u32[]{:S(2)}, u32[]{:S(2)}) collective-permute-start(f32[8,48,128]{2,1,0:T(8,128)S(1)} %get-tuple-element.21), channel_id=1, source_target_pairs={{8,0},{16,8},{24,16},{9,1},{17,9},{25,17},{10,2},{18,10},{26,18},{... | collective-permute-start | bytes 589832 | tf_op jit(solution)/shard_map/ppermute | solution.py:606
  8.6 0.1 pad_add_fusion.where_ref
  8.6 0.0 copy-start.4
  8.7 0.0 copy-start.5
  8.7 4.7 %kernel_spectrum.1 = (f32[63,128,128]{2,1,0:T(8,128)S(1)}, f32[63,128,128]{2,1,0:T(8,128)S(1)}) custom-call(s32[4]{0:T(128)S(1)} %pad_add_fusion.where_ref, f32[6,31,31,31]{3,2,1,0:T(8,128)} %psf_in.1, bf16[256,256]{1,0:T(8,128)(2,1)} %constant.29.clone.y_in, bf16[128,192]{1,0:T(8,128)(2,1)} %constant.34.clone.x_in), custom_call_target="tpu_custom_call" | custom-call | flops 100000000 | tf_op jit(solution)/shard_map/kernel_spectrum/pallas_call | solution.py:558
  13.4 0.0 collective-permute-done.below_ref
  13.4 3.5 %collective-permute-done.1.above_ref = f32[8,48,128]{2,1,0:T(8,128)S(1)} collective-permute-done((f32[8,48,128]{2,1,0:T(8,128)S(1)}, f32[8,48,128]{2,1,0:T(8,128)S(1)}, u32[]{:S(2)}, u32[]{:S(2)}) %collective-permute-start.1) | collective-permute-done | bytes 196640 | tf_op jit(solution)/shard_map/ppermute | solution.py:606
  16.9 0.8 %pack.1 = (f32[8,224,128]{2,1,0:T(8,128)S(1)}, f32[352,128]{1,0:T(8,128)S(1)}, f32[352,128]{1,0:T(8,128)S(1)}) custom-call(s32[4]{0:T(128)S(1)} %pad_add_fusion.where_ref, f32[8,64,128]{2,1,0:T(8,128)S(1)} %get-tuple-element.18.e_ref, f32[8,64,128]{2,1,0:T(8,128)S(1)} %get-tuple-element.19.v_ref, f32[8,48,128]{2,1,0:T(8,128)S(1)} %collective-permute-done.below_ref, ...), custom_call_target="tpu_custom_call" | custom-call | tf_op jit(solution)/shard_map/pack/pallas_call | solution.py:558
  17.7 0.1 collective-permute-start.2
  17.8 3.5 %collective-permute-start.3 = (f32[352,128]{1,0:T(8,128)S(1)}, f32[352,128]{1,0:T(8,128)S(1)}, u32[]{:S(2)}, u32[]{:S(2)}) collective-permute-start(f32[352,128]{1,0:T(8,128)S(1)} %get-tuple-element.24), channel_id=1, source_target_pairs={{0,2},{2,4},{3,1},{4,6},{5,3},{7,5},{8,10},{10,12},{11,9},{12,14},... | collective-permute-start | bytes 540680 | tf_op jit(solution)/shard_map/ppermute | solution.py:633
  21.3 0.7 %collective-permute-start.4 = (f32[352,128]{1,0:T(8,128)S(1)}, f32[352,128]{1,0:T(8,128)S(1)}, u32[]{:S(2)}, u32[]{:S(2)}) collective-permute-start(f32[352,128]{1,0:T(8,128)S(1)} %get-tuple-element.25), channel_id=1, source_target_pairs={{1,2},{3,4},{2,1},{5,6},{4,3},{6,5},{9,10},{11,12},{10,9},{13,14},... | collective-permute-start | bytes 540680 | tf_op jit(solution)/shard_map/ppermute | solution.py:634
  22.0 2.3 %collective-permute-done.3.same_ref = f32[352,128]{1,0:T(8,128)S(1)} collective-permute-done((f32[352,128]{1,0:T(8,128)S(1)}, f32[352,128]{1,0:T(8,128)S(1)}, u32[]{:S(2)}, u32[]{:S(2)}) %collective-permute-start.3) | collective-permute-done | bytes 180256 | tf_op jit(solution)/shard_map/ppermute | solution.py:633
  24.3 0.0 collective-permute-done.4.other_ref
  24.3 0.0 collective-permute-done.2.partner_ref
  24.3 0.0 copy-done
  24.3 0.0 copy-done.1
  24.3 0.0 copy-done.2
  24.3 8.9 %update.1 = (f32[688,128]{1,0:T(8,128)S(1)}, f32[688,128]{1,0:T(8,128)S(1)}, f32[32,1,128]{2,1,0:T(1,128)S(1)}) custom-call(s32[4]{0:T(128)S(1)} %pad_add_fusion.where_ref, f32[8,224,128]{2,1,0:T(8,128)S(1)} %get-tuple-element.23.own_ref, f32[8,224,128]{2,1,0:T(8,128)S(1)} %collective-permute-done.2.partner_ref, ...), custom_call_target="tpu_custom_call" | custom-call | tf_op jit(solution)/shard_map/update/pallas_call | solution.py:558
  33.2 3.9 %collective-permute-start.5 = (f32[688,128]{1,0:T(8,128)S(1)}, f32[688,128]{1,0:T(8,128)S(1)}, u32[]{:S(2)}, u32[]{:S(2)}) collective-permute-start(f32[688,128]{1,0:T(8,128)S(1)} %get-tuple-element.28), channel_id=1, source_target_pairs={{0,1},{1,0},{2,3},{3,2},{4,5},{5,4},{6,7},{7,6},{8,9},{9,8},{10,11... | collective-permute-start | bytes 1056776 | tf_op jit(solution)/shard_map/ppermute | solution.py:687
  37.1 11.0 %all_to_all.5.fives_ref = f32[32,1,128]{2,1,0:T(1,128)S(1)} all-to-all(f32[32,1,128]{2,1,0:T(1,128)S(1)} %get-tuple-element.29), channel_id=1, replica_groups=mesh['gx'=4,'gy'=4,'gz'=2] {'gx','gy','gz'}, dimensions={0} | all-to-all | bytes 32768 | tf_op jit(solution)/shard_map/all_to_all | solution.py:688
  48.1 0.0 collective-permute-done.5.got_ref
  48.1 0.8 %assemble.1 = (f32[8,64,128]{2,1,0:T(8,128)}, f32[4,32,64]{2,1,0:T(8,128)}, f32[2,16,32]{2,1,0:T(8,128)}, f32[1,8,16]{2,1,0:T(8,128)}, f32[1,4,8]{2,1,0:T(4,128)}, /*index=5*/f32[1,8,16]{2,1,0:T(8,128)}) custom-call(f32[688,128]{1,0:T(8,128)S(1)} %get-tuple-element.27.mine_ref, f32[688,128]{1,0:T(8,128)S(1)} %collective-permute-done.5.got_ref, ...), custom_call_target="tpu_custom_call" | custom-call | tf_op jit(solution)/shard_map/assemble/pallas_call | solution.py:692
  (7 shorter events, 0.0 us)
Async XLA Ops:
  1.7 11.7 %collective-permute-start = (f32[8,48,128]{2,1,0:T(8,128)S(1)}, f32[8,48,128]{2,1,0:T(8,128)S(1)}, u32[]{:S(2)}, u32[]{:S(2)}) collective-permute-start(f32[8,48,128]{2,1,0:T(8,128)S(1)} %get-tuple-element.20), channel_id=1, source_target_pairs={{0,8},{8,16},{16,24},{1,9},{9,17},{17,25},{2,10},{10,18},{18,26},{... | collective-permute-start | bytes 589832 | tf_op jit(solution)/shard_map/ppermute | solution.py:605
  6.6 10.3 %collective-permute-start.1 = (f32[8,48,128]{2,1,0:T(8,128)S(1)}, f32[8,48,128]{2,1,0:T(8,128)S(1)}, u32[]{:S(2)}, u32[]{:S(2)}) collective-permute-start(f32[8,48,128]{2,1,0:T(8,128)S(1)} %get-tuple-element.21), channel_id=1, source_target_pairs={{8,0},{16,8},{24,16},{9,1},{17,9},{25,17},{10,2},{18,10},{26,18},{... | collective-permute-start | bytes 589832 | tf_op jit(solution)/shard_map/ppermute | solution.py:606
  8.6 15.6 %copy-start = (bf16[2,256,256]{2,1,0:T(8,128)(2,1)S(1)}, bf16[2,256,256]{2,1,0:T(8,128)(2,1)}, u32[]{:S(2)}) copy-start(bf16[2,256,256]{2,1,0:T(8,128)(2,1)} %constant.28.clone.yi_ref) | copy-start | bytes 786436
  8.6 15.6 %copy-start.1 = (bf16[2,256,256]{2,1,0:T(8,128)(2,1)S(1)}, bf16[2,256,256]{2,1,0:T(8,128)(2,1)}, u32[]{:S(2)}) copy-start(bf16[2,256,256]{2,1,0:T(8,128)(2,1)} %constant.27.clone.yf_ref) | copy-start | bytes 786436
  8.6 15.7 %copy-start.2 = (bf16[256,288]{1,0:T(8,128)(2,1)S(1)}, bf16[256,288]{1,0:T(8,128)(2,1)}, u32[]{:S(2)}) copy-start(bf16[256,288]{1,0:T(8,128)(2,1)} %constant.31.clone.xn_ref) | copy-start | bytes 442372
  8.6 15.7 %copy-start.3 = (bf16[256,384]{1,0:T(8,128)(2,1)S(1)}, bf16[256,384]{1,0:T(8,128)(2,1)}, u32[]{:S(2)}) copy-start(bf16[256,384]{1,0:T(8,128)(2,1)} %constant.30.clone.xw_ref) | copy-start | bytes 589828
  8.6 15.7 %copy-start.4 = (bf16[192,384]{1,0:T(8,128)(2,1)S(1)}, bf16[192,384]{1,0:T(8,128)(2,1)}, u32[]{:S(2)}) copy-start(bf16[192,384]{1,0:T(8,128)(2,1)} %constant.32.clone.xbn_ref) | copy-start | bytes 442372
  8.7 15.7 %copy-start.5 = (bf16[128,384]{1,0:T(8,128)(2,1)S(1)}, bf16[128,384]{1,0:T(8,128)(2,1)}, u32[]{:S(2)}) copy-start(bf16[128,384]{1,0:T(8,128)(2,1)} %constant.33.clone.xbo_ref) | copy-start | bytes 294916
  17.7 6.6 %collective-permute-start.2 = (f32[8,224,128]{2,1,0:T(8,128)S(1)}, f32[8,224,128]{2,1,0:T(8,128)S(1)}, u32[]{:S(2)}, u32[]{:S(2)}) collective-permute-start(f32[8,224,128]{2,1,0:T(8,128)S(1)} %get-tuple-element.23.own_ref), channel_id=1, source_target_pairs={{0,1},{1,0},{2,3},{3,2},{4,5},{5,4},{6,7},{7,6},{8,9},{9,8},{10,11... | collective-permute-start | bytes 2752520 | tf_op jit(solution)/shard_map/ppermute | solution.py:632
  17.8 6.5 %collective-permute-start.3 = (f32[352,128]{1,0:T(8,128)S(1)}, f32[352,128]{1,0:T(8,128)S(1)}, u32[]{:S(2)}, u32[]{:S(2)}) collective-permute-start(f32[352,128]{1,0:T(8,128)S(1)} %get-tuple-element.24), channel_id=1, source_target_pairs={{0,2},{2,4},{3,1},{4,6},{5,3},{7,5},{8,10},{10,12},{11,9},{12,14},... | collective-permute-start | bytes 540680 | tf_op jit(solution)/shard_map/ppermute | solution.py:633
  21.3 3.0 %collective-permute-start.4 = (f32[352,128]{1,0:T(8,128)S(1)}, f32[352,128]{1,0:T(8,128)S(1)}, u32[]{:S(2)}, u32[]{:S(2)}) collective-permute-start(f32[352,128]{1,0:T(8,128)S(1)} %get-tuple-element.25), channel_id=1, source_target_pairs={{1,2},{3,4},{2,1},{5,6},{4,3},{6,5},{9,10},{11,12},{10,9},{13,14},... | collective-permute-start | bytes 540680 | tf_op jit(solution)/shard_map/ppermute | solution.py:634
  33.2 14.9 %collective-permute-start.5 = (f32[688,128]{1,0:T(8,128)S(1)}, f32[688,128]{1,0:T(8,128)S(1)}, u32[]{:S(2)}, u32[]{:S(2)}) collective-permute-start(f32[688,128]{1,0:T(8,128)S(1)} %get-tuple-element.28), channel_id=1, source_target_pairs={{0,1},{1,0},{2,3},{3,2},{4,5},{5,4},{6,7},{7,6},{8,9},{9,8},{10,11... | collective-permute-start | bytes 1056776 | tf_op jit(solution)/shard_map/ppermute | solution.py:687

commit v2 on v1

--- a/solution.py
+++ b/solution.py
@@ -60,49 +60,47 @@
     return np.block([[high, low], [high, np.zeros_like(low)]])
 
 
+def left_pair(matrix):
+    high, low = split_np(matrix)
+    return np.block([[high, high], [low, np.zeros_like(low)]])
+
+
 def tables(s):
     y_freq = 2.0 * np.pi * (np.arange(s.freqs) + 0.5) / s.cols
-    x_freq = 2.0 * np.pi * np.arange(s.length) / s.length
+    x_freq = 2.0 * np.pi * (np.arange(s.length // 2) + 0.5) / s.length
     y_forward, y_inverse = [], []
     for core in (0, 1):
         angle = lane_positions(s, core)[:, None] * y_freq[None, :]
-        y_forward.append(right_pair(np.concatenate([np.cos(angle), -np.sin(angle)], 1)))
-        back = np.concatenate([np.cos(angle), -np.sin(angle)], 1).T * (2.0 / s.cols / s.length)
-        y_inverse.append(right_pair(back))
-    offset = np.zeros(s.cols)
-    offset[: s.extent] = np.arange(s.extent) - s.radius
+        both = np.concatenate([np.cos(angle), np.sin(angle)], 1)
+        y_forward.append(right_pair(both))
+        y_inverse.append(right_pair(both.T * (2.0 / s.cols / s.length)))
+    offset = np.arange(s.cols) - s.radius
     angle = offset[:, None] * y_freq[None, :]
-    y_kernel = np.concatenate([np.cos(angle), -np.sin(angle)], 1)
+    y_kernel = np.concatenate([np.cos(angle), np.sin(angle)], 1)
     y_kernel[s.extent :] = 0.0
 
-    def x_matrix(positions):
+    def x_forward(positions):
         angle = x_freq[:, None] * positions[None, :]
-        return np.cos(angle), np.sin(angle)
-
-    def stacked(cosine, sine):
-        high, low = split_np(np.concatenate([cosine, sine], 0))
-        return np.concatenate([high, high, low], 1)
+        return np.concatenate([np.cos(angle), np.sin(angle)], 0)
+
+    def x_inverse(positions):
+        angle = positions[:, None] * x_freq[None, :]
+        return np.concatenate([np.cos(angle), -np.sin(angle)], 1)
 
     window = np.arange(s.length) - s.wide
     near = np.arange(s.view_rows) - s.near
     own = np.arange(s.rows)
     taps = np.arange(up8(s.extent)) - s.radius
-    x_window = stacked(*x_matrix(window))
-    x_near = stacked(*x_matrix(near))
-    cosine, sine = x_matrix(near)
-    x_back_near = stacked(cosine.T, sine.T)
-    cosine, sine = x_matrix(own)
-    x_back_own = stacked(cosine.T, sine.T)
-    high, low = split_np(np.concatenate(x_matrix(taps), 1))
-    x_kernel = np.concatenate([high, low, high], 1)
+    high, low = split_np(x_forward(taps))
+    x_kernel = np.concatenate([high, high, low], 1)
     return dict(
         y_forward=np.stack(y_forward),
         y_inverse=np.stack(y_inverse),
         y_kernel=right_pair(y_kernel),
-        x_window=x_window,
-        x_near=x_near,
-        x_back_near=x_back_near,
-        x_back_own=x_back_own,
+        x_window=left_pair(x_forward(window)),
+        x_near=left_pair(x_forward(near)),
+        x_back_near=left_pair(x_inverse(near)),
+        x_back_own=left_pair(x_inverse(own)),
         x_kernel=x_kernel,
     )
 
@@ -129,20 +127,26 @@
     return jnp.concatenate(split(x), 1)
 
 
+def tall_split(x):
+    return jnp.concatenate(split(x), 0)
+
+
 def fold(both):
     width = both.shape[1] // 2
     return both[:, :width] + both[:, width:]
 
 
-def signs(rows, cols, left):
-    return jnp.where(lane_iota(rows, cols) < cols // 2, left, -left).astype(F32)
-
-
-def quarter_turn(x, sign):
-    half = x.shape[1] // 2
-    lanes = lane_iota(*x.shape)
-    moved = turn(x, half)
-    return jnp.where((lanes < half) == (sign > 0), moved, -moved)
+def fold_rows(both):
+    count = both.shape[0] // 2
+    return both[:count] + both[count:]
+
+
+def spectrum_of(cosine, sine):
+    half = cosine.shape[1] // 2
+    left = lane_iota(*cosine.shape) < half
+    moved = turn(sine, half)
+    minus, plus = cosine - moved, turn(cosine + moved, half)
+    return jnp.where(left, minus, plus), jnp.where(left, -plus, minus)
 
 
 def send_kernel(s, e_in, v_in, e_ref, v_ref, up_ref, down_ref, sem_ref):
@@ -195,34 +199,17 @@
         put(s.pack_e + low * s.r_near, s.r_near, last, first)
 
 
-def toeplitz_parts(taps, size):
-    half = size // 2
-    middle = size - 1
-    parts = [[], [], []]
-    for d in range(-half + 1, half):
-        centre = taps[middle + d]
-        parts[0].append(centre)
-        for part, other in ((1, taps[middle + d - half]), (2, taps[middle + d + half])):
-            parts[part].append([other, centre])
-    return parts
-
-
-def combine(load, expression):
-    if isinstance(expression, int):
-        return load(expression)
-    return combine(load, expression[0]) - combine(load, expression[1])
-
-
-def leaves(s):
-    found = []
-    first = s.radius - (s.depth - 1)
-    for part in toeplitz_parts(list(range(first, first + 2 * s.depth - 1)), s.depth):
-        found += toeplitz_parts(part, s.depth // 2)
-    return found
+def toeplitz_parts(taps):
+    middle = len(taps) // 2
+    half = (middle + 1) // 2
+    centre = taps[middle - half + 1 : middle + half]
+    upper = [p - q for p, q in zip(taps[middle - 2 * half + 1 : middle], centre)]
+    lower = [p - q for p, q in zip(taps[middle + 1 : middle + 2 * half], centre)]
+    return centre, upper, lower
 
 
 def kernel_spectrum(
-    s, where_ref, psf_in, y_in, x_in, k1_ref, k2_ref, pad_ref, a_ref, k_ref, psf_ref, y_ref, x_ref, sem_ref
+    s, where_ref, psf_in, y_in, x_in, k_ref, ks_ref, kd_ref, pad_ref, a_ref, re_ref, im_ref, psf_ref, y_ref, x_ref, sem_ref
 ):
     taps = up8(s.extent)
     moves = [
@@ -243,42 +230,34 @@
         pad_ref[a * taps : a * taps + s.extent, : s.extent] = psf_ref[0, a] / total
     a_ref[...] = fold(dot(wide_split(pad_ref[...]), y_ref[...]))
     for pair in range((s.extent + 1) // 2):
-        one = a_ref[2 * pair * taps : (2 * pair + 1) * taps]
-        two = a_ref[(2 * pair + 1) * taps : (2 * pair + 2) * taps]
-        right = jnp.concatenate(
-            [
-                jnp.concatenate([one, two], 1),
-                jnp.concatenate([quarter_turn(one, 1), quarter_turn(two, 1)], 1),
-            ],
-            0,
-        )
-        high, low = split(right)
-        out = dot(x_ref[...], jnp.concatenate([high, high, low], 0))
+        columns = []
+        for side in (0, 1):
+            a = 2 * pair + side
+            high, low = split(a_ref[a * taps : (a + 1) * taps])
+            columns.append(jnp.concatenate([high, low, high], 0))
+        out = dot(x_ref[...], jnp.concatenate(columns, 1))
         for side in (0, 1):
             if 2 * pair + side < s.extent:
-                k_ref[2 * pair + side] = out[:, side * s.cols : (side + 1) * s.cols]
-    per_leaf = s.depth // 2 - 1
-    lanes = lane_iota(8, s.cols)
-    half = s.cols // 2
+                value = out[:, side * s.cols : (side + 1) * s.cols]
+                re_ref[2 * pair + side], im_ref[2 * pair + side] = spectrum_of(value[: s.length // 2], value[s.length // 2 :])
+    first = s.radius - (s.depth - 1)
 
     def tile(t, carry):
         rows = pl.ds(t * 8, 8)
-        planes = {}
-
-        def load(a):
-            if a not in planes:
-                planes[a] = k_ref[a, rows]
-            return planes[a]
-
-        for leaf, diagonals in enumerate(leaves(s)):
-            for d, expression in enumerate(diagonals):
-                value = combine(load, expression)
-                moved = turn(value, half)
-                k1_ref[leaf * per_leaf + d, rows] = jnp.where(lanes < half, value, moved)
-                k2_ref[leaf * per_leaf + d, rows] = jnp.where(lanes < half, -moved, value)
+        real = [re_ref[a, rows] for a in range(first, first + 2 * s.depth - 1)]
+        imag = [im_ref[a, rows] for a in range(first, first + 2 * s.depth - 1)]
+        total = [p + q for p, q in zip(real, imag)]
+        change = [q - p for p, q in zip(real, imag)]
+        for out_ref, values in ((k_ref, real), (ks_ref, total), (kd_ref, change)):
+            place = 0
+            for part in toeplitz_parts(values):
+                for inner in toeplitz_parts(part):
+                    for value in inner:
+                        out_ref[place, rows] = value
+                        place += 1
         return carry
 
-    lax.fori_loop(0, s.length // 8, tile, 0)
+    lax.fori_loop(0, s.length // 16, tile, 0)
 
 
 def main_kernel(
@@ -288,8 +267,9 @@
     partner_ref,
     same_ref,
     other_ref,
-    k1_ref,
-    k2_ref,
+    k_ref,
+    ks_ref,
+    kd_ref,
     yf_ref,
     yi_ref,
     xw_ref,
@@ -301,9 +281,10 @@
     five_ref,
     e_ref,
     v_ref,
-    x1_ref,
-    x2_ref,
-    p_ref,
+    re_ref,
+    im_ref,
+    pr_ref,
+    pi_ref,
     u_ref,
     t_ref,
     l_ref,
@@ -326,7 +307,9 @@
                 first = q * s.r_wide
                 rows = slice(first, first + s.r_wide)
                 value = jnp.where(from_halo, turn(packed, -q * s.wide), source_ref[z, rows])
-                l_ref[base + z, rows] = wide_split(value)
+                high, low = split(value)
+                l_ref[base + z, rows] = high
+                l_ref[base + z, s.length + first : s.length + first + s.r_wide] = low
                 if s.wide <= first < s.wide + s.rows:
                     e_ref[base + z, first - s.wide : first - s.wide + s.r_wide] = value
         lanes = lane_iota(s.r_near, s.cols)
@@ -343,87 +326,88 @@
                     source_ref[plane, s.length + start : s.length + start + s.r_near],
                 )
 
-    def forward(rows, x_table, sign):
+    freqs = s.length // 2
+
+    def forward(rows, x_table):
+        for z in range(0, depth, 2):
+            both = jnp.concatenate([l_ref[z, : 2 * rows], l_ref[z + 1, : 2 * rows]], 1)
+            out = fold_rows(dot(x_table[...], both))
+            for side in (0, 1):
+                a_ref[z + side] = wide_split(out[:, side * s.cols : (side + 1) * s.cols])
         for z in range(0, depth, group):
-            left = l_ref[z : z + group, :rows].reshape(group * rows, 2 * s.cols)
-            high, low = split(fold(dot(left, yf_ref[0])))
-            a_ref[z : z + group, :rows] = high.reshape(group, rows, s.cols)
-            a_ref[z : z + group, s.length : s.length + rows] = low.reshape(group, rows, s.cols)
-        turned = signs(s.length, s.cols, 1.0)
-        for z in range(0, depth, 2):
-            columns = []
-            for side in (z, z + 1):
-                high, low = a_ref[side, :rows], a_ref[side, s.length : s.length + rows]
-                columns.append(jnp.concatenate([high, low, high], 0))
-            out = dot(x_table[...], jnp.concatenate(columns, 1))
-            for side in (0, 1):
-                value = out[:, side * s.cols : (side + 1) * s.cols]
-                value = value[: s.length] + turned * turn(value[s.length :], half)
-                moved = turn(value, half)
-                x1_ref[z + side] = value
-                x2_ref[z + side] = moved if sign > 0 else -moved
+            out = fold(dot(a_ref[z : z + group].reshape(group * s.length, 2 * s.cols), yf_ref[0]))
+            for k in range(group):
+                value = out[k * s.length : (k + 1) * s.length]
+                re_ref[z + k], im_ref[z + k] = spectrum_of(value[:freqs], value[freqs:])
 
     def along_z(flip):
         quarter = depth // 4
+        order = (lambda z: depth - 1 - z) if flip else (lambda z: z)
+        for_re, for_im = (kd_ref, ks_ref) if flip else (ks_ref, kd_ref)
+
+        def parts(x):
+            n = len(x) // 2
+            return [p + q for p, q in zip(x[:n], x[n:])], x[n:], x[:n]
+
+        def joined(pieces):
+            middle, upper, lower = pieces
+            return [p + q for p, q in zip(middle, upper)] + [p + q for p, q in zip(middle, lower)]
 
         def tile(t, carry):
             rows = pl.ds(t * 8, 8)
-            order = (lambda z: depth - 1 - z) if flip else (lambda z: z)
-            sources = [[ref[order(z), rows] for z in range(depth)] for ref in (x1_ref, x2_ref)]
-            middle = 2 * quarter
-
-            def parts(x):
-                n = len(x) // 2
-                return [[p + q for p, q in zip(x[:n], x[n:])], x[n:], x[:n]]
-
-            def small(leaf, first, second):
-                out = []
-                for i in range(quarter):
-                    total = None
-                    for j in range(quarter):
-                        d = leaf * (2 * quarter - 1) + i - j + quarter - 1
-                        term = k1_ref[d, rows] * first[j] + k2_ref[d, rows] * second[j]
-                        total = term if total is None else total + term
-                    out.append(total)
-                return out
-
-            ones, twos = parts(sources[0]), parts(sources[1])
+            real = [re_ref[order(z), rows] for z in range(depth)]
+            imag = [im_ref[order(z), rows] for z in range(depth)]
+            outer = [parts(x) for x in ([p + q for p, q in zip(real, imag)], imag, real)]
             kept = None
             for part in range(3):
-                inner_ones, inner_twos = parts(ones[part]), parts(twos[part])
-                whole_part, upper, lower = (
-                    small(3 * part + k, inner_ones[k], inner_twos[k]) for k in range(3)
-                )
-                value = [p + q for p, q in zip(whole_part, upper)] + [p + q for p, q in zip(whole_part, lower)]
+                inner = [parts(x[part]) for x in outer]
+                pieces = []
+                for piece in range(3):
+                    found = []
+                    for i in range(quarter):
+                        sums = []
+                        for table, values in zip((k_ref, for_re, for_im), inner):
+                            total = None
+                            for j in range(quarter):
+                                d = (3 * part + piece) * (2 * quarter - 1) + i - j + quarter - 1
+                                term = table[d, rows] * values[piece][j]
+                                total = term if total is None else total + term
+                            sums.append(total)
+                        if flip:
+                            found.append((sums[0] + sums[1], sums[0] - sums[2]))
+                        else:
+                            found.append((sums[0] - sums[1], sums[0] + sums[2]))
+                    pieces.append(found)
+                value = [joined([[f[k] for f in found] for found in pieces]) for k in (0, 1)]
                 if part == 0:
                     kept = value
                 else:
-                    start = 0 if part == 1 else middle
-                    for i in range(middle):
-                        p_ref[order(start + i), rows] = kept[i] + value[i]
+                    start = 0 if part == 1 else 2 * quarter
+                    for i in range(2 * quarter):
+                        pr_ref[order(start + i), rows] = kept[0][i] + value[0][i]
+                        pi_ref[order(start + i), rows] = kept[1][i] + value[1][i]
             return carry
 
-        lax.fori_loop(0, s.length // 8, tile, 0)
+        lax.fori_loop(0, freqs // 8, tile, 0)
 
     def backward(rows, x_table, use):
-        turned = signs(rows, s.cols, -1.0)
+        half_lanes = lane_iota(freqs, s.cols) < half
+        for z in range(0, depth, group):
+            pieces = []
+            for k in range(group):
+                real, imag = pr_ref[z + k], pi_ref[z + k]
+                turned_real, turned_imag = turn(real, half), turn(imag, half)
+                pieces.append(jnp.where(half_lanes, real + turned_real, imag - turned_imag))
+                pieces.append(jnp.where(half_lanes, imag + turned_imag, turned_real - real))
+            out = fold(dot(wide_split(jnp.concatenate(pieces, 0)), yi_ref[0]))
+            for k in range(group):
+                b_ref[z + k] = tall_split(out[k * s.length : (k + 1) * s.length])
         for z in range(0, depth, 2):
-            columns = []
-            for side in (z, z + 1):
-                high, low = split(p_ref[side])
-                columns.append(jnp.concatenate([high, low, high], 0))
-            out = dot(x_table[...], jnp.concatenate(columns, 1))
+            out = fold_rows(dot(x_table[...], jnp.concatenate([b_ref[z], b_ref[z + 1]], 1)))
             for side in (0, 1):
-                value = out[:, side * s.cols : (side + 1) * s.cols]
-                value = value[:rows] + turned * turn(value[rows:], half)
-                b_ref[z + side, :rows] = wide_split(value)
-        for z in range(0, depth, group):
-            left = b_ref[z : z + group, :rows].reshape(group * rows, 2 * s.cols)
-            out = fold(dot(left, yi_ref[0]))
-            for k in range(group):
-                use(z + k, out[k * rows : (k + 1) * rows])
-
-    forward(s.length, xw_ref, 1)
+                use(z + side, out[:, side * s.cols : (side + 1) * s.cols])
+
+    forward(s.length, xw_ref)
     along_z(False)
 
     shape = (s.view_rows, s.cols)
@@ -438,10 +422,10 @@
 
     def to_ratio(z, blurred):
         safe = jnp.where(inside, blurred, 1.0)
-        l_ref[z, : s.view_rows] = wide_split(jnp.where(inside, v_ref[z] / safe, 0.0))
+        l_ref[z, : 2 * s.view_rows] = tall_split(jnp.where(inside, v_ref[z] / safe, 0.0))
 
     backward(s.view_rows, xbn_ref, to_ratio)
-    forward(s.view_rows, xn_ref, -1)
+    forward(s.view_rows, xn_ref)
     along_z(True)
 
     lane = lane_iota(s.rows, s.cols)
@@ -606,13 +590,13 @@
     above = lax.ppermute(down, "gx", shift("gx", -1))
     psf_shape = (1,) + psf_stack.shape[1:]
     taps = up8(s.extent)
-    k1, k2 = call(
+    k, ks, kd = call(
         functools.partial(kernel_spectrum, s),
         where,
         (in_hbm(psf_stack), in_hbm(t["y_kernel"]), in_hbm(t["x_kernel"])),
         [pl.BlockSpec(memory_space=pltpu.HBM)] * 3,
-        [(9 * (s.depth // 2 - 1), s.length, s.cols)] * 2,
-        scratch=[((s.extent + 1) // 2 * 2 * taps, s.cols)] * 2 + [(s.extent, s.length, s.cols), psf_shape],
+        [(9 * (s.depth // 2 - 1), s.length // 2, s.cols)] * 3,
+        scratch=[((s.extent + 1) // 2 * 2 * taps, s.cols)] * 2 + [(s.extent, s.length // 2, s.cols)] * 2 + [psf_shape],
         narrow=[t["y_kernel"].shape, t["x_kernel"].shape],
         copies=[pltpu.SemaphoreType.DMA((3,))],
         name="kernel_spectrum",
@@ -624,7 +608,7 @@
     stack, same, other = call(
         functools.partial(pack_kernel, s),
         where,
-        arrays + (k1,),
+        arrays + (k,),
         [whole(a.shape) for a in arrays] + [pl.BlockSpec(memory_space=pl.ANY)],
         [stack_shape, slab_shape, slab_shape],
         name="pack",
@@ -648,8 +632,9 @@
         partner,
         same,
         other,
-        k1,
-        k2,
+        k,
+        ks,
+        kd,
         t["y_forward"],
         t["y_inverse"],
         t["x_window"],
@@ -658,9 +643,9 @@
         t["x_back_own"],
     )
     specs = [whole(a.shape) for a in arrays]
-    for k in (6, 7):
+    for k in (7, 8):
         specs[k] = pl.BlockSpec((1,) + arrays[k].shape[1:], lambda i, w: (w[1], 0, 0))
-    spectrum = (s.depth, s.length, s.cols)
+    spectrum = (s.depth, s.length // 2, s.cols)
     mine, theirs, five = call(
         functools.partial(main_kernel, s),
         where,
@@ -673,13 +658,14 @@
             spectrum,
             spectrum,
             spectrum,
+            spectrum,
             (s.depth, s.rows, s.cols),
             (4, s.depth // 2, s.rows, s.cols),
         ],
         narrow=[
+            (s.depth, 2 * s.length, s.cols),
             (s.depth, s.length, 2 * s.cols),
             (s.depth, 2 * s.length, s.cols),
-            (s.depth, s.view_rows, 2 * s.cols),
         ],
         name="update",
         mib=24,

time: 49.1 us -> 47.8 us (0.974)
  Pallas kernels: 16.2 us -> 13.9 us
  waiting for transfers between devices: 5.79 us -> 6.87 us
    pallas_call x3, Pallas kernels: 14.4 us -> 12 us  [call(): pl.pallas_call(body, grid_spec=grid_spec, out_shape=[jax.ShapeDtypeStruct...]
    ppermute x1, waiting for transfers between devices: 3.48 us -> 4.55 us  [local(): above = lax.ppermute(down, 'gx', shift('gx', -1))]
  transfers between devices with their start and end apart: 6 -> 6, of which waited for: 2 -> 2; matrix products, arithmetic and copies ran while one was open for 0% -> 0% of each run, Pallas kernels for 10% -> 8%
where the time goes in v2:
time: 47.8 us; the launch traced here: 47.6 us
  starting transfers between devices  14.3 us (30%)
  Pallas kernels  13.9 us (29%)
  blocking collectives  11 us (23%)
  waiting for transfers between devices  6.87 us (14%)
  between operations  1.46 us (3%)
    pallas_call x3, Pallas kernels, call(): pl.pallas_call(body, grid_spec=grid_spec, out_shape=[jax.ShapeDtypeStruct...  12 us
    all_to_all x1, blocking collectives, local(): fives = lax.all_to_all(five, ALL, split_axis=0, concat_axis=0, tiled=True)  11 us
    ppermute x1, starting transfers between devices, local(): below = lax.ppermute(up, 'gx', shift('gx', 1))  4.88 us
    ppermute x1, waiting for transfers between devices, local(): above = lax.ppermute(down, 'gx', shift('gx', -1))  4.55 us
    ppermute x1, starting transfers between devices, local(): got = lax.ppermute(theirs, 'gz', [(0, 1), (1, 0)])  3.86 us
    ppermute x1, starting transfers between devices, local(): same = lax.ppermute(same, ('gy', 'gz'), to_side(True))  3.49 us
    ppermute x1, waiting for transfers between devices, local(): same = lax.ppermute(same, ('gy', 'gz'), to_side(True))  2.3 us
    ppermute x1, starting transfers between devices, local(): above = lax.ppermute(down, 'gx', shift('gx', -1))  1.29 us
  transfers between devices with their start and end apart: 6, of which 2 were waited for; matrix products, arithmetic and copies ran while one was open for 0% of the time, Pallas kernels for 8%

profile of v2, /device:TPU:0, one launch (start us, length us, event | category | flops | bytes accessed | tf_op | source)
XLA Modules:
  0.0 47.6 jit_solution(17768381192753152657)
XLA Ops:
  0.6 1.1 %send.1 = (f32[8,64,128]{2,1,0:T(8,128)S(1)}, f32[8,64,128]{2,1,0:T(8,128)S(1)}, f32[8,48,128]{2,1,0:T(8,128)S(1)}, f32[8,48,128]{2,1,0:T(8,128)S(1)}) custom-call(f32[8,64,128]{2,1,0:T(8,128)} %e_in.1, f32[8,64,128]{2,1,0:T(8,128)} %v_in.1), custom_call_target="tpu_custom_call" | custom-call | tf_op jit(solution)/shard_map/send/pallas_call | solution.py:580
  1.7 4.9 %collective-permute-start = (f32[8,48,128]{2,1,0:T(8,128)S(1)}, f32[8,48,128]{2,1,0:T(8,128)S(1)}, u32[]{:S(2)}, u32[]{:S(2)}) collective-permute-start(f32[8,48,128]{2,1,0:T(8,128)S(1)} %get-tuple-element.21), channel_id=1, source_target_pairs={{0,8},{8,16},{16,24},{1,9},{9,17},{17,25},{2,10},{10,18},{18,26},{... | collective-permute-start | bytes 589832 | tf_op jit(solution)/shard_map/ppermute | solution.py:589
  6.6 1.3 %collective-permute-start.1 = (f32[8,48,128]{2,1,0:T(8,128)S(1)}, f32[8,48,128]{2,1,0:T(8,128)S(1)}, u32[]{:S(2)}, u32[]{:S(2)}) collective-permute-start(f32[8,48,128]{2,1,0:T(8,128)S(1)} %get-tuple-element.22), channel_id=1, source_target_pairs={{8,0},{16,8},{24,16},{9,1},{17,9},{25,17},{10,2},{18,10},{26,18},{... | collective-permute-start | bytes 589832 | tf_op jit(solution)/shard_map/ppermute | solution.py:590
  8.6 0.1 pad_add_fusion.where_ref
  8.6 3.6 %kernel_spectrum.1 = (f32[63,64,128]{2,1,0:T(8,128)S(1)}, f32[63,64,128]{2,1,0:T(8,128)S(1)}, f32[63,64,128]{2,1,0:T(8,128)S(1)}) custom-call(s32[4]{0:T(128)S(1)} %pad_add_fusion.where_ref, f32[6,31,31,31]{3,2,1,0:T(8,128)} %psf_in.1, bf16[256,256]{1,0:T(8,128)(2,1)} %constant.29.clone.y_in, bf16[128,96]{1,0:T(8,128)(2,1)} %constant.34.clone.x_in), custom_call_target="tpu_custom_call" | custom-call | flops 100000000 | tf_op jit(solution)/shard_map/kernel_spectrum/pallas_call | solution.py:542
  12.3 0.0 copy-start
  12.3 0.0 copy-start.1
  12.3 0.0 copy-start.2
  12.3 0.0 copy-start.3
  12.3 0.0 copy-start.4
  12.3 0.0 copy-start.5
  12.3 0.0 collective-permute-done.below_ref
  12.3 4.6 %collective-permute-done.1.above_ref = f32[8,48,128]{2,1,0:T(8,128)S(1)} collective-permute-done((f32[8,48,128]{2,1,0:T(8,128)S(1)}, f32[8,48,128]{2,1,0:T(8,128)S(1)}, u32[]{:S(2)}, u32[]{:S(2)}) %collective-permute-start.1) | collective-permute-done | bytes 196640 | tf_op jit(solution)/shard_map/ppermute | solution.py:590
  16.9 0.8 %pack.1 = (f32[8,224,128]{2,1,0:T(8,128)S(1)}, f32[352,128]{1,0:T(8,128)S(1)}, f32[352,128]{1,0:T(8,128)S(1)}) custom-call(s32[4]{0:T(128)S(1)} %pad_add_fusion.where_ref, f32[8,64,128]{2,1,0:T(8,128)S(1)} %get-tuple-element.19.e_ref, f32[8,64,128]{2,1,0:T(8,128)S(1)} %get-tuple-element.20.v_ref, f32[8,48,128]{2,1,0:T(8,128)S(1)} %collective-permute-done.below_ref, ...), custom_call_target="tpu_custom_call" | custom-call | tf_op jit(solution)/shard_map/pack/pallas_call | solution.py:542
  17.7 0.1 collective-permute-start.2
  17.8 3.5 %collective-permute-start.3 = (f32[352,128]{1,0:T(8,128)S(1)}, f32[352,128]{1,0:T(8,128)S(1)}, u32[]{:S(2)}, u32[]{:S(2)}) collective-permute-start(f32[352,128]{1,0:T(8,128)S(1)} %get-tuple-element.25), channel_id=1, source_target_pairs={{0,2},{2,4},{3,1},{4,6},{5,3},{7,5},{8,10},{10,12},{11,9},{12,14},... | collective-permute-start | bytes 540680 | tf_op jit(solution)/shard_map/ppermute | solution.py:617
  21.3 0.7 %collective-permute-start.4 = (f32[352,128]{1,0:T(8,128)S(1)}, f32[352,128]{1,0:T(8,128)S(1)}, u32[]{:S(2)}, u32[]{:S(2)}) collective-permute-start(f32[352,128]{1,0:T(8,128)S(1)} %get-tuple-element.26), channel_id=1, source_target_pairs={{1,2},{3,4},{2,1},{5,6},{4,3},{6,5},{9,10},{11,12},{10,9},{13,14},... | collective-permute-start | bytes 540680 | tf_op jit(solution)/shard_map/ppermute | solution.py:618
  22.0 2.3 %collective-permute-done.3.same_ref = f32[352,128]{1,0:T(8,128)S(1)} collective-permute-done((f32[352,128]{1,0:T(8,128)S(1)}, f32[352,128]{1,0:T(8,128)S(1)}, u32[]{:S(2)}, u32[]{:S(2)}) %collective-permute-start.3) | collective-permute-done | bytes 180256 | tf_op jit(solution)/shard_map/ppermute | solution.py:617
  24.3 0.0 collective-permute-done.4.other_ref
  24.3 0.0 collective-permute-done.2.partner_ref
  24.3 7.6 %update.1 = (f32[688,128]{1,0:T(8,128)S(1)}, f32[688,128]{1,0:T(8,128)S(1)}, f32[32,1,128]{2,1,0:T(1,128)S(1)}) custom-call(s32[4]{0:T(128)S(1)} %pad_add_fusion.where_ref, f32[8,224,128]{2,1,0:T(8,128)S(1)} %get-tuple-element.24.own_ref, f32[8,224,128]{2,1,0:T(8,128)S(1)} %collective-permute-done.2.partner_ref, ...), custom_call_target="tpu_custom_call" | custom-call | tf_op jit(solution)/shard_map/update/pallas_call | solution.py:542
  31.9 3.9 %collective-permute-start.5 = (f32[688,128]{1,0:T(8,128)S(1)}, f32[688,128]{1,0:T(8,128)S(1)}, u32[]{:S(2)}, u32[]{:S(2)}) collective-permute-start(f32[688,128]{1,0:T(8,128)S(1)} %get-tuple-element.30), channel_id=1, source_target_pairs={{0,1},{1,0},{2,3},{3,2},{4,5},{5,4},{6,7},{7,6},{8,9},{9,8},{10,11... | collective-permute-start | bytes 1056776 | tf_op jit(solution)/shard_map/ppermute | solution.py:673
  35.8 11.0 %all_to_all.5.fives_ref = f32[32,1,128]{2,1,0:T(1,128)S(1)} all-to-all(f32[32,1,128]{2,1,0:T(1,128)S(1)} %get-tuple-element.31), channel_id=1, replica_groups=mesh['gx'=4,'gy'=4,'gz'=2] {'gx','gy','gz'}, dimensions={0} | all-to-all | bytes 32768 | tf_op jit(solution)/shard_map/all_to_all | solution.py:674
  46.8 0.8 %assemble.1 = (f32[8,64,128]{2,1,0:T(8,128)}, f32[4,32,64]{2,1,0:T(8,128)}, f32[2,16,32]{2,1,0:T(8,128)}, f32[1,8,16]{2,1,0:T(8,128)}, f32[1,4,8]{2,1,0:T(4,128)}, /*index=5*/f32[1,8,16]{2,1,0:T(8,128)}) custom-call(f32[688,128]{1,0:T(8,128)S(1)} %get-tuple-element.29.mine_ref, f32[688,128]{1,0:T(8,128)S(1)} %collective-permute-done.5.got_ref, ...), custom_call_target="tpu_custom_call" | custom-call | tf_op jit(solution)/shard_map/assemble/pallas_call | solution.py:678
  (7 shorter events, 0.0 us)
Async XLA Ops:
  1.7 10.6 %collective-permute-start = (f32[8,48,128]{2,1,0:T(8,128)S(1)}, f32[8,48,128]{2,1,0:T(8,128)S(1)}, u32[]{:S(2)}, u32[]{:S(2)}) collective-permute-start(f32[8,48,128]{2,1,0:T(8,128)S(1)} %get-tuple-element.21), channel_id=1, source_target_pairs={{0,8},{8,16},{16,24},{1,9},{9,17},{17,25},{2,10},{10,18},{18,26},{... | collective-permute-start | bytes 589832 | tf_op jit(solution)/shard_map/ppermute | solution.py:589
  6.6 10.3 %collective-permute-start.1 = (f32[8,48,128]{2,1,0:T(8,128)S(1)}, f32[8,48,128]{2,1,0:T(8,128)S(1)}, u32[]{:S(2)}, u32[]{:S(2)}) collective-permute-start(f32[8,48,128]{2,1,0:T(8,128)S(1)} %get-tuple-element.22), channel_id=1, source_target_pairs={{8,0},{16,8},{24,16},{9,1},{17,9},{25,17},{10,2},{18,10},{26,18},{... | collective-permute-start | bytes 589832 | tf_op jit(solution)/shard_map/ppermute | solution.py:590
  12.3 12.0 %copy-start = (bf16[2,256,256]{2,1,0:T(8,128)(2,1)S(1)}, bf16[2,256,256]{2,1,0:T(8,128)(2,1)}, u32[]{:S(2)}) copy-start(bf16[2,256,256]{2,1,0:T(8,128)(2,1)} %constant.28.clone.yi_ref) | copy-start | bytes 786436
  12.3 12.0 %copy-start.1 = (bf16[2,256,256]{2,1,0:T(8,128)(2,1)S(1)}, bf16[2,256,256]{2,1,0:T(8,128)(2,1)}, u32[]{:S(2)}) copy-start(bf16[2,256,256]{2,1,0:T(8,128)(2,1)} %constant.27.clone.yf_ref) | copy-start | bytes 786436
  12.3 12.0 %copy-start.2 = (bf16[256,192]{1,0:T(8,128)(2,1)S(1)}, bf16[256,192]{1,0:T(8,128)(2,1)}, u32[]{:S(2)}) copy-start(bf16[256,192]{1,0:T(8,128)(2,1)} %constant.31.clone.xn_ref) | copy-start | bytes 294916
  12.3 12.0 %copy-start.3 = (bf16[256,256]{1,0:T(8,128)(2,1)S(1)}, bf16[256,256]{1,0:T(8,128)(2,1)}, u32[]{:S(2)}) copy-start(bf16[256,256]{1,0:T(8,128)(2,1)} %constant.30.clone.xw_ref) | copy-start | bytes 393220
  12.3 12.0 %copy-start.4 = (bf16[192,256]{1,0:T(8,128)(2,1)S(1)}, bf16[192,256]{1,0:T(8,128)(2,1)}, u32[]{:S(2)}) copy-start(bf16[192,256]{1,0:T(8,128)(2,1)} %constant.32.clone.xbn_ref) | copy-start | bytes 294916
  12.3 12.0 %copy-start.5 = (bf16[128,256]{1,0:T(8,128)(2,1)S(1)}, bf16[128,256]{1,0:T(8,128)(2,1)}, u32[]{:S(2)}) copy-start(bf16[128,256]{1,0:T(8,128)(2,1)} %constant.33.clone.xbo_ref) | copy-start | bytes 196612
  17.7 6.6 %collective-permute-start.2 = (f32[8,224,128]{2,1,0:T(8,128)S(1)}, f32[8,224,128]{2,1,0:T(8,128)S(1)}, u32[]{:S(2)}, u32[]{:S(2)}) collective-permute-start(f32[8,224,128]{2,1,0:T(8,128)S(1)} %get-tuple-element.24.own_ref), channel_id=1, source_target_pairs={{0,1},{1,0},{2,3},{3,2},{4,5},{5,4},{6,7},{7,6},{8,9},{9,8},{10,11... | collective-permute-start | bytes 2752520 | tf_op jit(solution)/shard_map/ppermute | solution.py:616
  17.8 6.5 %collective-permute-start.3 = (f32[352,128]{1,0:T(8,128)S(1)}, f32[352,128]{1,0:T(8,128)S(1)}, u32[]{:S(2)}, u32[]{:S(2)}) collective-permute-start(f32[352,128]{1,0:T(8,128)S(1)} %get-tuple-element.25), channel_id=1, source_target_pairs={{0,2},{2,4},{3,1},{4,6},{5,3},{7,5},{8,10},{10,12},{11,9},{12,14},... | collective-permute-start | bytes 540680 | tf_op jit(solution)/shard_map/ppermute | solution.py:617
  21.3 3.0 %collective-permute-start.4 = (f32[352,128]{1,0:T(8,128)S(1)}, f32[352,128]{1,0:T(8,128)S(1)}, u32[]{:S(2)}, u32[]{:S(2)}) collective-permute-start(f32[352,128]{1,0:T(8,128)S(1)} %get-tuple-element.26), channel_id=1, source_target_pairs={{1,2},{3,4},{2,1},{5,6},{4,3},{6,5},{9,10},{11,12},{10,9},{13,14},... | collective-permute-start | bytes 540680 | tf_op jit(solution)/shard_map/ppermute | solution.py:618
  31.9 14.9 %collective-permute-start.5 = (f32[688,128]{1,0:T(8,128)S(1)}, f32[688,128]{1,0:T(8,128)S(1)}, u32[]{:S(2)}, u32[]{:S(2)}) collective-permute-start(f32[688,128]{1,0:T(8,128)S(1)} %get-tuple-element.30), channel_id=1, source_target_pairs={{0,1},{1,0},{2,3},{3,2},{4,5},{5,4},{6,7},{7,6},{8,9},{9,8},{10,11... | collective-permute-start | bytes 1056776 | tf_op jit(solution)/shard_map/ppermute | solution.py:673

commit v3 on v2

--- a/solution.py
+++ b/solution.py
@@ -30,17 +30,14 @@
         self.near = up8(self.radius)
         self.length = self.rows + 2 * self.wide
         self.view_rows = self.rows + 2 * self.near
-        self.stack_rows = self.length + self.view_rows
         self.freqs = self.cols // 2
         self.q_wide = self.cols // self.wide
-        self.r_wide = self.length // self.q_wide
         self.q_near = self.cols // self.near
-        self.r_near = self.view_rows * 2 // self.q_near
-        self.pack_e = self.planes * self.r_wide
-        self.pack_v = self.planes // 2 * self.r_near
+        self.pack_e = self.depth // self.q_wide * self.length
+        self.pack_v = self.depth // self.q_near * self.view_rows
         self.gx, self.gy = gx, gy
         assert self.half + 2 * self.wide == self.cols == 128
-        assert self.wide <= self.rows and self.r_wide % 8 == 0 and self.r_near % 8 == 0
+        assert self.wide <= self.rows and self.depth % self.q_near == 0
         assert self.depth == 16
 
 
@@ -149,54 +146,68 @@
     return jnp.where(left, minus, plus), jnp.where(left, -plus, minus)
 
 
-def send_kernel(s, e_in, v_in, e_ref, v_ref, up_ref, down_ref, sem_ref):
+def send_kernel(s, e_in, v_in, both_ref, even_ref, odd_ref, sem_ref):
     moves = [
-        pltpu.make_async_copy(e_in, e_ref, sem_ref.at[0]),
-        pltpu.make_async_copy(v_in, v_ref, sem_ref.at[1]),
+        pltpu.make_async_copy(e_in, both_ref.at[:, : s.rows], sem_ref.at[0]),
+        pltpu.make_async_copy(v_in, both_ref.at[:, s.rows :], sem_ref.at[1]),
     ]
     for move in moves:
         move.start()
+    even = lax.axis_index("gx") % 2 == 0
     for move in moves:
         move.wait()
-    up_ref[:, : s.wide] = e_ref[:, s.rows - s.wide :]
-    up_ref[:, s.wide :] = v_ref[:, s.rows - s.near :]
-    down_ref[:, : s.wide] = e_ref[:, : s.wide]
-    down_ref[:, s.wide :] = v_ref[:, : s.near]
-
-
-def pack_kernel(s, where_ref, e_ref, v_ref, below_ref, above_ref, k_ref, stack_ref, same_ref, other_ref):
-    w, n, length = s.wide, s.near, s.length
-    stack_ref[:, :w] = below_ref[:, :w]
-    stack_ref[:, w : w + s.rows] = e_ref[...]
-    stack_ref[:, w + s.rows : length] = above_ref[:, :w]
-    stack_ref[:, length : length + n] = below_ref[:, w:]
-    stack_ref[:, length + n : length + n + s.rows] = v_ref[...]
-    stack_ref[:, length + n + s.rows :] = above_ref[:, w:]
-    first_core = where_ref[1] == 0
-
-    def put(start, count, last, first):
-        same_ref[pl.ds(start, count)] = jnp.where(first_core, last, first)
-        other_ref[pl.ds(start, count)] = jnp.where(first_core, first, last)
-
-    group = lane_iota(s.r_wide, s.cols) // w
+    place = 0
     for z in range(s.planes):
-        last = first = jnp.zeros((s.r_wide, s.cols), F32)
-        for q in range(s.q_wide):
-            moved = turn(stack_ref[z, q * s.r_wide : (q + 1) * s.r_wide], q * w)
-            last = jnp.where(group == (q - 1) % s.q_wide, moved, last)
-            first = jnp.where(group == q, moved, first)
-        put(z * s.r_wide, s.r_wide, last, first)
-    group = lane_iota(s.r_near, s.cols) // n
-    per_plane = s.q_near // 2
-    for low in range(s.planes // 2):
-        last = first = jnp.zeros((s.r_near, s.cols), F32)
-        for j in range(s.q_near):
-            plane = j // per_plane * (s.planes // 2) + low
-            start = length + j % per_plane * s.r_near
-            moved = turn(stack_ref[plane, start : start + s.r_near], j * n)
-            last = jnp.where(group == (j - 1) % s.q_near, moved, last)
-            first = jnp.where(group == j, moved, first)
-        put(s.pack_e + low * s.r_near, s.r_near, last, first)
+        for start, count in ((0, 2 * s.radius), (s.rows, s.radius)):
+            low = both_ref[z, start : start + count]
+            high = both_ref[z, start + s.rows - count : start + s.rows]
+            even_ref[place : place + count] = jnp.where(even, high, low)
+            odd_ref[place : place + count] = jnp.where(even, low, high)
+            place += count
+
+
+def pack_kernel(
+    s, where_ref, own_ref, partner_ref, even_ref, odd_ref, even2_ref, odd2_ref, k_ref, l_ref, v_ref, e_slab_ref, v_slab_ref, w_ref
+):
+    core = where_ref[1]
+    even = where_ref[2] % 2 == 0
+    wide, near = 2 * s.radius, s.radius
+    for both_ref, e_x_ref, o_x_ref, base in (
+        (own_ref, even_ref, odd_ref, core * s.planes),
+        (partner_ref, even2_ref, odd2_ref, (1 - core) * s.planes),
+    ):
+        for z in range(s.planes):
+            here = base + z
+            first = z * (wide + near)
+            for start, count, pad, rows, out_ref, source in (
+                (first, wide, s.wide, s.length, w_ref, 0),
+                (first + wide, near, s.near, s.view_rows, v_ref, s.rows),
+            ):
+                part = slice(start, start + count)
+                out_ref[here, :8] = jnp.zeros((8, s.cols), F32)
+                out_ref[here, rows - 8 :] = jnp.zeros((8, s.cols), F32)
+                out_ref[here, pad - count : pad] = jnp.where(even, o_x_ref[part], e_x_ref[part])
+                out_ref[here, pad : pad + s.rows] = both_ref[z, source : source + s.rows]
+                out_ref[here, pad + s.rows : pad + s.rows + count] = jnp.where(even, e_x_ref[part], o_x_ref[part])
+    for z in range(s.depth):
+        l_ref[z] = tall_split(w_ref[z])
+    for rows, group, width, slab_ref, source_ref in (
+        (s.length, s.q_wide, s.wide, e_slab_ref, w_ref),
+        (s.view_rows, s.q_near, s.near, v_slab_ref, v_ref),
+    ):
+        lanes = (lane_iota(rows, s.cols) // width + core) % group
+        for q in range(s.depth // group):
+            packed = source_ref[q * group]
+            for p in range(1, group):
+                packed = jnp.where(lanes == p, turn(source_ref[q * group + p], p * width), packed)
+            slab_ref[q * rows : (q + 1) * rows] = packed
+
+
+def along_x_kernel(s, l_ref, x_ref, t_ref):
+    for z in range(0, s.depth, 2):
+        out = fold_rows(dot(x_ref[...], jnp.concatenate([l_ref[z], l_ref[z + 1]], 1)))
+        for side in (0, 1):
+            t_ref[z + side] = out[:, side * s.cols : (side + 1) * s.cols]
 
 
 def toeplitz_parts(taps):
@@ -260,80 +271,25 @@
     lax.fori_loop(0, s.length // 16, tile, 0)
 
 
-def main_kernel(
-    s,
-    where_ref,
-    own_ref,
-    partner_ref,
-    same_ref,
-    other_ref,
-    k_ref,
-    ks_ref,
-    kd_ref,
-    yf_ref,
-    yi_ref,
-    xw_ref,
-    xn_ref,
-    xbn_ref,
-    xbo_ref,
-    mine_ref,
-    theirs_ref,
-    five_ref,
-    e_ref,
-    v_ref,
-    re_ref,
-    im_ref,
-    pr_ref,
-    pi_ref,
-    u_ref,
-    t_ref,
-    l_ref,
-    a_ref,
-    b_ref,
-):
-    core, gx, gy = where_ref[1], where_ref[2], where_ref[3]
+def from_side(core, rows, cols, width):
+    lanes = lane_iota(rows, cols)
+    return jnp.where(core == 0, lanes - (cols - width), width - 1 - lanes) >= 0
+
+
+def stages(s, k_ref, ks_ref, kd_ref, yf_ref, yi_ref, re_ref, im_ref, pr_ref, pi_ref, a_ref, b_ref, l_ref=None):
     half = s.cols // 2
     depth = s.depth
     group = 4
-    for source_ref, halo_ref, base in (
-        (own_ref, same_ref, core * s.planes),
-        (partner_ref, other_ref, (1 - core) * s.planes),
-    ):
-        lanes = lane_iota(s.r_wide, s.cols)
-        from_halo = jnp.where(core == 0, lanes - (s.cols - s.wide), s.wide - 1 - lanes) >= 0
-        for z in range(s.planes):
-            packed = halo_ref[z * s.r_wide : (z + 1) * s.r_wide]
-            for q in range(s.q_wide):
-                first = q * s.r_wide
-                rows = slice(first, first + s.r_wide)
-                value = jnp.where(from_halo, turn(packed, -q * s.wide), source_ref[z, rows])
-                high, low = split(value)
-                l_ref[base + z, rows] = high
-                l_ref[base + z, s.length + first : s.length + first + s.r_wide] = low
-                if s.wide <= first < s.wide + s.rows:
-                    e_ref[base + z, first - s.wide : first - s.wide + s.r_wide] = value
-        lanes = lane_iota(s.r_near, s.cols)
-        from_halo = jnp.where(core == 0, lanes - (s.cols - s.near), s.near - 1 - lanes) >= 0
-        per_plane = s.q_near // 2
-        for low in range(s.planes // 2):
-            packed = halo_ref[s.pack_e + low * s.r_near : s.pack_e + (low + 1) * s.r_near]
-            for j in range(s.q_near):
-                plane = j // per_plane * (s.planes // 2) + low
-                start = j % per_plane * s.r_near
-                v_ref[base + plane, start : start + s.r_near] = jnp.where(
-                    from_halo,
-                    turn(packed, -j * s.near),
-                    source_ref[plane, s.length + start : s.length + start + s.r_near],
-                )
-
     freqs = s.length // 2
 
-    def forward(rows, x_table):
+    def forward_x(rows, x_table):
         for z in range(0, depth, 2):
             both = jnp.concatenate([l_ref[z, : 2 * rows], l_ref[z + 1, : 2 * rows]], 1)
             out = fold_rows(dot(x_table[...], both))
             for side in (0, 1):
                 a_ref[z + side] = wide_split(out[:, side * s.cols : (side + 1) * s.cols])
+
+    def forward_y():
         for z in range(0, depth, group):
             out = fold(dot(a_ref[z : z + group].reshape(group * s.length, 2 * s.cols), yf_ref[0]))
             for k in range(group):
@@ -407,8 +363,46 @@
             for side in (0, 1):
                 use(z + side, out[:, side * s.cols : (side + 1) * s.cols])
 
-    forward(s.length, xw_ref)
+    return forward_x, forward_y, along_z, backward
+
+
+def first_kernel(
+    s, where_ref, t_in_ref, slab_ref, k_ref, ks_ref, kd_ref, yf_ref, yi_ref, xw_ref, xbn_ref, blurred_ref,
+    re_ref, im_ref, pr_ref, pi_ref, a_ref, b_ref,
+):
+    core = where_ref[1]
+    _, forward_y, along_z, backward = stages(
+        s, k_ref, ks_ref, kd_ref, yf_ref, yi_ref, re_ref, im_ref, pr_ref, pi_ref, a_ref, b_ref
+    )
+    arrived = from_side(core, s.length, s.cols, s.wide)
+    for q in range(0, s.depth // s.q_wide, 2):
+        both = jnp.concatenate([slab_ref[(q + k) * s.length : (q + k + 1) * s.length] for k in (0, 1)], 1)
+        out = fold_rows(dot(xw_ref[...], tall_split(both)))
+        for k in (0, 1):
+            side = out[:, k * s.cols : (k + 1) * s.cols]
+            for p in range(s.q_wide):
+                z = (q + k) * s.q_wide + p
+                a_ref[z] = wide_split(jnp.where(arrived, turn(side, -p * s.wide), t_in_ref[z]))
+    forward_y()
     along_z(False)
+
+    def keep(z, blurred):
+        blurred_ref[z] = blurred
+
+    backward(s.view_rows, xbn_ref, keep)
+
+
+def second_kernel(
+    s, where_ref, blurred_ref, v_in_ref, own_ref, partner_ref, slab_ref, k_ref, ks_ref, kd_ref, yf_ref, yi_ref,
+    xn_ref, xbo_ref, mine_ref, theirs_ref, five_ref,
+    re_ref, im_ref, pr_ref, pi_ref, u_ref, t_ref, l_ref, a_ref, b_ref,
+):
+    core, gx, gy = where_ref[1], where_ref[2], where_ref[3]
+    half = s.cols // 2
+    depth = s.depth
+    forward_x, forward_y, along_z, backward = stages(
+        s, k_ref, ks_ref, kd_ref, yf_ref, yi_ref, re_ref, im_ref, pr_ref, pi_ref, a_ref, b_ref, l_ref
+    )
 
     shape = (s.view_rows, s.cols)
     row = lax.broadcasted_iota(jnp.int32, shape, 0) - s.near
@@ -420,20 +414,24 @@
     begin = core * half - s.near
     inside = inside & (column >= begin) & (column < begin + half + 2 * s.near)
 
-    def to_ratio(z, blurred):
-        safe = jnp.where(inside, blurred, 1.0)
-        l_ref[z, : 2 * s.view_rows] = tall_split(jnp.where(inside, v_ref[z] / safe, 0.0))
-
-    backward(s.view_rows, xbn_ref, to_ratio)
-    forward(s.view_rows, xn_ref)
+    near_arrived = from_side(core, s.view_rows, s.cols, s.near)
+    for z in range(depth):
+        safe = jnp.where(inside, blurred_ref[z], 1.0)
+        first = z // s.q_near * s.view_rows
+        side = turn(slab_ref[first : first + s.view_rows], -(z % s.q_near) * s.near)
+        recorded = jnp.where(near_arrived, side, v_in_ref[z])
+        l_ref[z, : 2 * s.view_rows] = tall_split(jnp.where(inside, recorded / safe, 0.0))
+    forward_x(s.view_rows, xn_ref)
+    forward_y()
     along_z(True)
 
     lane = lane_iota(s.rows, s.cols)
     owned = (lane // half) == core
 
     def to_update(z, correction):
-        value = jnp.where(owned, e_ref[z] * correction, 0.0)
-        u_ref[z] = value
+        plane = z % s.planes
+        estimate = jnp.where(core == z // s.planes, own_ref[plane, : s.rows], partner_ref[plane, : s.rows])
+        u_ref[z] = jnp.where(owned, estimate * correction, 0.0)
 
     backward(s.rows, xbo_ref, to_update)
 
@@ -532,36 +530,35 @@
 
 
 def call(body, where, arrays, in_specs, outs, scratch=(), narrow=(), name=None, flops=0, mib=16, copies=()):
+    outs = [out if isinstance(out[0], tuple) else (out, F32) for out in outs]
     grid_spec = pltpu.PrefetchScalarGridSpec(
         num_scalar_prefetch=1,
         grid=(1,),
         in_specs=in_specs,
-        out_specs=[whole(shape) for shape in outs],
+        out_specs=[whole(shape) for shape, _ in outs],
         scratch_shapes=[pltpu.VMEM(shape, F32) for shape in scratch] + [pltpu.VMEM(shape, BF16) for shape in narrow] + list(copies),
     )
     return pl.pallas_call(
         body,
         grid_spec=grid_spec,
-        out_shape=[jax.ShapeDtypeStruct(shape, F32) for shape in outs],
+        out_shape=[jax.ShapeDtypeStruct(*out) for out in outs],
         compiler_params=pltpu.CompilerParams(vmem_limit_bytes=mib * MIB),
         cost_estimate=pl.CostEstimate(flops=flops, bytes_accessed=0, transcendentals=0) if flops else None,
         name=name,
     )(where, *arrays)
 
 
-def shift(axis, step):
-    count = lax.axis_size(axis)
-    return [(i, i + step) for i in range(count) if 0 <= i + step < count]
-
-
-def to_side(same):
+def neighbours(first):
     pairs = []
-    for h in range(lax.axis_size("gy")):
-        sender_up, sender_down = (0, 1) if same else (1, 0)
-        if h + 1 < lax.axis_size("gy"):
-            pairs.append((2 * h + sender_up, 2 * (h + 1)))
-        if h > 0:
-            pairs.append((2 * h + sender_down, 2 * (h - 1) + 1))
+    for i in range(first, lax.axis_size("gx") - 1, 2):
+        pairs += [(i, i + 1), (i + 1, i)]
+    return pairs
+
+
+def to_side():
+    pairs = []
+    for h in range(lax.axis_size("gy") - 1):
+        pairs += [(2 * h + 1, 2 * h + 2), (2 * h + 2, 2 * h + 1)]
     return pairs
 
 
@@ -574,10 +571,10 @@
         [view_index[0], lax.axis_index("gz"), lax.axis_index("gx"), lax.axis_index("gy")]
     ).astype(jnp.int32)
 
-    slab = (s.planes, s.wide + s.near, s.cols)
-    outs = [estimate.shape, view_data.shape, slab, slab]
-    arrays = (in_hbm(estimate), in_hbm(view_data))
-    estimate_here, view_here, up, down = pl.pallas_call(
+    both_shape = (s.planes, 2 * s.rows, s.cols)
+    strip = (s.planes * 3 * s.radius, s.cols)
+    outs = [both_shape, strip, strip]
+    own, to_even, to_odd = pl.pallas_call(
         functools.partial(send_kernel, s),
         in_specs=[pl.BlockSpec(memory_space=pltpu.HBM)] * 2,
         out_specs=[pl.BlockSpec(memory_space=pltpu.VMEM)] * len(outs),
@@ -585,9 +582,11 @@
         scratch_shapes=[pltpu.SemaphoreType.DMA((2,))],
         compiler_params=pltpu.CompilerParams(vmem_limit_bytes=8 * MIB),
         name="send",
-    )(*arrays)
-    below = lax.ppermute(up, "gx", shift("gx", 1))
-    above = lax.ppermute(down, "gx", shift("gx", -1))
+    )(in_hbm(estimate), in_hbm(view_data))
+    across = [(0, 1), (1, 0)]
+    partner = lax.ppermute(own, "gz", across)
+    even = lax.ppermute(to_even, "gx", neighbours(0))
+    odd = lax.ppermute(to_odd, "gx", neighbours(1))
     psf_shape = (1,) + psf_stack.shape[1:]
     taps = up8(s.extent)
     k, ks, kd = call(
@@ -602,20 +601,31 @@
         name="kernel_spectrum",
         flops=10**8,
     )
-    stack_shape = (s.planes, s.stack_rows, s.cols)
-    slab_shape = (s.pack_e + s.pack_v, s.cols)
-    arrays = (estimate_here, view_here, below, above)
-    stack, same, other = call(
+    even, _ = lax.optimization_barrier((even, k))
+    even_partner = lax.ppermute(even, "gz", across)
+    odd, _ = lax.optimization_barrier((odd, even_partner))
+    odd_partner = lax.ppermute(odd, "gz", across)
+    arrays = (own, partner, even, odd, even_partner, odd_partner)
+    window = (s.depth, s.length, s.cols)
+    view_window = (s.depth, s.view_rows, s.cols)
+    split_window, view_here, slab, view_slab = call(
         functools.partial(pack_kernel, s),
         where,
         arrays + (k,),
         [whole(a.shape) for a in arrays] + [pl.BlockSpec(memory_space=pl.ANY)],
-        [stack_shape, slab_shape, slab_shape],
+        [((s.depth, 2 * s.length, s.cols), BF16), view_window, (s.pack_e, s.cols), (s.pack_v, s.cols)],
+        scratch=[window],
         name="pack",
     )
-    partner = lax.ppermute(stack, "gz", [(0, 1), (1, 0)])
-    same = lax.ppermute(same, ("gy", "gz"), to_side(True))
-    other = lax.ppermute(other, ("gy", "gz"), to_side(False))
+    view_slab = lax.ppermute(view_slab, ("gy", "gz"), to_side())
+    slab = lax.ppermute(slab, ("gy", "gz"), to_side())
+    along_x = pl.pallas_call(
+        functools.partial(along_x_kernel, s),
+        out_shape=jax.ShapeDtypeStruct(window, F32),
+        compiler_params=pltpu.CompilerParams(vmem_limit_bytes=16 * MIB),
+        cost_estimate=pl.CostEstimate(flops=10**8, bytes_accessed=0, transcendentals=0),
+        name="along_x",
+    )(split_window, t["x_window"])
 
     u_rows = s.planes * s.rows
     out_rows = u_rows
@@ -627,46 +637,36 @@
         out_rows += up8(level_shapes[-1][0] * rows)
     devices = 2 * gx * gy
     five_shape = (rows // 2 * gx, columns // 2 * gy)
-    arrays = (
-        stack,
-        partner,
-        same,
-        other,
-        k,
-        ks,
-        kd,
-        t["y_forward"],
-        t["y_inverse"],
-        t["x_window"],
-        t["x_near"],
-        t["x_back_near"],
-        t["x_back_own"],
-    )
-    specs = [whole(a.shape) for a in arrays]
-    for k in (7, 8):
-        specs[k] = pl.BlockSpec((1,) + arrays[k].shape[1:], lambda i, w: (w[1], 0, 0))
-    spectrum = (s.depth, s.length // 2, s.cols)
+    spectra = [(s.depth, s.length // 2, s.cols)] * 4
+    halves = [(s.depth, s.length, 2 * s.cols), (s.depth, 2 * s.length, s.cols)]
+
+    def of_core(x):
+        return pl.BlockSpec((1,) + x.shape[1:], lambda i, w: (w[1], 0, 0))
+
+    tables_of = (k, ks, kd, t["y_forward"], t["y_inverse"])
+    tables_specs = [whole(a.shape) for a in tables_of[:3]] + [of_core(a) for a in tables_of[3:]]
+    before, after = (along_x, slab), (t["x_window"], t["x_back_near"])
+    (blurred,) = call(
+        functools.partial(first_kernel, s),
+        where,
+        before + tables_of + after,
+        [whole(a.shape) for a in before] + tables_specs + [whole(a.shape) for a in after],
+        [view_window],
+        scratch=spectra,
+        narrow=halves,
+        name="blur",
+        mib=24,
+        flops=10**8,
+    )
+    before, after = (blurred, view_here, own, partner, view_slab), (t["x_near"], t["x_back_own"])
     mine, theirs, five = call(
-        functools.partial(main_kernel, s),
+        functools.partial(second_kernel, s),
         where,
-        arrays,
-        specs,
+        before + tables_of + after,
+        [whole(a.shape) for a in before] + tables_specs + [whole(a.shape) for a in after],
         [(out_rows, s.cols), (out_rows, s.cols), (devices, 1, five_shape[0] * five_shape[1])],
-        scratch=[
-            (s.depth, s.rows, s.cols),
-            (s.depth, s.view_rows, s.cols),
-            spectrum,
-            spectrum,
-            spectrum,
-            spectrum,
-            (s.depth, s.rows, s.cols),
-            (4, s.depth // 2, s.rows, s.cols),
-        ],
-        narrow=[
-            (s.depth, 2 * s.length, s.cols),
-            (s.depth, s.length, 2 * s.cols),
-            (s.depth, 2 * s.length, s.cols),
-        ],
+        scratch=spectra + [(s.depth, s.rows, s.cols), (4, s.depth // 2, s.rows, s.cols)],
+        narrow=[(s.depth, 2 * s.view_rows, s.cols)] + halves,
         name="update",
         mib=24,
     )

time: 47.8 us -> 46.3 us (0.969)
  waiting for transfers between devices: 6.87 us -> 2.12 us
  blocking collectives: 11 us -> 14.8 us
  starting transfers between devices: 14.3 us -> 12.4 us
  Pallas kernels: 13.9 us -> 15.2 us
    ppermute x5 -> x7, waiting for transfers between devices: 6.86 us -> 2.12 us  [the longest x1 1.05 us: local(): even_partner = lax.ppermute(even, 'gz', across)]
    ppermute x5 -> x7, starting transfers between devices: 10.4 us -> 6.11 us  [the longest x1 3.03 us: local(): even = lax.ppermute(to_even, 'gx', neighbours(0))]
    all_to_all x1, blocking collectives: 11 us -> 14.8 us  [local(): fives = lax.all_to_all(five, ALL, split_axis=0, concat_axis=0, tiled=True)]
    ppermute x1, starting transfers between devices: 3.86 us -> 6.3 us  [local(): got = lax.ppermute(theirs, 'gz', [(0, 1), (1, 0)])]
    pallas_call x3 -> x4, Pallas kernels: 12 us -> 12.9 us  [call(): pl.pallas_call(body, grid_spec=grid_spec, out_shape=[jax.ShapeDtypeStruct...]
  transfers between devices with their start and end apart: 6 -> 8, of which waited for: 2 -> 2; matrix products, arithmetic and copies ran while one was open for 0% -> 0% of each run, Pallas kernels for 8% -> 17%
where the time goes in v3:
time: 46.3 us; the launch traced here: 46.1 us
  Pallas kernels  15.2 us (33%)
  blocking collectives  14.8 us (32%)
  starting transfers between devices  12.4 us (27%)
  waiting for transfers between devices  2.12 us (5%)
  between operations  1.47 us (3%)
    all_to_all x1, blocking collectives, local(): fives = lax.all_to_all(five, ALL, split_axis=0, concat_axis=0, tiled=True)  14.8 us
    pallas_call x4, Pallas kernels, call(): pl.pallas_call(body, grid_spec=grid_spec, out_shape=[jax.ShapeDtypeStruct...  12.9 us
    ppermute x1, starting transfers between devices, local(): got = lax.ppermute(theirs, 'gz', [(0, 1), (1, 0)])  6.3 us
    ppermute x1, starting transfers between devices, local(): even = lax.ppermute(to_even, 'gx', neighbours(0))  3.03 us
    pallas_call x1, Pallas kernels, local(): pl.pallas_call(functools.partial(send_kernel, s), in_specs=[pl.BlockSpec(...  1.08 us
    ppermute x1, waiting for transfers between devices, local(): even_partner = lax.ppermute(even, 'gz', across)  1.05 us
    ppermute x1, waiting for transfers between devices, local(): odd_partner = lax.ppermute(odd, 'gz', across)  1.05 us
  transfers between devices with their start and end apart: 8, of which 2 were waited for; matrix products, arithmetic and copies ran while one was open for 0% of the time, Pallas kernels for 17%

profile of v3, /device:TPU:0, one launch (start us, length us, event | category | flops | bytes accessed | tf_op | source)
XLA Modules:
  0.0 46.1 jit_solution(4110650802759518740)
XLA Ops:
  0.6 1.1 %send.1 = (f32[8,128,128]{2,1,0:T(8,128)S(1)}, f32[360,128]{1,0:T(8,128)S(1)}, f32[360,128]{1,0:T(8,128)S(1)}) custom-call(f32[8,64,128]{2,1,0:T(8,128)} %e_in.1, f32[8,64,128]{2,1,0:T(8,128)} %v_in.1), custom_call_target="tpu_custom_call" | custom-call | tf_op jit(solution)/shard_map/send/pallas_call | solution.py:577
  1.7 3.0 %collective-permute-start.1 = (f32[360,128]{1,0:T(8,128)S(1)}, f32[360,128]{1,0:T(8,128)S(1)}, u32[]{:S(2)}, u32[]{:S(2)}) collective-permute-start(f32[360,128]{1,0:T(8,128)S(1)} %get-tuple-element.22), channel_id=1, source_target_pairs={{0,8},{8,0},{16,24},{24,16},{1,9},{9,1},{17,25},{25,17},{2,10},{10... | collective-permute-start | bytes 552968 | tf_op jit(solution)/shard_map/ppermute | solution.py:588
  4.8 0.7 %collective-permute-start.2 = (f32[360,128]{1,0:T(8,128)S(1)}, f32[360,128]{1,0:T(8,128)S(1)}, u32[]{:S(2)}, u32[]{:S(2)}) collective-permute-start(f32[360,128]{1,0:T(8,128)S(1)} %get-tuple-element.25), channel_id=1, source_target_pairs={{8,16},{16,8},{9,17},{17,9},{10,18},{18,10},{11,19},{19,11},{12,20... | collective-permute-start | bytes 552968 | tf_op jit(solution)/shard_map/ppermute | solution.py:589
  6.1 0.1 pad_add_fusion.where_ref
  6.1 3.6 %kernel_spectrum.1 = (f32[63,64,128]{2,1,0:T(8,128)S(1)}, f32[63,64,128]{2,1,0:T(8,128)S(1)}, f32[63,64,128]{2,1,0:T(8,128)S(1)}) custom-call(s32[4]{0:T(128)S(1)} %pad_add_fusion.where_ref, f32[6,31,31,31]{3,2,1,0:T(8,128)} %psf_in.1, bf16[256,256]{1,0:T(8,128)(2,1)} %constant.29.clone.y_in, bf16[128,96]{1,0:T(8,128)(2,1)} %constant.34.clone.x_in), custom_call_target="tpu_custom_call" | custom-call | flops 100000000 | tf_op jit(solution)/shard_map/kernel_spectrum/pallas_call | solution.py:541
  9.8 0.0 copy-start.2
  9.8 0.6 %collective-permute-start.3 = (f32[360,128]{1,0:T(8,128)S(1)}, f32[360,128]{1,0:T(8,128)S(1)}, u32[]{:S(2)}, u32[]{:S(2)}) collective-permute-start(f32[360,128]{1,0:T(8,128)S(1)} %collective-permute-done.1.even_ref), channel_id=1, source_target_pairs={{0,1},{1,0},{2,3},{3,2},{4,5},{5,4},{6,7},{7,6},{8,9},{9,8},{10,11... | collective-permute-start | bytes 552968 | tf_op jit(solution)/shard_map/ppermute | solution.py:605
  10.4 1.1 %collective-permute-done.3.even2_ref = f32[360,128]{1,0:T(8,128)S(1)} collective-permute-done((f32[360,128]{1,0:T(8,128)S(1)}, f32[360,128]{1,0:T(8,128)S(1)}, u32[]{:S(2)}, u32[]{:S(2)}) %collective-permute-start.3) | collective-permute-done | bytes 184352 | tf_op jit(solution)/shard_map/ppermute | solution.py:605
  11.4 0.4 collective-permute-start.4
  11.8 1.1 %collective-permute-done.4.odd2_ref = f32[360,128]{1,0:T(8,128)S(1)} collective-permute-done((f32[360,128]{1,0:T(8,128)S(1)}, f32[360,128]{1,0:T(8,128)S(1)}, u32[]{:S(2)}, u32[]{:S(2)}) %collective-permute-start.4) | collective-permute-done | bytes 184352 | tf_op jit(solution)/shard_map/ppermute | solution.py:607
  12.8 1.1 %pack.1 = (bf16[16,256,128]{2,1,0:T(8,128)(2,1)S(1)}, f32[16,96,128]{2,1,0:T(8,128)S(1)}, f32[512,128]{1,0:T(8,128)S(1)}, f32[192,128]{1,0:T(8,128)S(1)}) custom-call(s32[4]{0:T(128)S(1)} %pad_add_fusion.where_ref, f32[8,128,128]{2,1,0:T(8,128)S(1)} %get-tuple-element.21.own_ref, f32[8,128,128]{2,1,0:T(8,128)S(1)} %collective-permute-done.partner_ref, ...), custom_call_target="tpu_custom_call" | custom-call | tf_op jit(solution)/shard_map/pack/pallas_call | solution.py:541
  14.0 0.0 copy-start
  14.0 0.0 copy-start.1
  14.0 0.0 copy-start.4
  14.0 0.8 %collective-permute-start.5 = (f32[512,128]{1,0:T(8,128)S(1)}, f32[512,128]{1,0:T(8,128)S(1)}, u32[]{:S(2)}, u32[]{:S(2)}) collective-permute-start(f32[512,128]{1,0:T(8,128)S(1)} %get-tuple-element.28), channel_id=1, source_target_pairs={{1,2},{2,1},{3,4},{4,3},{5,6},{6,5},{9,10},{10,9},{11,12},{12,11},... | collective-permute-start | bytes 786440 | tf_op jit(solution)/shard_map/ppermute | solution.py:621
  14.8 0.7 %collective-permute-start.6 = (f32[192,128]{1,0:T(8,128)S(1)}, f32[192,128]{1,0:T(8,128)S(1)}, u32[]{:S(2)}, u32[]{:S(2)}) collective-permute-start(f32[192,128]{1,0:T(8,128)S(1)} %get-tuple-element.32), channel_id=1, source_target_pairs={{1,2},{2,1},{3,4},{4,3},{5,6},{6,5},{9,10},{10,9},{11,12},{12,11},... | collective-permute-start | bytes 294920 | tf_op jit(solution)/shard_map/ppermute | solution.py:620
  15.5 0.4 along_x.1.t_in_ref
  16.0 0.0 copy-start.3
  16.0 0.0 copy-start.5
  16.0 3.9 %blur.1.blurred_ref = f32[16,96,128]{2,1,0:T(8,128)S(1)} custom-call(s32[4]{0:T(128)S(1)} %pad_add_fusion.where_ref, f32[16,128,128]{2,1,0:T(8,128)S(1)} %along_x.1.t_in_ref, f32[512,128]{1,0:T(8,128)S(1)} %collective-permute-done.5.slab_ref, f32[63,64,128]{2,1,0:T(8,128)S(1)} %get-tuple-element.23.k_ref, f32[63,64,128]{2,1,0:T(8,128)S(1)} %get-tuple-element.29.ks_ref, ...), custom_call_target="tpu_custom_call" | custom-call | flops 100000000 | tf_op jit(solution)/shard_map/blur/pallas_call | solution.py:541
  19.9 4.3 %update.1 = (f32[688,128]{1,0:T(8,128)S(1)}, f32[688,128]{1,0:T(8,128)S(1)}, f32[32,1,128]{2,1,0:T(1,128)S(1)}) custom-call(s32[4]{0:T(128)S(1)} %pad_add_fusion.where_ref, f32[16,96,128]{2,1,0:T(8,128)S(1)} %blur.1.blurred_ref, f32[16,96,128]{2,1,0:T(8,128)S(1)} %get-tuple-element.31.v_in_ref, f32[8,128,128]{2,1,0:T(8,128)S(1)} %get-tuple-element.21.own_ref, ...), custom_call_target="tpu_custom_call" | custom-call | tf_op jit(solution)/shard_map/update/pallas_call | solution.py:541
  24.2 6.3 %collective-permute-start.7 = (f32[688,128]{1,0:T(8,128)S(1)}, f32[688,128]{1,0:T(8,128)S(1)}, u32[]{:S(2)}, u32[]{:S(2)}) collective-permute-start(f32[688,128]{1,0:T(8,128)S(1)} %get-tuple-element.34), channel_id=1, source_target_pairs={{0,1},{1,0},{2,3},{3,2},{4,5},{5,4},{6,7},{7,6},{8,9},{9,8},{10,11... | collective-permute-start | bytes 1056776 | tf_op jit(solution)/shard_map/ppermute | solution.py:673
  30.5 14.8 %all_to_all.5.fives_ref = f32[32,1,128]{2,1,0:T(1,128)S(1)} all-to-all(f32[32,1,128]{2,1,0:T(1,128)S(1)} %get-tuple-element.35), channel_id=1, replica_groups=mesh['gx'=4,'gy'=4,'gz'=2] {'gx','gy','gz'}, dimensions={0} | all-to-all | bytes 32768 | tf_op jit(solution)/shard_map/all_to_all | solution.py:674
  45.3 0.8 %assemble.1 = (f32[8,64,128]{2,1,0:T(8,128)}, f32[4,32,64]{2,1,0:T(8,128)}, f32[2,16,32]{2,1,0:T(8,128)}, f32[1,8,16]{2,1,0:T(8,128)}, f32[1,4,8]{2,1,0:T(4,128)}, /*index=5*/f32[1,8,16]{2,1,0:T(8,128)}) custom-call(f32[688,128]{1,0:T(8,128)S(1)} %get-tuple-element.33.mine_ref, f32[688,128]{1,0:T(8,128)S(1)} %collective-permute-done.7.got_ref, ...), custom_call_target="tpu_custom_call" | custom-call | tf_op jit(solution)/shard_map/assemble/pallas_call | solution.py:678
  (13 shorter events, 0.0 us)
Async XLA Ops:
  1.7 8.1 %collective-permute-start.1 = (f32[360,128]{1,0:T(8,128)S(1)}, f32[360,128]{1,0:T(8,128)S(1)}, u32[]{:S(2)}, u32[]{:S(2)}) collective-permute-start(f32[360,128]{1,0:T(8,128)S(1)} %get-tuple-element.22), channel_id=1, source_target_pairs={{0,8},{8,0},{16,24},{24,16},{1,9},{9,1},{17,25},{25,17},{2,10},{10... | collective-permute-start | bytes 552968 | tf_op jit(solution)/shard_map/ppermute | solution.py:588
  4.7 7.0 %collective-permute-start = (f32[8,128,128]{2,1,0:T(8,128)S(1)}, f32[8,128,128]{2,1,0:T(8,128)S(1)}, u32[]{:S(2)}, u32[]{:S(2)}) collective-permute-start(f32[8,128,128]{2,1,0:T(8,128)S(1)} %get-tuple-element.21.own_ref), channel_id=1, source_target_pairs={{0,1},{1,0},{2,3},{3,2},{4,5},{5,4},{6,7},{7,6},{8,9},{9,8},{10,11... | collective-permute-start | bytes 1572872 | tf_op jit(solution)/shard_map/ppermute | solution.py:587
  4.8 5.6 %collective-permute-start.2 = (f32[360,128]{1,0:T(8,128)S(1)}, f32[360,128]{1,0:T(8,128)S(1)}, u32[]{:S(2)}, u32[]{:S(2)}) collective-permute-start(f32[360,128]{1,0:T(8,128)S(1)} %get-tuple-element.25), channel_id=1, source_target_pairs={{8,16},{16,8},{9,17},{17,9},{10,18},{18,10},{11,19},{19,11},{12,20... | collective-permute-start | bytes 552968 | tf_op jit(solution)/shard_map/ppermute | solution.py:589
  9.8 5.8 %copy-start.2 = (bf16[256,256]{1,0:T(8,128)(2,1)S(1)}, bf16[256,256]{1,0:T(8,128)(2,1)}, u32[]{:S(2)}) copy-start(bf16[256,256]{1,0:T(8,128)(2,1)} %constant.30.clone.x_ref.xw_ref) | copy-start | bytes 393220
  9.8 1.6 %collective-permute-start.3 = (f32[360,128]{1,0:T(8,128)S(1)}, f32[360,128]{1,0:T(8,128)S(1)}, u32[]{:S(2)}, u32[]{:S(2)}) collective-permute-start(f32[360,128]{1,0:T(8,128)S(1)} %collective-permute-done.1.even_ref), channel_id=1, source_target_pairs={{0,1},{1,0},{2,3},{3,2},{4,5},{5,4},{6,7},{7,6},{8,9},{9,8},{10,11... | collective-permute-start | bytes 552968 | tf_op jit(solution)/shard_map/ppermute | solution.py:605
  11.4 1.4 %collective-permute-start.4 = (f32[360,128]{1,0:T(8,128)S(1)}, f32[360,128]{1,0:T(8,128)S(1)}, u32[]{:S(2)}, u32[]{:S(2)}) collective-permute-start(f32[360,128]{1,0:T(8,128)S(1)} %collective-permute-done.2.odd_ref), channel_id=1, source_target_pairs={{0,1},{1,0},{2,3},{3,2},{4,5},{5,4},{6,7},{7,6},{8,9},{9,8},{10,11... | collective-permute-start | bytes 552968 | tf_op jit(solution)/shard_map/ppermute | solution.py:607
  14.0 2.0 %copy-start = (bf16[2,256,256]{2,1,0:T(8,128)(2,1)S(1)}, bf16[2,256,256]{2,1,0:T(8,128)(2,1)}, u32[]{:S(2)}) copy-start(bf16[2,256,256]{2,1,0:T(8,128)(2,1)} %constant.28.clone.yi_ref) | copy-start | bytes 786436
  14.0 2.0 %copy-start.1 = (bf16[2,256,256]{2,1,0:T(8,128)(2,1)S(1)}, bf16[2,256,256]{2,1,0:T(8,128)(2,1)}, u32[]{:S(2)}) copy-start(bf16[2,256,256]{2,1,0:T(8,128)(2,1)} %constant.27.clone.yf_ref) | copy-start | bytes 786436
  14.0 2.0 %copy-start.4 = (bf16[192,256]{1,0:T(8,128)(2,1)S(1)}, bf16[192,256]{1,0:T(8,128)(2,1)}, u32[]{:S(2)}) copy-start(bf16[192,256]{1,0:T(8,128)(2,1)} %constant.32.clone.xbn_ref) | copy-start | bytes 294916
  14.0 1.9 %collective-permute-start.5 = (f32[512,128]{1,0:T(8,128)S(1)}, f32[512,128]{1,0:T(8,128)S(1)}, u32[]{:S(2)}, u32[]{:S(2)}) collective-permute-start(f32[512,128]{1,0:T(8,128)S(1)} %get-tuple-element.28), channel_id=1, source_target_pairs={{1,2},{2,1},{3,4},{4,3},{5,6},{6,5},{9,10},{10,9},{11,12},{12,11},... | collective-permute-start | bytes 786440 | tf_op jit(solution)/shard_map/ppermute | solution.py:621
  14.8 5.1 %collective-permute-start.6 = (f32[192,128]{1,0:T(8,128)S(1)}, f32[192,128]{1,0:T(8,128)S(1)}, u32[]{:S(2)}, u32[]{:S(2)}) collective-permute-start(f32[192,128]{1,0:T(8,128)S(1)} %get-tuple-element.32), channel_id=1, source_target_pairs={{1,2},{2,1},{3,4},{4,3},{5,6},{6,5},{9,10},{10,9},{11,12},{12,11},... | collective-permute-start | bytes 294920 | tf_op jit(solution)/shard_map/ppermute | solution.py:620
  16.0 3.9 %copy-start.3 = (bf16[256,192]{1,0:T(8,128)(2,1)S(1)}, bf16[256,192]{1,0:T(8,128)(2,1)}, u32[]{:S(2)}) copy-start(bf16[256,192]{1,0:T(8,128)(2,1)} %constant.31.clone.xn_ref) | copy-start | bytes 294916
  16.0 3.9 %copy-start.5 = (bf16[128,256]{1,0:T(8,128)(2,1)S(1)}, bf16[128,256]{1,0:T(8,128)(2,1)}, u32[]{:S(2)}) copy-start(bf16[128,256]{1,0:T(8,128)(2,1)} %constant.33.clone.xbo_ref) | copy-start | bytes 196612
  24.2 21.1 %collective-permute-start.7 = (f32[688,128]{1,0:T(8,128)S(1)}, f32[688,128]{1,0:T(8,128)S(1)}, u32[]{:S(2)}, u32[]{:S(2)}) collective-permute-start(f32[688,128]{1,0:T(8,128)S(1)} %get-tuple-element.34), channel_id=1, source_target_pairs={{0,1},{1,0},{2,3},{3,2},{4,5},{5,4},{6,7},{7,6},{8,9},{9,8},{10,11... | collective-permute-start | bytes 1056776 | tf_op jit(solution)/shard_map/ppermute | solution.py:673

commit v4 on v3

--- a/solution.py
+++ b/solution.py
@@ -8,6 +8,7 @@
 from jax.experimental import pallas as pl
 from jax.experimental.pallas import tpu as pltpu
 from jax.sharding import PartitionSpec as P
+
 
 F32 = jnp.float32
 BF16 = jnp.bfloat16
@@ -146,61 +147,56 @@
     return jnp.where(left, minus, plus), jnp.where(left, -plus, minus)
 
 
-def send_kernel(s, e_in, v_in, both_ref, even_ref, odd_ref, sem_ref):
+def send_kernel(s, e_in, v_in, e_ref, v_ref, even_ref, odd_ref, sem_ref):
     moves = [
-        pltpu.make_async_copy(e_in, both_ref.at[:, : s.rows], sem_ref.at[0]),
-        pltpu.make_async_copy(v_in, both_ref.at[:, s.rows :], sem_ref.at[1]),
+        pltpu.make_async_copy(e_in, e_ref, sem_ref.at[0]),
+        pltpu.make_async_copy(v_in, v_ref, sem_ref.at[1]),
     ]
     for move in moves:
         move.start()
     even = lax.axis_index("gx") % 2 == 0
     for move in moves:
         move.wait()
-    place = 0
-    for z in range(s.planes):
-        for start, count in ((0, 2 * s.radius), (s.rows, s.radius)):
-            low = both_ref[z, start : start + count]
-            high = both_ref[z, start + s.rows - count : start + s.rows]
-            even_ref[place : place + count] = jnp.where(even, high, low)
-            odd_ref[place : place + count] = jnp.where(even, low, high)
-            place += count
-
-
-def pack_kernel(
-    s, where_ref, own_ref, partner_ref, even_ref, odd_ref, even2_ref, odd2_ref, k_ref, l_ref, v_ref, e_slab_ref, v_slab_ref, w_ref
-):
-    core = where_ref[1]
-    even = where_ref[2] % 2 == 0
-    wide, near = 2 * s.radius, s.radius
-    for both_ref, e_x_ref, o_x_ref, base in (
-        (own_ref, even_ref, odd_ref, core * s.planes),
-        (partner_ref, even2_ref, odd2_ref, (1 - core) * s.planes),
-    ):
+    for ref, begin, count in ((e_ref, 0, 2 * s.radius), (v_ref, s.planes * 2 * s.radius, s.radius)):
+        for z in range(s.planes):
+            low, high = ref[z, :count], ref[z, s.rows - count :]
+            part = slice(begin + z * count, begin + (z + 1) * count)
+            even_ref[part] = jnp.where(even, high, low)
+            odd_ref[part] = jnp.where(even, low, high)
+
+
+def pack(s, begin, count, pad, group, mine, partners, window_ref, slab_ref):
+    core = lax.axis_index("gz")
+    even = lax.axis_index("gx") % 2 == 0
+    rows = s.rows + 2 * pad
+    for (body_ref, even_ref, odd_ref), base in ((mine, core * s.planes), (partners, (1 - core) * s.planes)):
         for z in range(s.planes):
             here = base + z
-            first = z * (wide + near)
-            for start, count, pad, rows, out_ref, source in (
-                (first, wide, s.wide, s.length, w_ref, 0),
-                (first + wide, near, s.near, s.view_rows, v_ref, s.rows),
-            ):
-                part = slice(start, start + count)
-                out_ref[here, :8] = jnp.zeros((8, s.cols), F32)
-                out_ref[here, rows - 8 :] = jnp.zeros((8, s.cols), F32)
-                out_ref[here, pad - count : pad] = jnp.where(even, o_x_ref[part], e_x_ref[part])
-                out_ref[here, pad : pad + s.rows] = both_ref[z, source : source + s.rows]
-                out_ref[here, pad + s.rows : pad + s.rows + count] = jnp.where(even, e_x_ref[part], o_x_ref[part])
+            part = slice(begin + z * count, begin + (z + 1) * count)
+            window_ref[here, :8] = jnp.zeros((8, s.cols), F32)
+            window_ref[here, rows - 8 :] = jnp.zeros((8, s.cols), F32)
+            window_ref[here, pad - count : pad] = jnp.where(even, odd_ref[part], even_ref[part])
+            window_ref[here, pad : pad + s.rows] = body_ref[z]
+            window_ref[here, pad + s.rows : pad + s.rows + count] = jnp.where(even, even_ref[part], odd_ref[part])
+    lanes = (lane_iota(rows, s.cols) // pad + core) % group
+    for q in range(s.depth // group):
+        packed = window_ref[q * group]
+        for p in range(1, group):
+            packed = jnp.where(lanes == p, turn(window_ref[q * group + p], p * pad), packed)
+        slab_ref[q * rows : (q + 1) * rows] = packed
+
+
+def pack_estimate(s, e_ref, e2_ref, even_ref, odd_ref, even2_ref, odd2_ref, l_ref, slab_ref, w_ref):
+    pack(
+        s, 0, 2 * s.radius, s.wide, s.q_wide, (e_ref, even_ref, odd_ref), (e2_ref, even2_ref, odd2_ref), w_ref, slab_ref
+    )
     for z in range(s.depth):
         l_ref[z] = tall_split(w_ref[z])
-    for rows, group, width, slab_ref, source_ref in (
-        (s.length, s.q_wide, s.wide, e_slab_ref, w_ref),
-        (s.view_rows, s.q_near, s.near, v_slab_ref, v_ref),
-    ):
-        lanes = (lane_iota(rows, s.cols) // width + core) % group
-        for q in range(s.depth // group):
-            packed = source_ref[q * group]
-            for p in range(1, group):
-                packed = jnp.where(lanes == p, turn(source_ref[q * group + p], p * width), packed)
-            slab_ref[q * rows : (q + 1) * rows] = packed
+
+
+def pack_view(s, v_ref, v2_ref, even_ref, odd_ref, even2_ref, odd2_ref, after_ref, window_ref, slab_ref):
+    begin = s.planes * 2 * s.radius
+    pack(s, begin, s.radius, s.near, s.q_near, (v_ref, even_ref, odd_ref), (v2_ref, even2_ref, odd2_ref), window_ref, slab_ref)
 
 
 def along_x_kernel(s, l_ref, x_ref, t_ref):
@@ -220,11 +216,11 @@
 
 
 def kernel_spectrum(
-    s, where_ref, psf_in, y_in, x_in, k_ref, ks_ref, kd_ref, pad_ref, a_ref, re_ref, im_ref, psf_ref, y_ref, x_ref, sem_ref
+    s, view_ref, psf_in, y_in, x_in, re_ref, im_ref, pad_ref, a_ref, psf_ref, y_ref, x_ref, sem_ref
 ):
     taps = up8(s.extent)
     moves = [
-        pltpu.make_async_copy(psf_in.at[pl.ds(where_ref[0], 1)], psf_ref, sem_ref.at[0]),
+        pltpu.make_async_copy(psf_in.at[pl.ds(view_ref[0], 1)], psf_ref, sem_ref.at[0]),
         pltpu.make_async_copy(y_in, y_ref, sem_ref.at[1]),
         pltpu.make_async_copy(x_in, x_ref, sem_ref.at[2]),
     ]
@@ -251,6 +247,9 @@
             if 2 * pair + side < s.extent:
                 value = out[:, side * s.cols : (side + 1) * s.cols]
                 re_ref[2 * pair + side], im_ref[2 * pair + side] = spectrum_of(value[: s.length // 2], value[s.length // 2 :])
+
+
+def kernel_leaves(s, re_ref, im_ref, k_ref, ks_ref, kd_ref):
     first = s.radius - (s.depth - 1)
 
     def tile(t, carry):
@@ -291,7 +290,7 @@
 
     def forward_y():
         for z in range(0, depth, group):
-            out = fold(dot(a_ref[z : z + group].reshape(group * s.length, 2 * s.cols), yf_ref[0]))
+            out = fold(dot(a_ref[z : z + group].reshape(group * s.length, 2 * s.cols), yf_ref[lax.axis_index("gz")]))
             for k in range(group):
                 value = out[k * s.length : (k + 1) * s.length]
                 re_ref[z + k], im_ref[z + k] = spectrum_of(value[:freqs], value[freqs:])
@@ -355,7 +354,7 @@
                 turned_real, turned_imag = turn(real, half), turn(imag, half)
                 pieces.append(jnp.where(half_lanes, real + turned_real, imag - turned_imag))
                 pieces.append(jnp.where(half_lanes, imag + turned_imag, turned_real - real))
-            out = fold(dot(wide_split(jnp.concatenate(pieces, 0)), yi_ref[0]))
+            out = fold(dot(wide_split(jnp.concatenate(pieces, 0)), yi_ref[lax.axis_index("gz")]))
             for k in range(group):
                 b_ref[z + k] = tall_split(out[k * s.length : (k + 1) * s.length])
         for z in range(0, depth, 2):
@@ -367,10 +366,10 @@
 
 
 def first_kernel(
-    s, where_ref, t_in_ref, slab_ref, k_ref, ks_ref, kd_ref, yf_ref, yi_ref, xw_ref, xbn_ref, blurred_ref,
+    s, t_in_ref, slab_ref, k_ref, ks_ref, kd_ref, yf_ref, yi_ref, xw_ref, xbn_ref, blurred_ref,
     re_ref, im_ref, pr_ref, pi_ref, a_ref, b_ref,
 ):
-    core = where_ref[1]
+    core = lax.axis_index("gz")
     _, forward_y, along_z, backward = stages(
         s, k_ref, ks_ref, kd_ref, yf_ref, yi_ref, re_ref, im_ref, pr_ref, pi_ref, a_ref, b_ref
     )
@@ -393,11 +392,11 @@
 
 
 def second_kernel(
-    s, where_ref, blurred_ref, v_in_ref, own_ref, partner_ref, slab_ref, k_ref, ks_ref, kd_ref, yf_ref, yi_ref,
+    s, blurred_ref, v_in_ref, own_ref, partner_ref, slab_ref, k_ref, ks_ref, kd_ref, yf_ref, yi_ref,
     xn_ref, xbo_ref, mine_ref, theirs_ref, five_ref,
     re_ref, im_ref, pr_ref, pi_ref, u_ref, t_ref, l_ref, a_ref, b_ref,
 ):
-    core, gx, gy = where_ref[1], where_ref[2], where_ref[3]
+    core, gx, gy = lax.axis_index("gz"), lax.axis_index("gx"), lax.axis_index("gy")
     half = s.cols // 2
     depth = s.depth
     forward_x, forward_y, along_z, backward = stages(
@@ -430,7 +429,7 @@
 
     def to_update(z, correction):
         plane = z % s.planes
-        estimate = jnp.where(core == z // s.planes, own_ref[plane, : s.rows], partner_ref[plane, : s.rows])
+        estimate = jnp.where(core == z // s.planes, own_ref[plane], partner_ref[plane])
         u_ref[z] = jnp.where(owned, estimate * correction, 0.0)
 
     backward(s.rows, xbo_ref, to_update)
@@ -525,27 +524,22 @@
     return pltpu.with_memory_space_constraint(x, pltpu.HBM)
 
 
-def whole(shape):
-    return pl.BlockSpec(shape, lambda *_: (0,) * len(shape))
-
-
-def call(body, where, arrays, in_specs, outs, scratch=(), narrow=(), name=None, flops=0, mib=16, copies=()):
+def call(body, arrays, outs, scratch=(), narrow=(), copies=(), mib=16, flops=10**7, prefetch=(), where=None):
     outs = [out if isinstance(out[0], tuple) else (out, F32) for out in outs]
-    grid_spec = pltpu.PrefetchScalarGridSpec(
-        num_scalar_prefetch=1,
-        grid=(1,),
-        in_specs=in_specs,
-        out_specs=[whole(shape) for shape, _ in outs],
-        scratch_shapes=[pltpu.VMEM(shape, F32) for shape in scratch] + [pltpu.VMEM(shape, BF16) for shape in narrow] + list(copies),
-    )
     return pl.pallas_call(
         body,
-        grid_spec=grid_spec,
+        grid_spec=pltpu.PrefetchScalarGridSpec(
+            num_scalar_prefetch=len(prefetch),
+            in_specs=[pl.BlockSpec(memory_space=where or pltpu.VMEM)] * len(arrays),
+            out_specs=[pl.BlockSpec(memory_space=pltpu.VMEM)] * len(outs),
+            scratch_shapes=[pltpu.VMEM(shape, F32) for shape in scratch]
+            + [pltpu.VMEM(shape, BF16) for shape in narrow]
+            + list(copies),
+        ),
         out_shape=[jax.ShapeDtypeStruct(*out) for out in outs],
         compiler_params=pltpu.CompilerParams(vmem_limit_bytes=mib * MIB),
-        cost_estimate=pl.CostEstimate(flops=flops, bytes_accessed=0, transcendentals=0) if flops else None,
-        name=name,
-    )(where, *arrays)
+        cost_estimate=pl.CostEstimate(flops=flops, bytes_accessed=0, transcendentals=0),
+    )(*prefetch, *arrays)
 
 
 def neighbours(first):
@@ -567,65 +561,59 @@
     gx, gy = lax.axis_size("gx"), lax.axis_size("gy")
     s = Sizes(estimate.shape, psf_stack.shape, gx, gy)
     t = {key: jnp.asarray(value) for key, value in tables(s).items()}
-    where = jnp.stack(
-        [view_index[0], lax.axis_index("gz"), lax.axis_index("gx"), lax.axis_index("gy")]
-    ).astype(jnp.int32)
-
-    both_shape = (s.planes, 2 * s.rows, s.cols)
+    across = [(0, 1), (1, 0)]
     strip = (s.planes * 3 * s.radius, s.cols)
-    outs = [both_shape, strip, strip]
-    own, to_even, to_odd = pl.pallas_call(
+    own, own_view, even, odd = call(
         functools.partial(send_kernel, s),
-        in_specs=[pl.BlockSpec(memory_space=pltpu.HBM)] * 2,
-        out_specs=[pl.BlockSpec(memory_space=pltpu.VMEM)] * len(outs),
-        out_shape=[jax.ShapeDtypeStruct(shape, F32) for shape in outs],
-        scratch_shapes=[pltpu.SemaphoreType.DMA((2,))],
-        compiler_params=pltpu.CompilerParams(vmem_limit_bytes=8 * MIB),
-        name="send",
-    )(in_hbm(estimate), in_hbm(view_data))
-    across = [(0, 1), (1, 0)]
+        (in_hbm(estimate), in_hbm(view_data)),
+        [estimate.shape, estimate.shape, strip, strip],
+        copies=[pltpu.SemaphoreType.DMA((2,))],
+        mib=8,
+        where=pltpu.HBM,
+    )
+    even = lax.ppermute(even, "gx", neighbours(0))
+    odd = lax.ppermute(odd, "gx", neighbours(1))
     partner = lax.ppermute(own, "gz", across)
-    even = lax.ppermute(to_even, "gx", neighbours(0))
-    odd = lax.ppermute(to_odd, "gx", neighbours(1))
+    partner_view = lax.ppermute(own_view, "gz", across)
+
+    taps = up8(s.extent)
     psf_shape = (1,) + psf_stack.shape[1:]
-    taps = up8(s.extent)
-    k, ks, kd = call(
+    kernel_planes = (s.extent, s.length // 2, s.cols)
+    re, im = call(
         functools.partial(kernel_spectrum, s),
-        where,
         (in_hbm(psf_stack), in_hbm(t["y_kernel"]), in_hbm(t["x_kernel"])),
-        [pl.BlockSpec(memory_space=pltpu.HBM)] * 3,
-        [(9 * (s.depth // 2 - 1), s.length // 2, s.cols)] * 3,
-        scratch=[((s.extent + 1) // 2 * 2 * taps, s.cols)] * 2 + [(s.extent, s.length // 2, s.cols)] * 2 + [psf_shape],
+        [kernel_planes] * 2,
+        scratch=[((s.extent + 1) // 2 * 2 * taps, s.cols)] * 2 + [psf_shape],
         narrow=[t["y_kernel"].shape, t["x_kernel"].shape],
         copies=[pltpu.SemaphoreType.DMA((3,))],
-        name="kernel_spectrum",
-        flops=10**8,
-    )
-    even, _ = lax.optimization_barrier((even, k))
-    even_partner = lax.ppermute(even, "gz", across)
-    odd, _ = lax.optimization_barrier((odd, even_partner))
-    odd_partner = lax.ppermute(odd, "gz", across)
-    arrays = (own, partner, even, odd, even_partner, odd_partner)
+        prefetch=(view_index,),
+        where=pltpu.HBM,
+    )
+    k, ks, kd = call(
+        functools.partial(kernel_leaves, s), (re, im), [(9 * (s.depth // 2 - 1), s.length // 2, s.cols)] * 3
+    )
+
+    even, _ = lax.optimization_barrier((even, re))
+    even2 = lax.ppermute(even, "gz", across)
+    odd, _ = lax.optimization_barrier((odd, (even2, k)))
+    odd2 = lax.ppermute(odd, "gz", across)
     window = (s.depth, s.length, s.cols)
     view_window = (s.depth, s.view_rows, s.cols)
-    split_window, view_here, slab, view_slab = call(
-        functools.partial(pack_kernel, s),
-        where,
-        arrays + (k,),
-        [whole(a.shape) for a in arrays] + [pl.BlockSpec(memory_space=pl.ANY)],
-        [((s.depth, 2 * s.length, s.cols), BF16), view_window, (s.pack_e, s.cols), (s.pack_v, s.cols)],
+    split_window, slab = call(
+        functools.partial(pack_estimate, s),
+        (own, partner, even, odd, even2, odd2),
+        [((s.depth, 2 * s.length, s.cols), BF16), (s.pack_e, s.cols)],
         scratch=[window],
-        name="pack",
+    )
+    slab_here = slab
+    slab = lax.ppermute(slab, ("gy", "gz"), to_side())
+    view_here, view_slab = call(
+        functools.partial(pack_view, s),
+        (own_view, partner_view, even, odd, even2, odd2, slab_here),
+        [view_window, (s.pack_v, s.cols)],
     )
     view_slab = lax.ppermute(view_slab, ("gy", "gz"), to_side())
-    slab = lax.ppermute(slab, ("gy", "gz"), to_side())
-    along_x = pl.pallas_call(
-        functools.partial(along_x_kernel, s),
-        out_shape=jax.ShapeDtypeStruct(window, F32),
-        compiler_params=pltpu.CompilerParams(vmem_limit_bytes=16 * MIB),
-        cost_estimate=pl.CostEstimate(flops=10**8, bytes_accessed=0, transcendentals=0),
-        name="along_x",
-    )(split_window, t["x_window"])
+    (along_x,) = call(functools.partial(along_x_kernel, s), (split_window, t["x_window"]), [window])
 
     u_rows = s.planes * s.rows
     out_rows = u_rows
@@ -639,51 +627,33 @@
     five_shape = (rows // 2 * gx, columns // 2 * gy)
     spectra = [(s.depth, s.length // 2, s.cols)] * 4
     halves = [(s.depth, s.length, 2 * s.cols), (s.depth, 2 * s.length, s.cols)]
-
-    def of_core(x):
-        return pl.BlockSpec((1,) + x.shape[1:], lambda i, w: (w[1], 0, 0))
-
-    tables_of = (k, ks, kd, t["y_forward"], t["y_inverse"])
-    tables_specs = [whole(a.shape) for a in tables_of[:3]] + [of_core(a) for a in tables_of[3:]]
-    before, after = (along_x, slab), (t["x_window"], t["x_back_near"])
+    shared = (k, ks, kd, t["y_forward"], t["y_inverse"])
     (blurred,) = call(
         functools.partial(first_kernel, s),
-        where,
-        before + tables_of + after,
-        [whole(a.shape) for a in before] + tables_specs + [whole(a.shape) for a in after],
+        (along_x, slab) + shared + (t["x_window"], t["x_back_near"]),
         [view_window],
         scratch=spectra,
         narrow=halves,
-        name="blur",
         mib=24,
         flops=10**8,
     )
-    before, after = (blurred, view_here, own, partner, view_slab), (t["x_near"], t["x_back_own"])
     mine, theirs, five = call(
         functools.partial(second_kernel, s),
-        where,
-        before + tables_of + after,
-        [whole(a.shape) for a in before] + tables_specs + [whole(a.shape) for a in after],
+        (blurred, view_here, own, partner, view_slab) + shared + (t["x_near"], t["x_back_own"]),
         [(out_rows, s.cols), (out_rows, s.cols), (devices, 1, five_shape[0] * five_shape[1])],
         scratch=spectra + [(s.depth, s.rows, s.cols), (4, s.depth // 2, s.rows, s.cols)],
         narrow=[(s.depth, 2 * s.view_rows, s.cols)] + halves,
-        name="update",
         mib=24,
     )
-    got = lax.ppermute(theirs, "gz", [(0, 1), (1, 0)])
+    got = lax.ppermute(theirs, "gz", across)
     fives = lax.all_to_all(five, ALL, split_axis=0, concat_axis=0, tiled=True)
-    outs = [estimate.shape] + level_shapes + [(1,) + five_shape]
-    arrays = (mine, got, fives)
     return tuple(
-        pl.pallas_call(
+        call(
             functools.partial(last_kernel, s),
-            in_specs=[whole(a.shape) for a in arrays],
-            out_specs=[whole(shape) for shape in outs],
-            out_shape=[jax.ShapeDtypeStruct(shape, F32) for shape in outs],
-            grid=(1,),
-            compiler_params=pltpu.CompilerParams(vmem_limit_bytes=8 * MIB),
-            name="assemble",
-        )(*arrays)
+            (mine, got, fives),
+            [estimate.shape] + level_shapes + [(1,) + five_shape],
+            mib=8,
+        )
     )
 
 

time: 46.3 us -> 44.5 us (0.961)
  Pallas kernels: 15.2 us -> 13.4 us
    pallas_call x7 -> x9, Pallas kernels: 15.2 us -> 13.4 us  [call(): pl.pallas_call(body, grid_spec=pltpu.PrefetchScalarGridSpec(num_scalar_pr...]
    ppermute x5 -> x6, starting transfers between devices: 10.9 us -> 10.1 us  [the longest x1 5.79 us: local(): got = lax.ppermute(theirs, 'gz', across)]
    ppermute x1, starting transfers between devices: 0.01 us -> 0.51 us  [local(): partner = lax.ppermute(own, 'gz', across)]
    ppermute x5 -> x6, waiting for transfers between devices: 2.11 us -> 2.03 us  [the longest x1 1.11 us: local(): even = lax.ppermute(even, 'gx', neighbours(0))]
  transfers between devices with their start and end apart: 8 -> 9, of which waited for: 2 -> 2; matrix products, arithmetic and copies ran while one was open for 0% -> 0% of each run, Pallas kernels for 17% -> 18%
where the time goes in v4:
time: 44.5 us; the launch traced here: 44.3 us
  blocking collectives  15.2 us (34%)
  Pallas kernels  13.4 us (30%)
  starting transfers between devices  12 us (27%)
  waiting for transfers between devices  2.04 us (5%)
  between operations  1.5 us (3%)
    all_to_all x1, blocking collectives, local(): fives = lax.all_to_all(five, ALL, split_axis=0, concat_axis=0, tiled=True)  15.2 us
    pallas_call x9, Pallas kernels, call(): pl.pallas_call(body, grid_spec=pltpu.PrefetchScalarGridSpec(num_scalar_pr...  13.4 us
    ppermute x1, starting transfers between devices, local(): got = lax.ppermute(theirs, 'gz', across)  5.79 us
    ppermute x1, starting transfers between devices, local(): even = lax.ppermute(even, 'gx', neighbours(0))  3.03 us
    ppermute x1, waiting for transfers between devices, local(): even = lax.ppermute(even, 'gx', neighbours(0))  1.11 us
    ppermute x1, waiting for transfers between devices, local(): odd2 = lax.ppermute(odd, 'gz', across)  0.91 us
  transfers between devices with their start and end apart: 9, of which 2 were waited for; matrix products, arithmetic and copies ran while one was open for 0% of the time, Pallas kernels for 18%

profile of v4, /device:TPU:0, one launch (start us, length us, event | category | flops | bytes accessed | tf_op | source)
XLA Modules:
  0.0 44.3 jit_solution(12741499616227484228)
XLA Ops:
  0.6 1.1 %shard_map.163 = (f32[8,64,128]{2,1,0:T(8,128)S(1)}, f32[8,64,128]{2,1,0:T(8,128)S(1)}, f32[360,128]{1,0:T(8,128)S(1)}, f32[360,128]{1,0:T(8,128)S(1)}) custom-call(f32[8,64,128]{2,1,0:T(8,128)} %e_in.1, f32[8,64,128]{2,1,0:T(8,128)} %v_in.1), custom_call_target="tpu_custom_call" | custom-call | flops 10000000 | tf_op jit(solution)/shard_map/pallas_call | solution.py:529
  1.7 3.0 %collective-permute-start.1 = (f32[360,128]{1,0:T(8,128)S(1)}, f32[360,128]{1,0:T(8,128)S(1)}, u32[]{:S(2)}, u32[]{:S(2)}) collective-permute-start(f32[360,128]{1,0:T(8,128)S(1)} %get-tuple-element.25), channel_id=1, source_target_pairs={{0,8},{8,0},{16,24},{24,16},{1,9},{9,1},{17,25},{25,17},{2,10},{10... | collective-permute-start | bytes 552968 | tf_op jit(solution)/shard_map/ppermute | solution.py:574
  4.7 0.7 %collective-permute-start.2 = (f32[360,128]{1,0:T(8,128)S(1)}, f32[360,128]{1,0:T(8,128)S(1)}, u32[]{:S(2)}, u32[]{:S(2)}) collective-permute-start(f32[360,128]{1,0:T(8,128)S(1)} %get-tuple-element.28), channel_id=1, source_target_pairs={{8,16},{16,8},{9,17},{17,9},{10,18},{18,10},{11,19},{19,11},{12,20... | collective-permute-start | bytes 552968 | tf_op jit(solution)/shard_map/ppermute | solution.py:575
  6.1 2.2 %shard_map.164 = (f32[31,64,128]{2,1,0:T(8,128)S(1)}, f32[31,64,128]{2,1,0:T(8,128)S(1)}) custom-call(s32[1]{0:T(128)S(6)} %copy.18.view_ref, f32[6,31,31,31]{3,2,1,0:T(8,128)} %psf_in.1, bf16[256,256]{1,0:T(8,128)(2,1)} %constant.18.clone.y_in, bf16[128,96]{1,0:T(8,128)(2,1)} %constant.23.clone.x_in), custom_call_target="tpu_custom_call" | custom-call | flops 10000000 | tf_op jit(solution)/shard_map/pallas_call | solution.py:529
  8.3 1.1 %collective-permute-done.1.even_ref = f32[360,128]{1,0:T(8,128)S(1)} collective-permute-done((f32[360,128]{1,0:T(8,128)S(1)}, f32[360,128]{1,0:T(8,128)S(1)}, u32[]{:S(2)}, u32[]{:S(2)}) %collective-permute-start.1) | collective-permute-done | bytes 184352 | tf_op jit(solution)/shard_map/ppermute | solution.py:574
  9.4 0.5 %collective-permute-start = (f32[8,64,128]{2,1,0:T(8,128)S(1)}, f32[8,64,128]{2,1,0:T(8,128)S(1)}, u32[]{:S(2)}, u32[]{:S(2)}) collective-permute-start(f32[8,64,128]{2,1,0:T(8,128)S(1)} %get-tuple-element.24.e_ref.own_ref), channel_id=1, source_target_pairs={{0,1},{1,0},{2,3},{3,2},{4,5},{5,4},{6,7},{7,6},{8,9},{9,8},{10,11... | collective-permute-start | bytes 786440 | tf_op jit(solution)/shard_map/ppermute | solution.py:576
  9.9 1.1 %shard_map.165 = (f32[63,64,128]{2,1,0:T(8,128)S(1)}, f32[63,64,128]{2,1,0:T(8,128)S(1)}, f32[63,64,128]{2,1,0:T(8,128)S(1)}) custom-call(f32[31,64,128]{2,1,0:T(8,128)S(1)} %get-tuple-element.26.re_ref, f32[31,64,128]{2,1,0:T(8,128)S(1)} %get-tuple-element.29.im_ref), custom_call_target="tpu_custom_call" | custom-call | flops 10000000 | tf_op jit(solution)/shard_map/pallas_call | solution.py:529
  11.0 0.1 collective-permute-start.4
  11.1 0.5 %collective-permute-start.6 = (f32[8,64,128]{2,1,0:T(8,128)S(1)}, f32[8,64,128]{2,1,0:T(8,128)S(1)}, u32[]{:S(2)}, u32[]{:S(2)}) collective-permute-start(f32[8,64,128]{2,1,0:T(8,128)S(1)} %get-tuple-element.36.v_ref), channel_id=1, source_target_pairs={{0,1},{1,0},{2,3},{3,2},{4,5},{5,4},{6,7},{7,6},{8,9},{9,8},{10,11... | collective-permute-start | bytes 786440 | tf_op jit(solution)/shard_map/ppermute | solution.py:577
  11.6 0.9 %collective-permute-done.4.odd2_ref = f32[360,128]{1,0:T(8,128)S(1)} collective-permute-done((f32[360,128]{1,0:T(8,128)S(1)}, f32[360,128]{1,0:T(8,128)S(1)}, u32[]{:S(2)}, u32[]{:S(2)}) %collective-permute-start.4) | collective-permute-done | bytes 184352 | tf_op jit(solution)/shard_map/ppermute | solution.py:599
  12.5 0.5 %shard_map.166 = (bf16[16,256,128]{2,1,0:T(8,128)(2,1)S(1)}, f32[512,128]{1,0:T(8,128)S(1)}) custom-call(f32[8,64,128]{2,1,0:T(8,128)S(1)} %get-tuple-element.24.e_ref.own_ref, f32[8,64,128]{2,1,0:T(8,128)S(1)} %collective-permute-done.e2_ref.partner_ref, f32[360,128]{1,0:T(8,128)S(1)} %collective-permute-done.1.even_ref, ...), custom_call_target="tpu_custom_call" | custom-call | flops 10000000 | tf_op jit(solution)/shard_map/pallas_call | solution.py:529
  13.0 0.0 copy-start
  13.0 0.0 copy-start.1
  13.0 0.0 copy-start.4
  13.0 0.8 %collective-permute-start.5 = (f32[512,128]{1,0:T(8,128)S(1)}, f32[512,128]{1,0:T(8,128)S(1)}, u32[]{:S(2)}, u32[]{:S(2)}) collective-permute-start(f32[512,128]{1,0:T(8,128)S(1)} %get-tuple-element.33.after_ref), channel_id=1, source_target_pairs={{1,2},{2,1},{3,4},{4,3},{5,6},{6,5},{9,10},{10,9},{11,12},{12,11},... | collective-permute-start | bytes 786440 | tf_op jit(solution)/shard_map/ppermute | solution.py:609
  13.8 0.3 shard_map.169
  14.2 0.7 %collective-permute-start.7 = (f32[192,128]{1,0:T(8,128)S(1)}, f32[192,128]{1,0:T(8,128)S(1)}, u32[]{:S(2)}, u32[]{:S(2)}) collective-permute-start(f32[192,128]{1,0:T(8,128)S(1)} %get-tuple-element.38), channel_id=1, source_target_pairs={{1,2},{2,1},{3,4},{4,3},{5,6},{6,5},{9,10},{10,9},{11,12},{12,11},... | collective-permute-start | bytes 294920 | tf_op jit(solution)/shard_map/ppermute | solution.py:615
  14.8 0.4 shard_map.167.t_in_ref
  15.3 0.0 copy-start.3
  15.4 3.3 %shard_map.168.blurred_ref = f32[16,96,128]{2,1,0:T(8,128)S(1)} custom-call(f32[16,128,128]{2,1,0:T(8,128)S(1)} %shard_map.167.t_in_ref, f32[512,128]{1,0:T(8,128)S(1)} %collective-permute-done.5.slab_ref, f32[63,64,128]{2,1,0:T(8,128)S(1)} %get-tuple-element.30.k_ref, f32[63,64,128]{2,1,0:T(8,128)S(1)} %get-tuple-element.34.ks_ref, ...), custom_call_target="tpu_custom_call" | custom-call | flops 100000000 | tf_op jit(solution)/shard_map/pallas_call | solution.py:529
  18.7 3.7 %shard_map.170 = (f32[688,128]{1,0:T(8,128)S(1)}, f32[688,128]{1,0:T(8,128)S(1)}, f32[32,1,128]{2,1,0:T(1,128)S(1)}) custom-call(f32[16,96,128]{2,1,0:T(8,128)S(1)} %shard_map.168.blurred_ref, f32[16,96,128]{2,1,0:T(8,128)S(1)} %get-tuple-element.37.v_in_ref, f32[8,64,128]{2,1,0:T(8,128)S(1)} %get-tuple-element.24.e_ref.own_ref, ...), custom_call_target="tpu_custom_call" | custom-call | flops 10000000 | tf_op jit(solution)/shard_map/pallas_call | solution.py:529
  22.5 5.8 %collective-permute-start.8 = (f32[688,128]{1,0:T(8,128)S(1)}, f32[688,128]{1,0:T(8,128)S(1)}, u32[]{:S(2)}, u32[]{:S(2)}) collective-permute-start(f32[688,128]{1,0:T(8,128)S(1)} %get-tuple-element.40), channel_id=1, source_target_pairs={{0,1},{1,0},{2,3},{3,2},{4,5},{5,4},{6,7},{7,6},{8,9},{9,8},{10,11... | collective-permute-start | bytes 1056776 | tf_op jit(solution)/shard_map/ppermute | solution.py:648
  28.2 15.2 %all_to_all.5.fives_ref = f32[32,1,128]{2,1,0:T(1,128)S(1)} all-to-all(f32[32,1,128]{2,1,0:T(1,128)S(1)} %get-tuple-element.41), channel_id=1, replica_groups=mesh['gx'=4,'gy'=4,'gz'=2] {'gx','gy','gz'}, dimensions={0} | all-to-all | bytes 32768 | tf_op jit(solution)/shard_map/all_to_all | solution.py:649
  43.5 0.8 %shard_map.171 = (f32[8,64,128]{2,1,0:T(8,128)}, f32[4,32,64]{2,1,0:T(8,128)}, f32[2,16,32]{2,1,0:T(8,128)}, f32[1,8,16]{2,1,0:T(8,128)}, f32[1,4,8]{2,1,0:T(4,128)}, /*index=5*/f32[1,8,16]{2,1,0:T(8,128)}) custom-call(f32[688,128]{1,0:T(8,128)S(1)} %get-tuple-element.39.mine_ref, f32[688,128]{1,0:T(8,128)S(1)} %collective-permute-done.8.got_ref, ...), custom_call_target="tpu_custom_call" | custom-call | flops 10000000 | tf_op jit(solution)/shard_map/pallas_call | solution.py:529
  (16 shorter events, 0.0 us)
Async XLA Ops:
  1.7 7.7 %collective-permute-start.1 = (f32[360,128]{1,0:T(8,128)S(1)}, f32[360,128]{1,0:T(8,128)S(1)}, u32[]{:S(2)}, u32[]{:S(2)}) collective-permute-start(f32[360,128]{1,0:T(8,128)S(1)} %get-tuple-element.25), channel_id=1, source_target_pairs={{0,8},{8,0},{16,24},{24,16},{1,9},{9,1},{17,25},{25,17},{2,10},{10... | collective-permute-start | bytes 552968 | tf_op jit(solution)/shard_map/ppermute | solution.py:574
  4.7 6.2 %collective-permute-start.2 = (f32[360,128]{1,0:T(8,128)S(1)}, f32[360,128]{1,0:T(8,128)S(1)}, u32[]{:S(2)}, u32[]{:S(2)}) collective-permute-start(f32[360,128]{1,0:T(8,128)S(1)} %get-tuple-element.28), channel_id=1, source_target_pairs={{8,16},{16,8},{9,17},{17,9},{10,18},{18,10},{11,19},{19,11},{12,20... | collective-permute-start | bytes 552968 | tf_op jit(solution)/shard_map/ppermute | solution.py:575
  9.4 1.6 %collective-permute-start.3 = (f32[360,128]{1,0:T(8,128)S(1)}, f32[360,128]{1,0:T(8,128)S(1)}, u32[]{:S(2)}, u32[]{:S(2)}) collective-permute-start(f32[360,128]{1,0:T(8,128)S(1)} %collective-permute-done.1.even_ref), channel_id=1, source_target_pairs={{0,1},{1,0},{2,3},{3,2},{4,5},{5,4},{6,7},{7,6},{8,9},{9,8},{10,11... | collective-permute-start | bytes 552968 | tf_op jit(solution)/shard_map/ppermute | solution.py:597
  9.4 2.2 %collective-permute-start = (f32[8,64,128]{2,1,0:T(8,128)S(1)}, f32[8,64,128]{2,1,0:T(8,128)S(1)}, u32[]{:S(2)}, u32[]{:S(2)}) collective-permute-start(f32[8,64,128]{2,1,0:T(8,128)S(1)} %get-tuple-element.24.e_ref.own_ref), channel_id=1, source_target_pairs={{0,1},{1,0},{2,3},{3,2},{4,5},{5,4},{6,7},{7,6},{8,9},{9,8},{10,11... | collective-permute-start | bytes 786440 | tf_op jit(solution)/shard_map/ppermute | solution.py:576
  9.9 4.9 %copy-start.2 = (bf16[256,256]{1,0:T(8,128)(2,1)S(1)}, bf16[256,256]{1,0:T(8,128)(2,1)}, u32[]{:S(2)}) copy-start(bf16[256,256]{1,0:T(8,128)(2,1)} %constant.19.clone.x_ref.xw_ref) | copy-start | bytes 393220
  11.0 1.5 %collective-permute-start.4 = (f32[360,128]{1,0:T(8,128)S(1)}, f32[360,128]{1,0:T(8,128)S(1)}, u32[]{:S(2)}, u32[]{:S(2)}) collective-permute-start(f32[360,128]{1,0:T(8,128)S(1)} %collective-permute-done.2.odd_ref), channel_id=1, source_target_pairs={{0,1},{1,0},{2,3},{3,2},{4,5},{5,4},{6,7},{7,6},{8,9},{9,8},{10,11... | collective-permute-start | bytes 552968 | tf_op jit(solution)/shard_map/ppermute | solution.py:599
  11.1 2.8 %collective-permute-start.6 = (f32[8,64,128]{2,1,0:T(8,128)S(1)}, f32[8,64,128]{2,1,0:T(8,128)S(1)}, u32[]{:S(2)}, u32[]{:S(2)}) collective-permute-start(f32[8,64,128]{2,1,0:T(8,128)S(1)} %get-tuple-element.36.v_ref), channel_id=1, source_target_pairs={{0,1},{1,0},{2,3},{3,2},{4,5},{5,4},{6,7},{7,6},{8,9},{9,8},{10,11... | collective-permute-start | bytes 786440 | tf_op jit(solution)/shard_map/ppermute | solution.py:577
  13.0 2.3 %copy-start = (bf16[2,256,256]{2,1,0:T(8,128)(2,1)S(1)}, bf16[2,256,256]{2,1,0:T(8,128)(2,1)}, u32[]{:S(2)}) copy-start(bf16[2,256,256]{2,1,0:T(8,128)(2,1)} %constant.16.clone.yf_ref) | copy-start | bytes 786436
  13.0 2.3 %copy-start.1 = (bf16[2,256,256]{2,1,0:T(8,128)(2,1)S(1)}, bf16[2,256,256]{2,1,0:T(8,128)(2,1)}, u32[]{:S(2)}) copy-start(bf16[2,256,256]{2,1,0:T(8,128)(2,1)} %constant.17.clone.yi_ref) | copy-start | bytes 786436
  13.0 2.3 %copy-start.4 = (bf16[192,256]{1,0:T(8,128)(2,1)S(1)}, bf16[192,256]{1,0:T(8,128)(2,1)}, u32[]{:S(2)}) copy-start(bf16[192,256]{1,0:T(8,128)(2,1)} %constant.21.clone.xbn_ref) | copy-start | bytes 294916
  13.0 2.3 %collective-permute-start.5 = (f32[512,128]{1,0:T(8,128)S(1)}, f32[512,128]{1,0:T(8,128)S(1)}, u32[]{:S(2)}, u32[]{:S(2)}) collective-permute-start(f32[512,128]{1,0:T(8,128)S(1)} %get-tuple-element.33.after_ref), channel_id=1, source_target_pairs={{1,2},{2,1},{3,4},{4,3},{5,6},{6,5},{9,10},{10,9},{11,12},{12,11},... | collective-permute-start | bytes 786440 | tf_op jit(solution)/shard_map/ppermute | solution.py:609
  14.2 4.5 %collective-permute-start.7 = (f32[192,128]{1,0:T(8,128)S(1)}, f32[192,128]{1,0:T(8,128)S(1)}, u32[]{:S(2)}, u32[]{:S(2)}) collective-permute-start(f32[192,128]{1,0:T(8,128)S(1)} %get-tuple-element.38), channel_id=1, source_target_pairs={{1,2},{2,1},{3,4},{4,3},{5,6},{6,5},{9,10},{10,9},{11,12},{12,11},... | collective-permute-start | bytes 294920 | tf_op jit(solution)/shard_map/ppermute | solution.py:615
  15.3 3.4 %copy-start.3 = (bf16[256,192]{1,0:T(8,128)(2,1)S(1)}, bf16[256,192]{1,0:T(8,128)(2,1)}, u32[]{:S(2)}) copy-start(bf16[256,192]{1,0:T(8,128)(2,1)} %constant.20.clone.xn_ref) | copy-start | bytes 294916
  15.3 3.4 %copy-start.5 = (bf16[128,256]{1,0:T(8,128)(2,1)S(1)}, bf16[128,256]{1,0:T(8,128)(2,1)}, u32[]{:S(2)}) copy-start(bf16[128,256]{1,0:T(8,128)(2,1)} %constant.22.clone.xbo_ref) | copy-start | bytes 196612
  22.5 21.0 %collective-permute-start.8 = (f32[688,128]{1,0:T(8,128)S(1)}, f32[688,128]{1,0:T(8,128)S(1)}, u32[]{:S(2)}, u32[]{:S(2)}) collective-permute-start(f32[688,128]{1,0:T(8,128)S(1)} %get-tuple-element.40), channel_id=1, source_target_pairs={{0,1},{1,0},{2,3},{3,2},{4,5},{5,4},{6,7},{7,6},{8,9},{9,8},{10,11... | collective-permute-start | bytes 1056776 | tf_op jit(solution)/shard_map/ppermute | solution.py:648

commit v5 on v4

--- a/solution.py
+++ b/solution.py
@@ -34,8 +34,6 @@
         self.freqs = self.cols // 2
         self.q_wide = self.cols // self.wide
         self.q_near = self.cols // self.near
-        self.pack_e = self.depth // self.q_wide * self.length
-        self.pack_v = self.depth // self.q_near * self.view_rows
         self.gx, self.gy = gx, gy
         assert self.half + 2 * self.wide == self.cols == 128
         assert self.wide <= self.rows and self.depth % self.q_near == 0
@@ -165,45 +163,69 @@
             odd_ref[part] = jnp.where(even, low, high)
 
 
-def pack(s, begin, count, pad, group, mine, partners, window_ref, slab_ref):
+def side_by_side(planes, group, width):
+    lanes = (lane_iota(*planes[0].shape) // width + lax.axis_index("gz")) % group
+    packed = planes[0]
+    for p in range(1, group):
+        packed = jnp.where(lanes == p, turn(planes[p], p * width), packed)
+    return packed
+
+
+def of_plane(s, z, mine_ref, partner_ref):
+    plane = z % s.planes
+    return jnp.where(lax.axis_index("gz") == z // s.planes, mine_ref[plane], partner_ref[plane])
+
+
+def pack_own(s, e_ref, e2_ref, v_ref, v2_ref, after_ref, slab_ref):
+    place = 0
+    for mine, partner, group, width in ((e_ref, e2_ref, s.q_wide, s.wide), (v_ref, v2_ref, s.q_near, s.near)):
+        for q in range(0, s.depth, group):
+            planes = [of_plane(s, z, mine, partner) for z in range(q, q + group)]
+            slab_ref[place : place + s.rows] = side_by_side(planes, group, width)
+            place += s.rows
+
+
+def pack_halo(s, even_ref, odd_ref, even2_ref, odd2_ref, e_ref, v_ref, slab_ref):
     core = lax.axis_index("gz")
     even = lax.axis_index("gx") % 2 == 0
-    rows = s.rows + 2 * pad
-    for (body_ref, even_ref, odd_ref), base in ((mine, core * s.planes), (partners, (1 - core) * s.planes)):
-        for z in range(s.planes):
-            here = base + z
-            part = slice(begin + z * count, begin + (z + 1) * count)
-            window_ref[here, :8] = jnp.zeros((8, s.cols), F32)
-            window_ref[here, rows - 8 :] = jnp.zeros((8, s.cols), F32)
-            window_ref[here, pad - count : pad] = jnp.where(even, odd_ref[part], even_ref[part])
-            window_ref[here, pad : pad + s.rows] = body_ref[z]
-            window_ref[here, pad + s.rows : pad + s.rows + count] = jnp.where(even, even_ref[part], odd_ref[part])
-    lanes = (lane_iota(rows, s.cols) // pad + core) % group
-    for q in range(s.depth // group):
-        packed = window_ref[q * group]
-        for p in range(1, group):
-            packed = jnp.where(lanes == p, turn(window_ref[q * group + p], p * pad), packed)
-        slab_ref[q * rows : (q + 1) * rows] = packed
-
-
-def pack_estimate(s, e_ref, e2_ref, even_ref, odd_ref, even2_ref, odd2_ref, l_ref, slab_ref, w_ref):
-    pack(
-        s, 0, 2 * s.radius, s.wide, s.q_wide, (e_ref, even_ref, odd_ref), (e2_ref, even2_ref, odd2_ref), w_ref, slab_ref
-    )
-    for z in range(s.depth):
-        l_ref[z] = tall_split(w_ref[z])
-
-
-def pack_view(s, v_ref, v2_ref, even_ref, odd_ref, even2_ref, odd2_ref, after_ref, window_ref, slab_ref):
-    begin = s.planes * 2 * s.radius
-    pack(s, begin, s.radius, s.near, s.q_near, (v_ref, even_ref, odd_ref), (v2_ref, even2_ref, odd2_ref), window_ref, slab_ref)
-
-
-def along_x_kernel(s, l_ref, x_ref, t_ref):
+    begin = place = 0
+    for out_ref, count, pad, group in (
+        (e_ref, 2 * s.radius, s.wide, s.q_wide),
+        (v_ref, s.radius, s.near, s.q_near),
+    ):
+        for e_x_ref, o_x_ref, base in (
+            (even_ref, odd_ref, core * s.planes),
+            (even2_ref, odd2_ref, (1 - core) * s.planes),
+        ):
+            for z in range(s.planes):
+                here = base + z
+                part = slice(begin + z * count, begin + (z + 1) * count)
+                out_ref[here, :8] = jnp.zeros((8, s.cols), F32)
+                out_ref[here, 2 * pad - 8 :] = jnp.zeros((8, s.cols), F32)
+                out_ref[here, pad - count : pad] = jnp.where(even, o_x_ref[part], e_x_ref[part])
+                out_ref[here, pad : pad + count] = jnp.where(even, e_x_ref[part], o_x_ref[part])
+        for q in range(0, s.depth, group):
+            slab_ref[place : place + 2 * pad] = side_by_side([out_ref[z] for z in range(q, q + group)], group, pad)
+            place += 2 * pad
+        begin += s.planes * count
+
+
+def framed(frame, body):
+    pad = frame.shape[0] // 2
+    return jnp.concatenate([frame[:pad], body, frame[pad:]], 0)
+
+
+def along_x_kernel(s, e_ref, e2_ref, halo_ref, x_ref, t_ref):
     for z in range(0, s.depth, 2):
-        out = fold_rows(dot(x_ref[...], jnp.concatenate([l_ref[z], l_ref[z + 1]], 1)))
+        both = [tall_split(framed(halo_ref[z + side], of_plane(s, z + side, e_ref, e2_ref))) for side in (0, 1)]
+        out = fold_rows(dot(x_ref[...], jnp.concatenate(both, 1)))
         for side in (0, 1):
             t_ref[z + side] = out[:, side * s.cols : (side + 1) * s.cols]
+
+
+def side_slab(s, q, own_ref, halo_ref, pad, own_begin, halo_begin):
+    own, halo = own_begin + q * s.rows, halo_begin + q * 2 * pad
+    return framed(halo_ref[halo : halo + 2 * pad], own_ref[own : own + s.rows])
 
 
 def toeplitz_parts(taps):
@@ -249,7 +271,7 @@
                 re_ref[2 * pair + side], im_ref[2 * pair + side] = spectrum_of(value[: s.length // 2], value[s.length // 2 :])
 
 
-def kernel_leaves(s, re_ref, im_ref, k_ref, ks_ref, kd_ref):
+def kernel_leaves(s, re_ref, im_ref, after_ref, k_ref, ks_ref, kd_ref):
     first = s.radius - (s.depth - 1)
 
     def tile(t, carry):
@@ -343,7 +365,7 @@
                         pi_ref[order(start + i), rows] = kept[1][i] + value[1][i]
             return carry
 
-        lax.fori_loop(0, freqs // 8, tile, 0)
+        lax.fori_loop(0, freqs // 8, tile, 0, unroll=2)
 
     def backward(rows, x_table, use):
         half_lanes = lane_iota(freqs, s.cols) < half
@@ -366,7 +388,7 @@
 
 
 def first_kernel(
-    s, t_in_ref, slab_ref, k_ref, ks_ref, kd_ref, yf_ref, yi_ref, xw_ref, xbn_ref, blurred_ref,
+    s, t_in_ref, own_slab_ref, halo_slab_ref, k_ref, ks_ref, kd_ref, yf_ref, yi_ref, xw_ref, xbn_ref, blurred_ref,
     re_ref, im_ref, pr_ref, pi_ref, a_ref, b_ref,
 ):
     core = lax.axis_index("gz")
@@ -375,7 +397,7 @@
     )
     arrived = from_side(core, s.length, s.cols, s.wide)
     for q in range(0, s.depth // s.q_wide, 2):
-        both = jnp.concatenate([slab_ref[(q + k) * s.length : (q + k + 1) * s.length] for k in (0, 1)], 1)
+        both = jnp.concatenate([side_slab(s, q + k, own_slab_ref, halo_slab_ref, s.wide, 0, 0) for k in (0, 1)], 1)
         out = fold_rows(dot(xw_ref[...], tall_split(both)))
         for k in (0, 1):
             side = out[:, k * s.cols : (k + 1) * s.cols]
@@ -392,7 +414,7 @@
 
 
 def second_kernel(
-    s, blurred_ref, v_in_ref, own_ref, partner_ref, slab_ref, k_ref, ks_ref, kd_ref, yf_ref, yi_ref,
+    s, blurred_ref, own_ref, partner_ref, v_ref, v2_ref, v_halo_ref, own_slab_ref, halo_slab_ref, k_ref, ks_ref, kd_ref, yf_ref, yi_ref,
     xn_ref, xbo_ref, mine_ref, theirs_ref, five_ref,
     re_ref, im_ref, pr_ref, pi_ref, u_ref, t_ref, l_ref, a_ref, b_ref,
 ):
@@ -416,9 +438,12 @@
     near_arrived = from_side(core, s.view_rows, s.cols, s.near)
     for z in range(depth):
         safe = jnp.where(inside, blurred_ref[z], 1.0)
-        first = z // s.q_near * s.view_rows
-        side = turn(slab_ref[first : first + s.view_rows], -(z % s.q_near) * s.near)
-        recorded = jnp.where(near_arrived, side, v_in_ref[z])
+        side = side_slab(
+            s, z // s.q_near, own_slab_ref, halo_slab_ref, s.near,
+            s.depth // s.q_wide * s.rows, s.depth // s.q_wide * 2 * s.wide,
+        )
+        side = turn(side, -(z % s.q_near) * s.near)
+        recorded = jnp.where(near_arrived, side, framed(v_halo_ref[z], of_plane(s, z, v_ref, v2_ref)))
         l_ref[z, : 2 * s.view_rows] = tall_split(jnp.where(inside, recorded / safe, 0.0))
     forward_x(s.view_rows, xn_ref)
     forward_y()
@@ -428,9 +453,7 @@
     owned = (lane // half) == core
 
     def to_update(z, correction):
-        plane = z % s.planes
-        estimate = jnp.where(core == z // s.planes, own_ref[plane], partner_ref[plane])
-        u_ref[z] = jnp.where(owned, estimate * correction, 0.0)
+        u_ref[z] = jnp.where(owned, of_plane(s, z, own_ref, partner_ref) * correction, 0.0)
 
     backward(s.rows, xbo_ref, to_update)
 
@@ -589,31 +612,29 @@
         prefetch=(view_index,),
         where=pltpu.HBM,
     )
-    k, ks, kd = call(
-        functools.partial(kernel_leaves, s), (re, im), [(9 * (s.depth // 2 - 1), s.length // 2, s.cols)] * 3
-    )
-
+    own_rows = (s.depth // s.q_wide + s.depth // s.q_near) * s.rows
+    (own_slab,) = call(functools.partial(pack_own, s), (own, partner, own_view, partner_view, re), [(own_rows, s.cols)])
+    own_slab = lax.ppermute(own_slab, ("gy", "gz"), to_side())
     even, _ = lax.optimization_barrier((even, re))
     even2 = lax.ppermute(even, "gz", across)
-    odd, _ = lax.optimization_barrier((odd, (even2, k)))
+    odd, _ = lax.optimization_barrier((odd, even2))
     odd2 = lax.ppermute(odd, "gz", across)
-    window = (s.depth, s.length, s.cols)
+    halo_rows = s.depth // s.q_wide * 2 * s.wide + s.depth // s.q_near * 2 * s.near
+    e_halo, v_halo, halo_slab_here = call(
+        functools.partial(pack_halo, s),
+        (even, odd, even2, odd2),
+        [(s.depth, 2 * s.wide, s.cols), (s.depth, 2 * s.near, s.cols), (halo_rows, s.cols)],
+    )
+    halo_slab = lax.ppermute(halo_slab_here, ("gy", "gz"), to_side())
+    k, ks, kd = call(
+        functools.partial(kernel_leaves, s),
+        (re, im, halo_slab_here),
+        [(9 * (s.depth // 2 - 1), s.length // 2, s.cols)] * 3,
+    )
     view_window = (s.depth, s.view_rows, s.cols)
-    split_window, slab = call(
-        functools.partial(pack_estimate, s),
-        (own, partner, even, odd, even2, odd2),
-        [((s.depth, 2 * s.length, s.cols), BF16), (s.pack_e, s.cols)],
-        scratch=[window],
-    )
-    slab_here = slab
-    slab = lax.ppermute(slab, ("gy", "gz"), to_side())
-    view_here, view_slab = call(
-        functools.partial(pack_view, s),
-        (own_view, partner_view, even, odd, even2, odd2, slab_here),
-        [view_window, (s.pack_v, s.cols)],
-    )
-    view_slab = lax.ppermute(view_slab, ("gy", "gz"), to_side())
-    (along_x,) = call(functools.partial(along_x_kernel, s), (split_window, t["x_window"]), [window])
+    (along_x,) = call(
+        functools.partial(along_x_kernel, s), (own, partner, e_halo, t["x_window"]), [(s.depth, s.length, s.cols)]
+    )
 
     u_rows = s.planes * s.rows
     out_rows = u_rows
@@ -630,7 +651,7 @@
     shared = (k, ks, kd, t["y_forward"], t["y_inverse"])
     (blurred,) = call(
         functools.partial(first_kernel, s),
-        (along_x, slab) + shared + (t["x_window"], t["x_back_near"]),
+        (along_x, own_slab, halo_slab) + shared + (t["x_window"], t["x_back_near"]),
         [view_window],
         scratch=spectra,
         narrow=halves,
@@ -639,7 +660,7 @@
     )
     mine, theirs, five = call(
         functools.partial(second_kernel, s),
-        (blurred, view_here, own, partner, view_slab) + shared + (t["x_near"], t["x_back_own"]),
+        (blurred, own, partner, own_view, partner_view, v_halo, own_slab, halo_slab) + shared + (t["x_near"], t["x_back_own"]),
         [(out_rows, s.cols), (out_rows, s.cols), (devices, 1, five_shape[0] * five_shape[1])],
         scratch=spectra + [(s.depth, s.rows, s.cols), (4, s.depth // 2, s.rows, s.cols)],
         narrow=[(s.depth, 2 * s.view_rows, s.cols)] + halves,

time: 44.5 us -> 44.3 us (level)
  blocking collectives: 15.2 us -> 13.6 us
  starting transfers between devices: 12 us -> 13.3 us
  waiting for transfers between devices: 2.04 us -> 2.63 us
    ppermute x1, starting transfers between devices: 5.79 us -> 7.62 us  [local(): got = lax.ppermute(theirs, 'gz', across)]
    all_to_all x1, blocking collectives: 15.2 us -> 13.6 us  [local(): fives = lax.all_to_all(five, ALL, split_axis=0, concat_axis=0, tiled=True)]
    ppermute x1, waiting for transfers between devices: 0.91 us -> 0.01 us  [local(): odd2 = lax.ppermute(odd, 'gz', across)]
    ppermute x1, waiting for transfers between devices: 0.01 us -> 0.9 us  [local(): even2 = lax.ppermute(even, 'gz', across)]
    ppermute x1, starting transfers between devices: 0.5 us -> 0.01 us  [local(): partner_view = lax.ppermute(own_view, 'gz', across)]
  transfers between devices with their start and end apart: 9 -> 9, of which waited for: 2 -> 4; matrix products, arithmetic and copies ran while one was open for 0% -> 0% of each run, Pallas kernels for 18% -> 10%
where the time goes in v5:
time: 44.3 us; the launch traced here: 44.1 us
  blocking collectives  13.6 us (31%)
  starting transfers between devices  13.3 us (30%)
  Pallas kernels  13 us (29%)
  waiting for transfers between devices  2.63 us (6%)
  between operations  1.47 us (3%)
    all_to_all x1, blocking collectives, local(): fives = lax.all_to_all(five, ALL, split_axis=0, concat_axis=0, tiled=True)  13.6 us
    pallas_call x9, Pallas kernels, call(): pl.pallas_call(body, grid_spec=pltpu.PrefetchScalarGridSpec(num_scalar_pr...  13 us
    ppermute x1, starting transfers between devices, local(): got = lax.ppermute(theirs, 'gz', across)  7.62 us
    ppermute x1, starting transfers between devices, local(): even = lax.ppermute(even, 'gx', neighbours(0))  3.03 us
    ppermute x1, waiting for transfers between devices, local(): even = lax.ppermute(even, 'gx', neighbours(0))  1.11 us
    ppermute x1, waiting for transfers between devices, local(): even2 = lax.ppermute(even, 'gz', across)  0.9 us
  transfers between devices with their start and end apart: 9, of which 4 were waited for; matrix products, arithmetic and copies ran while one was open for 0% of the time, Pallas kernels for 10%

profile of v5, /device:TPU:0, one launch (start us, length us, event | category | flops | bytes accessed | tf_op | source)
XLA Modules:
  0.0 44.1 jit_solution(10429464104596102674)
XLA Ops:
  0.6 1.1 %shard_map.163 = (f32[8,64,128]{2,1,0:T(8,128)S(1)}, f32[8,64,128]{2,1,0:T(8,128)S(1)}, f32[360,128]{1,0:T(8,128)S(1)}, f32[360,128]{1,0:T(8,128)S(1)}) custom-call(f32[8,64,128]{2,1,0:T(8,128)} %e_in.1, f32[8,64,128]{2,1,0:T(8,128)} %v_in.1), custom_call_target="tpu_custom_call" | custom-call | flops 10000000 | tf_op jit(solution)/shard_map/pallas_call | solution.py:552
  1.7 3.0 %collective-permute-start.1 = (f32[360,128]{1,0:T(8,128)S(1)}, f32[360,128]{1,0:T(8,128)S(1)}, u32[]{:S(2)}, u32[]{:S(2)}) collective-permute-start(f32[360,128]{1,0:T(8,128)S(1)} %get-tuple-element.24), channel_id=1, source_target_pairs={{0,8},{8,0},{16,24},{24,16},{1,9},{9,1},{17,25},{25,17},{2,10},{10... | collective-permute-start | bytes 552968 | tf_op jit(solution)/shard_map/ppermute | solution.py:597
  4.7 0.7 %collective-permute-start.2 = (f32[360,128]{1,0:T(8,128)S(1)}, f32[360,128]{1,0:T(8,128)S(1)}, u32[]{:S(2)}, u32[]{:S(2)}) collective-permute-start(f32[360,128]{1,0:T(8,128)S(1)} %get-tuple-element.27), channel_id=1, source_target_pairs={{8,16},{16,8},{9,17},{17,9},{10,18},{18,10},{11,19},{19,11},{12,20... | collective-permute-start | bytes 552968 | tf_op jit(solution)/shard_map/ppermute | solution.py:598
  6.1 2.2 %shard_map.164 = (f32[31,64,128]{2,1,0:T(8,128)S(1)}, f32[31,64,128]{2,1,0:T(8,128)S(1)}) custom-call(s32[1]{0:T(128)S(6)} %copy.18.view_ref, f32[6,31,31,31]{3,2,1,0:T(8,128)} %psf_in.1, bf16[256,256]{1,0:T(8,128)(2,1)} %constant.18.clone.y_in, bf16[128,96]{1,0:T(8,128)(2,1)} %constant.23.clone.x_in), custom_call_target="tpu_custom_call" | custom-call | flops 10000000 | tf_op jit(solution)/shard_map/pallas_call | solution.py:552
  8.3 1.1 %collective-permute-done.1.even_ref = f32[360,128]{1,0:T(8,128)S(1)} collective-permute-done((f32[360,128]{1,0:T(8,128)S(1)}, f32[360,128]{1,0:T(8,128)S(1)}, u32[]{:S(2)}, u32[]{:S(2)}) %collective-permute-start.1) | collective-permute-done | bytes 184352 | tf_op jit(solution)/shard_map/ppermute | solution.py:597
  9.4 0.5 %collective-permute-start = (f32[8,64,128]{2,1,0:T(8,128)S(1)}, f32[8,64,128]{2,1,0:T(8,128)S(1)}, u32[]{:S(2)}, u32[]{:S(2)}) collective-permute-start(f32[8,64,128]{2,1,0:T(8,128)S(1)} %get-tuple-element.23.e_ref.own_ref), channel_id=1, source_target_pairs={{0,1},{1,0},{2,3},{3,2},{4,5},{5,4},{6,7},{7,6},{8,9},{9,8},{10,11... | collective-permute-start | bytes 786440 | tf_op jit(solution)/shard_map/ppermute | solution.py:599
  9.9 0.9 %collective-permute-done.3.even2_ref = f32[360,128]{1,0:T(8,128)S(1)} collective-permute-done((f32[360,128]{1,0:T(8,128)S(1)}, f32[360,128]{1,0:T(8,128)S(1)}, u32[]{:S(2)}, u32[]{:S(2)}) %collective-permute-start.3) | collective-permute-done | bytes 184352 | tf_op jit(solution)/shard_map/ppermute | solution.py:619
  10.8 0.1 collective-permute-start.4
  11.0 0.2 collective-permute-done.e2_ref.partner_ref
  11.2 0.4 collective-permute-done.5.v2_ref
  11.6 0.3 shard_map.167
  11.9 0.7 %collective-permute-start.6 = (f32[384,128]{1,0:T(8,128)S(1)}, f32[384,128]{1,0:T(8,128)S(1)}, u32[]{:S(2)}, u32[]{:S(2)}) collective-permute-start(f32[384,128]{1,0:T(8,128)S(1)} %shard_map.167), channel_id=1, source_target_pairs={{1,2},{2,1},{3,4},{4,3},{5,6},{6,5},{9,10},{10,9},{11,12},{12,11},... | collective-permute-start | bytes 589832 | tf_op jit(solution)/shard_map/ppermute | solution.py:617
  12.5 0.3 shard_map.165
  12.9 0.7 %collective-permute-start.7 = (f32[320,128]{1,0:T(8,128)S(1)}, f32[320,128]{1,0:T(8,128)S(1)}, u32[]{:S(2)}, u32[]{:S(2)}) collective-permute-start(f32[320,128]{1,0:T(8,128)S(1)} %get-tuple-element.31.after_ref), channel_id=1, source_target_pairs={{1,2},{2,1},{3,4},{4,3},{5,6},{6,5},{9,10},{10,9},{11,12},{12,11},... | collective-permute-start | bytes 491528 | tf_op jit(solution)/shard_map/ppermute | solution.py:628
  13.5 0.0 copy-start
  13.5 0.0 copy-start.1
  13.6 0.0 copy-start.4
  13.6 1.1 %shard_map.168 = (f32[63,64,128]{2,1,0:T(8,128)S(1)}, f32[63,64,128]{2,1,0:T(8,128)S(1)}, f32[63,64,128]{2,1,0:T(8,128)S(1)}) custom-call(f32[31,64,128]{2,1,0:T(8,128)S(1)} %get-tuple-element.25.after_ref.re_ref, f32[31,64,128]{2,1,0:T(8,128)S(1)} %get-tuple-element.32.im_ref, f32[320,128]{1,0:T(8,128)S(1)} %get-tuple-element.31.after_ref), custom_call_target="tpu_custom_call" | custom-call | flops 10000000 | tf_op jit(solution)/shard_map/pallas_call | solution.py:552
  14.6 0.4 %shard_map.166.t_in_ref = f32[16,128,128]{2,1,0:T(8,128)S(1)} custom-call(f32[8,64,128]{2,1,0:T(8,128)S(1)} %get-tuple-element.23.e_ref.own_ref, f32[8,64,128]{2,1,0:T(8,128)S(1)} %collective-permute-done.e2_ref.partner_ref, f32[16,64,128]{2,1,0:T(8,128)S(1)} %get-tuple-element.29.halo_ref, bf16[256,256]{1,0:T(8,128)(2,1)S(1)} %copy-done.2), custom_call_target="tpu_custom_call" | custom-call | flops 10000000 | tf_op jit(solution)/shard_map/pallas_call | solution.py:552
  15.2 3.2 %shard_map.169.blurred_ref = f32[16,96,128]{2,1,0:T(8,128)S(1)} custom-call(f32[16,128,128]{2,1,0:T(8,128)S(1)} %shard_map.166.t_in_ref, f32[384,128]{1,0:T(8,128)S(1)} %collective-permute-done.6.own_slab_ref, f32[320,128]{1,0:T(8,128)S(1)} %collective-permute-done.7.halo_slab_ref, f32[63,64,128]{2,1,0:T(8,128)S(1)} %get-tuple-element.33.k_ref, ...), custom_call_target="tpu_custom_call" | custom-call | flops 100000000 | tf_op jit(solution)/shard_map/pallas_call | solution.py:552
  18.4 3.7 %shard_map.170 = (f32[688,128]{1,0:T(8,128)S(1)}, f32[688,128]{1,0:T(8,128)S(1)}, f32[32,1,128]{2,1,0:T(1,128)S(1)}) custom-call(f32[16,96,128]{2,1,0:T(8,128)S(1)} %shard_map.169.blurred_ref, f32[8,64,128]{2,1,0:T(8,128)S(1)} %get-tuple-element.23.e_ref.own_ref, f32[8,64,128]{2,1,0:T(8,128)S(1)} %collective-permute-done.e2_ref.partner_ref, ...), custom_call_target="tpu_custom_call" | custom-call | flops 10000000 | tf_op jit(solution)/shard_map/pallas_call | solution.py:552
  22.1 7.6 %collective-permute-start.8 = (f32[688,128]{1,0:T(8,128)S(1)}, f32[688,128]{1,0:T(8,128)S(1)}, u32[]{:S(2)}, u32[]{:S(2)}) collective-permute-start(f32[688,128]{1,0:T(8,128)S(1)} %get-tuple-element.38), channel_id=1, source_target_pairs={{0,1},{1,0},{2,3},{3,2},{4,5},{5,4},{6,7},{7,6},{8,9},{9,8},{10,11... | collective-permute-start | bytes 1056776 | tf_op jit(solution)/shard_map/ppermute | solution.py:669
  29.7 13.6 %all_to_all.5.fives_ref = f32[32,1,128]{2,1,0:T(1,128)S(1)} all-to-all(f32[32,1,128]{2,1,0:T(1,128)S(1)} %get-tuple-element.39), channel_id=1, replica_groups=mesh['gx'=4,'gy'=4,'gz'=2] {'gx','gy','gz'}, dimensions={0} | all-to-all | bytes 32768 | tf_op jit(solution)/shard_map/all_to_all | solution.py:670
  43.3 0.8 %shard_map.171 = (f32[8,64,128]{2,1,0:T(8,128)}, f32[4,32,64]{2,1,0:T(8,128)}, f32[2,16,32]{2,1,0:T(8,128)}, f32[1,8,16]{2,1,0:T(8,128)}, f32[1,4,8]{2,1,0:T(4,128)}, /*index=5*/f32[1,8,16]{2,1,0:T(8,128)}) custom-call(f32[688,128]{1,0:T(8,128)S(1)} %get-tuple-element.37.mine_ref, f32[688,128]{1,0:T(8,128)S(1)} %collective-permute-done.8.got_ref, ...), custom_call_target="tpu_custom_call" | custom-call | flops 10000000 | tf_op jit(solution)/shard_map/pallas_call | solution.py:552
  (16 shorter events, 0.0 us)
Async XLA Ops:
  1.7 7.7 %collective-permute-start.1 = (f32[360,128]{1,0:T(8,128)S(1)}, f32[360,128]{1,0:T(8,128)S(1)}, u32[]{:S(2)}, u32[]{:S(2)}) collective-permute-start(f32[360,128]{1,0:T(8,128)S(1)} %get-tuple-element.24), channel_id=1, source_target_pairs={{0,8},{8,0},{16,24},{24,16},{1,9},{9,1},{17,25},{25,17},{2,10},{10... | collective-permute-start | bytes 552968 | tf_op jit(solution)/shard_map/ppermute | solution.py:597
  4.7 5.2 %collective-permute-start.2 = (f32[360,128]{1,0:T(8,128)S(1)}, f32[360,128]{1,0:T(8,128)S(1)}, u32[]{:S(2)}, u32[]{:S(2)}) collective-permute-start(f32[360,128]{1,0:T(8,128)S(1)} %get-tuple-element.27), channel_id=1, source_target_pairs={{8,16},{16,8},{9,17},{17,9},{10,18},{18,10},{11,19},{19,11},{12,20... | collective-permute-start | bytes 552968 | tf_op jit(solution)/shard_map/ppermute | solution.py:598
  9.4 1.4 %collective-permute-start.3 = (f32[360,128]{1,0:T(8,128)S(1)}, f32[360,128]{1,0:T(8,128)S(1)}, u32[]{:S(2)}, u32[]{:S(2)}) collective-permute-start(f32[360,128]{1,0:T(8,128)S(1)} %collective-permute-done.1.even_ref), channel_id=1, source_target_pairs={{0,1},{1,0},{2,3},{3,2},{4,5},{5,4},{6,7},{7,6},{8,9},{9,8},{10,11... | collective-permute-start | bytes 552968 | tf_op jit(solution)/shard_map/ppermute | solution.py:619
  9.4 1.8 %collective-permute-start = (f32[8,64,128]{2,1,0:T(8,128)S(1)}, f32[8,64,128]{2,1,0:T(8,128)S(1)}, u32[]{:S(2)}, u32[]{:S(2)}) collective-permute-start(f32[8,64,128]{2,1,0:T(8,128)S(1)} %get-tuple-element.23.e_ref.own_ref), channel_id=1, source_target_pairs={{0,1},{1,0},{2,3},{3,2},{4,5},{5,4},{6,7},{7,6},{8,9},{9,8},{10,11... | collective-permute-start | bytes 786440 | tf_op jit(solution)/shard_map/ppermute | solution.py:599
  9.9 4.7 %copy-start.2 = (bf16[256,256]{1,0:T(8,128)(2,1)S(1)}, bf16[256,256]{1,0:T(8,128)(2,1)}, u32[]{:S(2)}) copy-start(bf16[256,256]{1,0:T(8,128)(2,1)} %constant.19.clone.x_ref.xw_ref) | copy-start | bytes 393220
  9.9 1.7 %collective-permute-start.5 = (f32[8,64,128]{2,1,0:T(8,128)S(1)}, f32[8,64,128]{2,1,0:T(8,128)S(1)}, u32[]{:S(2)}, u32[]{:S(2)}) collective-permute-start(f32[8,64,128]{2,1,0:T(8,128)S(1)} %get-tuple-element.30.v_ref), channel_id=1, source_target_pairs={{0,1},{1,0},{2,3},{3,2},{4,5},{5,4},{6,7},{7,6},{8,9},{9,8},{10,11... | collective-permute-start | bytes 786440 | tf_op jit(solution)/shard_map/ppermute | solution.py:600
  10.8 1.7 %collective-permute-start.4 = (f32[360,128]{1,0:T(8,128)S(1)}, f32[360,128]{1,0:T(8,128)S(1)}, u32[]{:S(2)}, u32[]{:S(2)}) collective-permute-start(f32[360,128]{1,0:T(8,128)S(1)} %collective-permute-done.2.odd_ref), channel_id=1, source_target_pairs={{0,1},{1,0},{2,3},{3,2},{4,5},{5,4},{6,7},{7,6},{8,9},{9,8},{10,11... | collective-permute-start | bytes 552968 | tf_op jit(solution)/shard_map/ppermute | solution.py:621
  11.9 3.2 %collective-permute-start.6 = (f32[384,128]{1,0:T(8,128)S(1)}, f32[384,128]{1,0:T(8,128)S(1)}, u32[]{:S(2)}, u32[]{:S(2)}) collective-permute-start(f32[384,128]{1,0:T(8,128)S(1)} %shard_map.167), channel_id=1, source_target_pairs={{1,2},{2,1},{3,4},{4,3},{5,6},{6,5},{9,10},{10,9},{11,12},{12,11},... | collective-permute-start | bytes 589832 | tf_op jit(solution)/shard_map/ppermute | solution.py:617
  12.9 2.3 %collective-permute-start.7 = (f32[320,128]{1,0:T(8,128)S(1)}, f32[320,128]{1,0:T(8,128)S(1)}, u32[]{:S(2)}, u32[]{:S(2)}) collective-permute-start(f32[320,128]{1,0:T(8,128)S(1)} %get-tuple-element.31.after_ref), channel_id=1, source_target_pairs={{1,2},{2,1},{3,4},{4,3},{5,6},{6,5},{9,10},{10,9},{11,12},{12,11},... | collective-permute-start | bytes 491528 | tf_op jit(solution)/shard_map/ppermute | solution.py:628
  13.5 1.6 %copy-start = (bf16[2,256,256]{2,1,0:T(8,128)(2,1)S(1)}, bf16[2,256,256]{2,1,0:T(8,128)(2,1)}, u32[]{:S(2)}) copy-start(bf16[2,256,256]{2,1,0:T(8,128)(2,1)} %constant.16.clone.yf_ref) | copy-start | bytes 786436
  13.5 1.6 %copy-start.1 = (bf16[2,256,256]{2,1,0:T(8,128)(2,1)S(1)}, bf16[2,256,256]{2,1,0:T(8,128)(2,1)}, u32[]{:S(2)}) copy-start(bf16[2,256,256]{2,1,0:T(8,128)(2,1)} %constant.17.clone.yi_ref) | copy-start | bytes 786436
  13.6 1.6 %copy-start.4 = (bf16[192,256]{1,0:T(8,128)(2,1)S(1)}, bf16[192,256]{1,0:T(8,128)(2,1)}, u32[]{:S(2)}) copy-start(bf16[192,256]{1,0:T(8,128)(2,1)} %constant.21.clone.xbn_ref) | copy-start | bytes 294916
  15.1 3.3 %copy-start.3 = (bf16[256,192]{1,0:T(8,128)(2,1)S(1)}, bf16[256,192]{1,0:T(8,128)(2,1)}, u32[]{:S(2)}) copy-start(bf16[256,192]{1,0:T(8,128)(2,1)} %constant.20.clone.xn_ref) | copy-start | bytes 294916
  15.2 3.3 %copy-start.5 = (bf16[128,256]{1,0:T(8,128)(2,1)S(1)}, bf16[128,256]{1,0:T(8,128)(2,1)}, u32[]{:S(2)}) copy-start(bf16[128,256]{1,0:T(8,128)(2,1)} %constant.22.clone.xbo_ref) | copy-start | bytes 196612
  22.1 21.2 %collective-permute-start.8 = (f32[688,128]{1,0:T(8,128)S(1)}, f32[688,128]{1,0:T(8,128)S(1)}, u32[]{:S(2)}, u32[]{:S(2)}) collective-permute-start(f32[688,128]{1,0:T(8,128)S(1)} %get-tuple-element.38), channel_id=1, source_target_pairs={{0,1},{1,0},{2,3},{3,2},{4,5},{5,4},{6,7},{7,6},{8,9},{9,8},{10,11... | collective-permute-start | bytes 1056776 | tf_op jit(solution)/shard_map/ppermute | solution.py:669

commit v6 on v5

--- a/solution.py
+++ b/solution.py
@@ -215,7 +215,9 @@
     return jnp.concatenate([frame[:pad], body, frame[pad:]], 0)
 
 
-def along_x_kernel(s, e_ref, e2_ref, halo_ref, x_ref, t_ref):
+def along_x_kernel(s, e_ref, e2_ref, halo_ref, x_ref, v_ref, v2_ref, v_halo_ref, t_ref, v_window_ref):
+    for z in range(s.depth):
+        v_window_ref[z] = framed(v_halo_ref[z], of_plane(s, z, v_ref, v2_ref))
     for z in range(0, s.depth, 2):
         both = [tall_split(framed(halo_ref[z + side], of_plane(s, z + side, e_ref, e2_ref))) for side in (0, 1)]
         out = fold_rows(dot(x_ref[...], jnp.concatenate(both, 1)))
@@ -289,7 +291,7 @@
                         place += 1
         return carry
 
-    lax.fori_loop(0, s.length // 16, tile, 0)
+    lax.fori_loop(0, s.length // 16, tile, 0, unroll=2)
 
 
 def from_side(core, rows, cols, width):
@@ -300,7 +302,7 @@
 def stages(s, k_ref, ks_ref, kd_ref, yf_ref, yi_ref, re_ref, im_ref, pr_ref, pi_ref, a_ref, b_ref, l_ref=None):
     half = s.cols // 2
     depth = s.depth
-    group = 4
+    group = 8
     freqs = s.length // 2
 
     def forward_x(rows, x_table):
@@ -414,7 +416,7 @@
 
 
 def second_kernel(
-    s, blurred_ref, own_ref, partner_ref, v_ref, v2_ref, v_halo_ref, own_slab_ref, halo_slab_ref, k_ref, ks_ref, kd_ref, yf_ref, yi_ref,
+    s, blurred_ref, own_ref, partner_ref, v_window_ref, own_slab_ref, halo_slab_ref, k_ref, ks_ref, kd_ref, yf_ref, yi_ref,
     xn_ref, xbo_ref, mine_ref, theirs_ref, five_ref,
     re_ref, im_ref, pr_ref, pi_ref, u_ref, t_ref, l_ref, a_ref, b_ref,
 ):
@@ -443,7 +445,7 @@
             s.depth // s.q_wide * s.rows, s.depth // s.q_wide * 2 * s.wide,
         )
         side = turn(side, -(z % s.q_near) * s.near)
-        recorded = jnp.where(near_arrived, side, framed(v_halo_ref[z], of_plane(s, z, v_ref, v2_ref)))
+        recorded = jnp.where(near_arrived, side, v_window_ref[z])
         l_ref[z, : 2 * s.view_rows] = tall_split(jnp.where(inside, recorded / safe, 0.0))
     forward_x(s.view_rows, xn_ref)
     forward_y()
@@ -632,8 +634,10 @@
         [(9 * (s.depth // 2 - 1), s.length // 2, s.cols)] * 3,
     )
     view_window = (s.depth, s.view_rows, s.cols)
-    (along_x,) = call(
-        functools.partial(along_x_kernel, s), (own, partner, e_halo, t["x_window"]), [(s.depth, s.length, s.cols)]
+    along_x, v_window = call(
+        functools.partial(along_x_kernel, s),
+        (own, partner, e_halo, t["x_window"], own_view, partner_view, v_halo),
+        [(s.depth, s.length, s.cols), view_window],
     )
 
     u_rows = s.planes * s.rows
@@ -660,7 +664,7 @@
     )
     mine, theirs, five = call(
         functools.partial(second_kernel, s),
-        (blurred, own, partner, own_view, partner_view, v_halo, own_slab, halo_slab) + shared + (t["x_near"], t["x_back_own"]),
+        (blurred, own, partner, v_window, own_slab, halo_slab) + shared + (t["x_near"], t["x_back_own"]),
         [(out_rows, s.cols), (out_rows, s.cols), (devices, 1, five_shape[0] * five_shape[1])],
         scratch=spectra + [(s.depth, s.rows, s.cols), (4, s.depth // 2, s.rows, s.cols)],
         narrow=[(s.depth, 2 * s.view_rows, s.cols)] + halves,

time: 44.3 us -> 44.3 us (level)
    ppermute x1, starting transfers between devices: 0.51 us -> 0.01 us  [local(): partner = lax.ppermute(own, 'gz', across)]
    ppermute x1, starting transfers between devices: 0.01 us -> 0.51 us  [local(): partner_view = lax.ppermute(own_view, 'gz', across)]
where the time goes in v6:
time: 44.3 us; the launch traced here: 44.1 us
  blocking collectives  13.6 us (31%)
  starting transfers between devices  13.3 us (30%)
  Pallas kernels  13.1 us (30%)
  waiting for transfers between devices  2.63 us (6%)
  between operations  1.47 us (3%)
    all_to_all x1, blocking collectives, local(): fives = lax.all_to_all(five, ALL, split_axis=0, concat_axis=0, tiled=True)  13.6 us
    pallas_call x9, Pallas kernels, call(): pl.pallas_call(body, grid_spec=pltpu.PrefetchScalarGridSpec(num_scalar_pr...  13.1 us
    ppermute x1, starting transfers between devices, local(): got = lax.ppermute(theirs, 'gz', across)  7.61 us
    ppermute x1, starting transfers between devices, local(): even = lax.ppermute(even, 'gx', neighbours(0))  3.03 us
    ppermute x1, waiting for transfers between devices, local(): even = lax.ppermute(even, 'gx', neighbours(0))  1.11 us
    ppermute x1, waiting for transfers between devices, local(): even2 = lax.ppermute(even, 'gz', across)  0.9 us
  transfers between devices with their start and end apart: 9, of which 4 were waited for; matrix products, arithmetic and copies ran while one was open for 0% of the time, Pallas kernels for 10%

profile of v6, /device:TPU:0, one launch (start us, length us, event | category | flops | bytes accessed | tf_op | source)
XLA Modules:
  0.0 44.1 jit_solution(5671040770971920606)
XLA Ops:
  0.6 1.1 %shard_map.163 = (f32[8,64,128]{2,1,0:T(8,128)S(1)}, f32[8,64,128]{2,1,0:T(8,128)S(1)}, f32[360,128]{1,0:T(8,128)S(1)}, f32[360,128]{1,0:T(8,128)S(1)}) custom-call(f32[8,64,128]{2,1,0:T(8,128)} %e_in.1, f32[8,64,128]{2,1,0:T(8,128)} %v_in.1), custom_call_target="tpu_custom_call" | custom-call | flops 10000000 | tf_op jit(solution)/shard_map/pallas_call | solution.py:554
  1.7 3.0 %collective-permute-start.1 = (f32[360,128]{1,0:T(8,128)S(1)}, f32[360,128]{1,0:T(8,128)S(1)}, u32[]{:S(2)}, u32[]{:S(2)}) collective-permute-start(f32[360,128]{1,0:T(8,128)S(1)} %get-tuple-element.26), channel_id=1, source_target_pairs={{0,8},{8,0},{16,24},{24,16},{1,9},{9,1},{17,25},{25,17},{2,10},{10... | collective-permute-start | bytes 552968 | tf_op jit(solution)/shard_map/ppermute | solution.py:599
  4.7 0.7 %collective-permute-start.2 = (f32[360,128]{1,0:T(8,128)S(1)}, f32[360,128]{1,0:T(8,128)S(1)}, u32[]{:S(2)}, u32[]{:S(2)}) collective-permute-start(f32[360,128]{1,0:T(8,128)S(1)} %get-tuple-element.29), channel_id=1, source_target_pairs={{8,16},{16,8},{9,17},{17,9},{10,18},{18,10},{11,19},{19,11},{12,20... | collective-permute-start | bytes 552968 | tf_op jit(solution)/shard_map/ppermute | solution.py:600
  6.1 2.2 %shard_map.164 = (f32[31,64,128]{2,1,0:T(8,128)S(1)}, f32[31,64,128]{2,1,0:T(8,128)S(1)}) custom-call(s32[1]{0:T(128)S(6)} %copy.18.view_ref, f32[6,31,31,31]{3,2,1,0:T(8,128)} %psf_in.1, bf16[256,256]{1,0:T(8,128)(2,1)} %constant.18.clone.y_in, bf16[128,96]{1,0:T(8,128)(2,1)} %constant.23.clone.x_in), custom_call_target="tpu_custom_call" | custom-call | flops 10000000 | tf_op jit(solution)/shard_map/pallas_call | solution.py:554
  8.3 1.1 %collective-permute-done.1.even_ref = f32[360,128]{1,0:T(8,128)S(1)} collective-permute-done((f32[360,128]{1,0:T(8,128)S(1)}, f32[360,128]{1,0:T(8,128)S(1)}, u32[]{:S(2)}, u32[]{:S(2)}) %collective-permute-start.1) | collective-permute-done | bytes 184352 | tf_op jit(solution)/shard_map/ppermute | solution.py:599
  9.4 0.5 %collective-permute-start.5 = (f32[8,64,128]{2,1,0:T(8,128)S(1)}, f32[8,64,128]{2,1,0:T(8,128)S(1)}, u32[]{:S(2)}, u32[]{:S(2)}) collective-permute-start(f32[8,64,128]{2,1,0:T(8,128)S(1)} %get-tuple-element.32.v_ref), channel_id=1, source_target_pairs={{0,1},{1,0},{2,3},{3,2},{4,5},{5,4},{6,7},{7,6},{8,9},{9,8},{10,11... | collective-permute-start | bytes 786440 | tf_op jit(solution)/shard_map/ppermute | solution.py:602
  9.9 0.9 %collective-permute-done.3.even2_ref = f32[360,128]{1,0:T(8,128)S(1)} collective-permute-done((f32[360,128]{1,0:T(8,128)S(1)}, f32[360,128]{1,0:T(8,128)S(1)}, u32[]{:S(2)}, u32[]{:S(2)}) %collective-permute-start.3) | collective-permute-done | bytes 184352 | tf_op jit(solution)/shard_map/ppermute | solution.py:621
  10.8 0.1 collective-permute-start.4
  11.0 0.2 collective-permute-done.5.v2_ref
  11.2 0.4 collective-permute-done.e2_ref.partner_ref
  11.6 0.3 shard_map.167
  11.9 0.7 %collective-permute-start.6 = (f32[384,128]{1,0:T(8,128)S(1)}, f32[384,128]{1,0:T(8,128)S(1)}, u32[]{:S(2)}, u32[]{:S(2)}) collective-permute-start(f32[384,128]{1,0:T(8,128)S(1)} %shard_map.167), channel_id=1, source_target_pairs={{1,2},{2,1},{3,4},{4,3},{5,6},{6,5},{9,10},{10,9},{11,12},{12,11},... | collective-permute-start | bytes 589832 | tf_op jit(solution)/shard_map/ppermute | solution.py:619
  12.5 0.3 shard_map.165
  12.9 0.7 %collective-permute-start.7 = (f32[320,128]{1,0:T(8,128)S(1)}, f32[320,128]{1,0:T(8,128)S(1)}, u32[]{:S(2)}, u32[]{:S(2)}) collective-permute-start(f32[320,128]{1,0:T(8,128)S(1)} %get-tuple-element.35.after_ref), channel_id=1, source_target_pairs={{1,2},{2,1},{3,4},{4,3},{5,6},{6,5},{9,10},{10,9},{11,12},{12,11},... | collective-permute-start | bytes 491528 | tf_op jit(solution)/shard_map/ppermute | solution.py:630
  13.5 0.0 copy-start
  13.5 0.0 copy-start.1
  13.6 0.0 copy-start.4
  13.6 1.0 %shard_map.168 = (f32[63,64,128]{2,1,0:T(8,128)S(1)}, f32[63,64,128]{2,1,0:T(8,128)S(1)}, f32[63,64,128]{2,1,0:T(8,128)S(1)}) custom-call(f32[31,64,128]{2,1,0:T(8,128)S(1)} %get-tuple-element.27.after_ref.re_ref, f32[31,64,128]{2,1,0:T(8,128)S(1)} %get-tuple-element.36.im_ref, f32[320,128]{1,0:T(8,128)S(1)} %get-tuple-element.35.after_ref), custom_call_target="tpu_custom_call" | custom-call | flops 10000000 | tf_op jit(solution)/shard_map/pallas_call | solution.py:554
  14.6 0.5 %shard_map.166 = (f32[16,128,128]{2,1,0:T(8,128)S(1)}, f32[16,96,128]{2,1,0:T(8,128)S(1)}) custom-call(f32[8,64,128]{2,1,0:T(8,128)S(1)} %get-tuple-element.25.e_ref.own_ref, f32[8,64,128]{2,1,0:T(8,128)S(1)} %collective-permute-done.e2_ref.partner_ref, f32[16,64,128]{2,1,0:T(8,128)S(1)} %get-tuple-element.31.halo_ref, bf16[256,256]{1,0:T(8,128)(2,1)S(1)} %copy-done.2, ...), custom_call_target="tpu_custom_call" | custom-call | flops 10000000 | tf_op jit(solution)/shard_map/pallas_call | solution.py:554
  15.2 3.3 %shard_map.169.blurred_ref = f32[16,96,128]{2,1,0:T(8,128)S(1)} custom-call(f32[16,128,128]{2,1,0:T(8,128)S(1)} %get-tuple-element.34.t_in_ref, f32[384,128]{1,0:T(8,128)S(1)} %collective-permute-done.6.own_slab_ref, f32[320,128]{1,0:T(8,128)S(1)} %collective-permute-done.7.halo_slab_ref, f32[63,64,128]{2,1,0:T(8,128)S(1)} %get-tuple-element.37.k_ref, ...), custom_call_target="tpu_custom_call" | custom-call | flops 100000000 | tf_op jit(solution)/shard_map/pallas_call | solution.py:554
  18.5 3.6 %shard_map.170 = (f32[688,128]{1,0:T(8,128)S(1)}, f32[688,128]{1,0:T(8,128)S(1)}, f32[32,1,128]{2,1,0:T(1,128)S(1)}) custom-call(f32[16,96,128]{2,1,0:T(8,128)S(1)} %shard_map.169.blurred_ref, f32[8,64,128]{2,1,0:T(8,128)S(1)} %get-tuple-element.25.e_ref.own_ref, f32[8,64,128]{2,1,0:T(8,128)S(1)} %collective-permute-done.e2_ref.partner_ref, ...), custom_call_target="tpu_custom_call" | custom-call | flops 10000000 | tf_op jit(solution)/shard_map/pallas_call | solution.py:554
  22.1 7.6 %collective-permute-start.8 = (f32[688,128]{1,0:T(8,128)S(1)}, f32[688,128]{1,0:T(8,128)S(1)}, u32[]{:S(2)}, u32[]{:S(2)}) collective-permute-start(f32[688,128]{1,0:T(8,128)S(1)} %get-tuple-element.42), channel_id=1, source_target_pairs={{0,1},{1,0},{2,3},{3,2},{4,5},{5,4},{6,7},{7,6},{8,9},{9,8},{10,11... | collective-permute-start | bytes 1056776 | tf_op jit(solution)/shard_map/ppermute | solution.py:673
  29.7 13.6 %all_to_all.5.fives_ref = f32[32,1,128]{2,1,0:T(1,128)S(1)} all-to-all(f32[32,1,128]{2,1,0:T(1,128)S(1)} %get-tuple-element.43), channel_id=1, replica_groups=mesh['gx'=4,'gy'=4,'gz'=2] {'gx','gy','gz'}, dimensions={0} | all-to-all | bytes 32768 | tf_op jit(solution)/shard_map/all_to_all | solution.py:674
  43.3 0.8 %shard_map.171 = (f32[8,64,128]{2,1,0:T(8,128)}, f32[4,32,64]{2,1,0:T(8,128)}, f32[2,16,32]{2,1,0:T(8,128)}, f32[1,8,16]{2,1,0:T(8,128)}, f32[1,4,8]{2,1,0:T(4,128)}, /*index=5*/f32[1,8,16]{2,1,0:T(8,128)}) custom-call(f32[688,128]{1,0:T(8,128)S(1)} %get-tuple-element.41.mine_ref, f32[688,128]{1,0:T(8,128)S(1)} %collective-permute-done.8.got_ref, ...), custom_call_target="tpu_custom_call" | custom-call | flops 10000000 | tf_op jit(solution)/shard_map/pallas_call | solution.py:554
  (16 shorter events, 0.0 us)
Async XLA Ops:
  1.7 7.7 %collective-permute-start.1 = (f32[360,128]{1,0:T(8,128)S(1)}, f32[360,128]{1,0:T(8,128)S(1)}, u32[]{:S(2)}, u32[]{:S(2)}) collective-permute-start(f32[360,128]{1,0:T(8,128)S(1)} %get-tuple-element.26), channel_id=1, source_target_pairs={{0,8},{8,0},{16,24},{24,16},{1,9},{9,1},{17,25},{25,17},{2,10},{10... | collective-permute-start | bytes 552968 | tf_op jit(solution)/shard_map/ppermute | solution.py:599
  4.7 5.2 %collective-permute-start.2 = (f32[360,128]{1,0:T(8,128)S(1)}, f32[360,128]{1,0:T(8,128)S(1)}, u32[]{:S(2)}, u32[]{:S(2)}) collective-permute-start(f32[360,128]{1,0:T(8,128)S(1)} %get-tuple-element.29), channel_id=1, source_target_pairs={{8,16},{16,8},{9,17},{17,9},{10,18},{18,10},{11,19},{19,11},{12,20... | collective-permute-start | bytes 552968 | tf_op jit(solution)/shard_map/ppermute | solution.py:600
  9.4 1.4 %collective-permute-start.3 = (f32[360,128]{1,0:T(8,128)S(1)}, f32[360,128]{1,0:T(8,128)S(1)}, u32[]{:S(2)}, u32[]{:S(2)}) collective-permute-start(f32[360,128]{1,0:T(8,128)S(1)} %collective-permute-done.1.even_ref), channel_id=1, source_target_pairs={{0,1},{1,0},{2,3},{3,2},{4,5},{5,4},{6,7},{7,6},{8,9},{9,8},{10,11... | collective-permute-start | bytes 552968 | tf_op jit(solution)/shard_map/ppermute | solution.py:621
  9.4 1.8 %collective-permute-start.5 = (f32[8,64,128]{2,1,0:T(8,128)S(1)}, f32[8,64,128]{2,1,0:T(8,128)S(1)}, u32[]{:S(2)}, u32[]{:S(2)}) collective-permute-start(f32[8,64,128]{2,1,0:T(8,128)S(1)} %get-tuple-element.32.v_ref), channel_id=1, source_target_pairs={{0,1},{1,0},{2,3},{3,2},{4,5},{5,4},{6,7},{7,6},{8,9},{9,8},{10,11... | collective-permute-start | bytes 786440 | tf_op jit(solution)/shard_map/ppermute | solution.py:602
  9.9 4.7 %copy-start.2 = (bf16[256,256]{1,0:T(8,128)(2,1)S(1)}, bf16[256,256]{1,0:T(8,128)(2,1)}, u32[]{:S(2)}) copy-start(bf16[256,256]{1,0:T(8,128)(2,1)} %constant.19.clone.x_ref.xw_ref) | copy-start | bytes 393220
  9.9 1.7 %collective-permute-start = (f32[8,64,128]{2,1,0:T(8,128)S(1)}, f32[8,64,128]{2,1,0:T(8,128)S(1)}, u32[]{:S(2)}, u32[]{:S(2)}) collective-permute-start(f32[8,64,128]{2,1,0:T(8,128)S(1)} %get-tuple-element.25.e_ref.own_ref), channel_id=1, source_target_pairs={{0,1},{1,0},{2,3},{3,2},{4,5},{5,4},{6,7},{7,6},{8,9},{9,8},{10,11... | collective-permute-start | bytes 786440 | tf_op jit(solution)/shard_map/ppermute | solution.py:601
  10.8 1.7 %collective-permute-start.4 = (f32[360,128]{1,0:T(8,128)S(1)}, f32[360,128]{1,0:T(8,128)S(1)}, u32[]{:S(2)}, u32[]{:S(2)}) collective-permute-start(f32[360,128]{1,0:T(8,128)S(1)} %collective-permute-done.2.odd_ref), channel_id=1, source_target_pairs={{0,1},{1,0},{2,3},{3,2},{4,5},{5,4},{6,7},{7,6},{8,9},{9,8},{10,11... | collective-permute-start | bytes 552968 | tf_op jit(solution)/shard_map/ppermute | solution.py:623
  11.9 3.3 %collective-permute-start.6 = (f32[384,128]{1,0:T(8,128)S(1)}, f32[384,128]{1,0:T(8,128)S(1)}, u32[]{:S(2)}, u32[]{:S(2)}) collective-permute-start(f32[384,128]{1,0:T(8,128)S(1)} %shard_map.167), channel_id=1, source_target_pairs={{1,2},{2,1},{3,4},{4,3},{5,6},{6,5},{9,10},{10,9},{11,12},{12,11},... | collective-permute-start | bytes 589832 | tf_op jit(solution)/shard_map/ppermute | solution.py:619
  12.9 2.3 %collective-permute-start.7 = (f32[320,128]{1,0:T(8,128)S(1)}, f32[320,128]{1,0:T(8,128)S(1)}, u32[]{:S(2)}, u32[]{:S(2)}) collective-permute-start(f32[320,128]{1,0:T(8,128)S(1)} %get-tuple-element.35.after_ref), channel_id=1, source_target_pairs={{1,2},{2,1},{3,4},{4,3},{5,6},{6,5},{9,10},{10,9},{11,12},{12,11},... | collective-permute-start | bytes 491528 | tf_op jit(solution)/shard_map/ppermute | solution.py:630
  13.5 1.6 %copy-start = (bf16[2,256,256]{2,1,0:T(8,128)(2,1)S(1)}, bf16[2,256,256]{2,1,0:T(8,128)(2,1)}, u32[]{:S(2)}) copy-start(bf16[2,256,256]{2,1,0:T(8,128)(2,1)} %constant.17.clone.yi_ref) | copy-start | bytes 786436
  13.5 1.6 %copy-start.1 = (bf16[2,256,256]{2,1,0:T(8,128)(2,1)S(1)}, bf16[2,256,256]{2,1,0:T(8,128)(2,1)}, u32[]{:S(2)}) copy-start(bf16[2,256,256]{2,1,0:T(8,128)(2,1)} %constant.16.clone.yf_ref) | copy-start | bytes 786436
  13.6 1.6 %copy-start.4 = (bf16[192,256]{1,0:T(8,128)(2,1)S(1)}, bf16[192,256]{1,0:T(8,128)(2,1)}, u32[]{:S(2)}) copy-start(bf16[192,256]{1,0:T(8,128)(2,1)} %constant.21.clone.xbn_ref) | copy-start | bytes 294916
  15.2 3.3 %copy-start.3 = (bf16[256,192]{1,0:T(8,128)(2,1)S(1)}, bf16[256,192]{1,0:T(8,128)(2,1)}, u32[]{:S(2)}) copy-start(bf16[256,192]{1,0:T(8,128)(2,1)} %constant.20.clone.xn_ref) | copy-start | bytes 294916
  15.2 3.3 %copy-start.5 = (bf16[128,256]{1,0:T(8,128)(2,1)S(1)}, bf16[128,256]{1,0:T(8,128)(2,1)}, u32[]{:S(2)}) copy-start(bf16[128,256]{1,0:T(8,128)(2,1)} %constant.22.clone.xbo_ref) | copy-start | bytes 196612
  22.1 21.2 %collective-permute-start.8 = (f32[688,128]{1,0:T(8,128)S(1)}, f32[688,128]{1,0:T(8,128)S(1)}, u32[]{:S(2)}, u32[]{:S(2)}) collective-permute-start(f32[688,128]{1,0:T(8,128)S(1)} %get-tuple-element.42), channel_id=1, source_target_pairs={{0,1},{1,0},{2,3},{3,2},{4,5},{5,4},{6,7},{7,6},{8,9},{9,8},{10,11... | collective-permute-start | bytes 1056776 | tf_op jit(solution)/shard_map/ppermute | solution.py:673
